TPU v7x, 256 devices: a whole 4x4x8 slice. The times are simulated.
256 devices in a mesh: tm: 8 (over z), space: 32 (over y, x, core).
Axes of the slice: x: 4, y: 4, z: 8, core: 2. Of those that a mesh axis runs over, the one named last changes fastest.
Arguments:
- labels: int32 [128, 64, 256], P('space'), may hold values from 0 to 3
- conductivity: float32 [4], replicated, may hold values from 0.02 to 1
- coil_pattern: float32 [3, 128, 64, 256], P(None, 'space'), may hold values from -18 to 18
- currents: float32 [8, 2, 3], P('tm'), may hold values from -4 to 4
- initial_state: float32 [128, 64, 256], P('space'), may hold values from -6 to 6
Outputs:
- slice_starts: float32 [8, 128, 64, 256], P('tm', 'space')
- fine_ends: float32 [8, 128, 64, 256], P('tm', 'space')
All inputs are finite; a program needn't handle non-finite values.
Results may differ from a plain program's by a relative error of at most 0.00021.
Values sent between devices are 32-bit elements; how exact they have to be, the bound alone decides.
No kernel may reach another device: no remote copies, remote signals or barrier semaphores. Data moves between devices by JAX's collectives and lax.ppermute only.
A program may use at most 64 MiB of HBM per device.

v0:
```python
import jax
import jax.numpy as jnp
from jax import lax
from jax.sharding import PartitionSpec as P

REGIONS = 4
PHASES = 3
FINE_STEPS = 2
CG_FINE = 2
CG_COARSE = 4
PARA_ITERS = 2


def with_halo(x, sides, width):
    for axis, dim in sides:
        count, length = (lax.axis_size(axis), x.shape[dim])
        up = [(i, (i + 1) % count) for i in range(count - 1)]
        down = [(j, i) for i, j in up]
        last = lax.slice_in_dim(x, length - width, length, axis=dim)
        initial = lax.slice_in_dim(x, 0, width, axis=dim)
        before = lax.ppermute(last, axis, up)
        after = lax.ppermute(initial, axis, down)
        x = jnp.concatenate([before, x, after], axis=dim)
    return x


def from_everyone(x, axis):
    copies = jnp.broadcast_to(x, (lax.axis_size(axis), *x.shape))
    return lax.all_to_all(copies, axis, split_axis=0, concat_axis=0, tiled=True)


def of_everyone(x, axis):
    return from_everyone(x, axis).sum(axis=0)


def together(arrays, axis):
    ravelled, at, outs = (jnp.concatenate([a.reshape(-1) for a in arrays]), 0, [])
    subtotal = of_everyone(ravelled, axis)
    for a in arrays:
        outs.append(subtotal[at : at + a.size].reshape(a.shape))
        at += a.size
    return tuple(outs)


def from_behind(value, axis, steps):
    count = lax.axis_size(axis)
    pairs = [(source, (source + steps) % count) for source in range(count)]
    return lax.ppermute(value, axis, pairs)


def gather_turned(arrays, axis, dims):
    turned = [jnp.moveaxis(a, dim, 0) for a, dim in zip(arrays, dims)]
    widths = [t[0].size for t in turned]
    both = jnp.concatenate([t.reshape(-1, w) for t, w in zip(turned, widths)], axis=1)
    whole = lax.all_gather(both, axis, axis=0, tiled=True)
    parts = jnp.split(whole, [sum(widths[:k]) for k in range(1, len(widths))], axis=1)
    return tuple(
        (
            jnp.moveaxis(b.reshape(-1, *t.shape[1:]), 0, dim)
            for b, t, dim in zip(parts, turned, dims)
        )
    )


def joined_along(parts, dim):
    parts = jnp.moveaxis(parts, 0, dim)
    lengths = parts.shape
    return parts.reshape(*lengths[:dim], lengths[dim] * lengths[dim + 1], *lengths[dim + 2 :])


def gathered_copies(x, axis, dim):
    return joined_along(from_everyone(x, axis), dim)


def restrict(volume):
    first_dim, second_dim, third_dim = volume.shape
    blocks = volume.reshape(first_dim // 4, 4, second_dim // 4, 4, third_dim // 4, 4)
    return jnp.mean(blocks, axis=(1, 3, 5))


def prolong(coarse_field):
    first_dim, second_dim, third_dim = coarse_field.shape
    spread = jnp.broadcast_to(
        coarse_field[:, None, :, None, :, None], (first_dim, 4, second_dim, 4, third_dim, 4)
    )
    return spread.reshape(first_dim * 4, second_dim * 4, third_dim * 4)


def neighbours(padded):
    summed = padded[2:, 1:-1, 1:-1] + padded[:-2, 1:-1, 1:-1]
    summed = summed + padded[1:-1, 2:, 1:-1] + padded[1:-1, :-2, 1:-1]
    return summed + padded[1:-1, 1:-1, 2:] + padded[1:-1, 1:-1, :-2]


def fine_operator(volume, weight):
    padded = with_halo(volume, (("space", 0),), 1)
    padded = jnp.pad(padded, ((0, 0), (1, 1), (1, 1)))
    beside = neighbours(padded)
    return weight * volume + (6.0 * volume - beside)


def coarse_operator(volume, weight):
    beside = neighbours(jnp.pad(volume, 1))
    return weight * volume + 0.0625 * (6.0 * volume - beside)


def conjugate(operator, right_side, guess, count):
    solution = guess
    residual = right_side - operator(solution)
    direction = residual
    res_norm = jnp.sum(residual * residual)
    for sweep_step in range(count):
        applied = operator(direction)
        step_len = res_norm / jnp.sum(direction * applied)
        solution = solution + step_len * direction
        residual = residual - step_len * applied
        if sweep_step + 1 < count:
            new_norm = jnp.sum(residual * residual)
            direction = residual + new_norm / res_norm * direction
            res_norm = new_norm
    return solution


def paired_sums(residual, applied):
    return together((jnp.sum(residual * residual), jnp.sum(residual * applied)), "space")


def fine_solve(right_side, guess, weight):
    solution = guess
    residual = right_side - fine_operator(solution, weight)
    applied = fine_operator(residual, weight)
    res_norm, product = paired_sums(residual, applied)
    step_len = res_norm / product
    direction, applied_dir = (residual, applied)
    for sweep_step in range(CG_FINE):
        solution = solution + step_len * direction
        residual = residual - step_len * applied_dir
        if sweep_step + 1 < CG_FINE:
            applied = fine_operator(residual, weight)
            new_norm, product = paired_sums(residual, applied)
            ratio = new_norm / res_norm
            step_len = new_norm / (product - ratio * new_norm / step_len)
            direction = residual + ratio * direction
            applied_dir = applied + ratio * applied_dir
            res_norm = new_norm
    return solution


def coarse_sweep(coarse_begin, correction, weight_coarse, source_coarse):
    slice_index = lax.axis_index("tm")
    slices = lax.axis_size("tm")

    def advance(vector_in):
        right_side = weight_coarse * vector_in + source_coarse
        return conjugate(
            lambda inner_vec: coarse_operator(inner_vec, weight_coarse),
            right_side,
            vector_in,
            CG_COARSE,
        )

    def keep_same(vector_in):
        return vector_in

    def one_turn(turn_index, loop_state):
        current, used_start, advanced = loop_state
        active = slice_index == turn_index
        stepped = lax.cond(active, advance, keep_same, current)
        outgoing = stepped + correction
        arrived = from_behind(outgoing, "tm", 1)
        receiver = slice_index == (turn_index + 1) % slices
        used_start = jnp.where(active, current, used_start)
        advanced = jnp.where(active, stepped, advanced)
        current = jnp.where(receiver, arrived, current)
        return (current, used_start, advanced)

    return lax.fori_loop(0, slices, one_turn, (coarse_begin, coarse_begin, coarse_begin))


def body(labels, conductivity, coil_pattern, currents, initial_state):
    sigma_cell = jnp.where(labels == 0, conductivity[0], 0.0)
    for region in range(1, REGIONS):
        sigma_cell = sigma_cell + jnp.where(labels == region, conductivity[region], 0.0)
    coarse_pattern = jnp.stack(
        [restrict(coil_pattern[phase_index]) for phase_index in range(PHASES)]
    )
    start_coarse, sigma_coarse, coils_coarse = gather_turned(
        (restrict(initial_state), restrict(sigma_cell), coarse_pattern), "space", (0, 0, 1)
    )
    slice_currents = currents[0]
    mean_current = jnp.mean(slice_currents, axis=0)
    source_coarse = mean_current[0] * coils_coarse[0]
    for phase_index in range(1, PHASES):
        source_coarse = source_coarse + mean_current[phase_index] * coils_coarse[phase_index]
    weight_coarse = sigma_coarse / float(FINE_STEPS)
    is_first = lax.axis_index("tm") == 0
    space_index = lax.axis_index("space")
    plane_count = initial_state.shape[0] // 4

    def own_share(whole_field):
        return lax.dynamic_slice_in_dim(whole_field, space_index * plane_count, plane_count, 0)

    earlier = initial_state - prolong(restrict(initial_state))
    latest = jnp.zeros_like(initial_state)
    correction = jnp.zeros_like(start_coarse)
    coarse_begin = start_coarse
    slice_state = initial_state
    fine_state = initial_state
    for para_index in range(PARA_ITERS + 1):
        landed, used_start, advanced = coarse_sweep(
            coarse_begin, correction, weight_coarse, source_coarse
        )
        slice_state = prolong(own_share(used_start)) + jnp.where(is_first, earlier, latest)
        if para_index < PARA_ITERS:
            volume = slice_state
            for step_index in range(FINE_STEPS):
                source = slice_currents[step_index, 0] * coil_pattern[0]
                for phase_index in range(1, PHASES):
                    source = (
                        source + slice_currents[step_index, phase_index] * coil_pattern[phase_index]
                    )
                volume = fine_solve(sigma_cell * volume + source, volume, sigma_cell)
            fine_state = volume
            fine_coarse = restrict(fine_state)
            correction = gathered_copies(fine_coarse - own_share(advanced), "space", 0)
            arrived_rest = from_behind(fine_state - prolong(fine_coarse), "tm", 1)
            earlier, latest = (latest, arrived_rest)
            coarse_begin = landed
    return (slice_state[None], fine_state[None])


def solution(mesh):
    in_specs = (
        P("space", None, None),
        P(),
        P(None, "space", None, None),
        P("tm", None, None),
        P("space", None, None),
    )
    out_specs = (P("tm", "space", None, None), P("tm", "space", None, None))
    return jax.shard_map(body, mesh=mesh, in_specs=in_specs, out_specs=out_specs, check_vma=False)
```

profile of v0, /device:TPU:225, one launch (start us, length us, event | category | flops | bytes accessed | tf_op | source)
XLA Modules:
  0.0 919.4 jit_solution(10221061463868674349)
XLA Ops:
  17.3 26.2 %all-gather = f32[32,1,5120]{2,1,0:T(1,128)S(1)} all-gather(f32[1,1,5120]{2,1,0:T(1,128)S(1)} %maximum_bitcast_fusion), channel_id=1, replica_groups=mesh['tm'=8,'space'=32] {'space'}, dimensions={0}, use_global_device_ids=true | all-gather | bytes 675840 | tf_op jit(solution)/shard_map/all_gather | solution.py:55
  51.7 165.0 %while.64 = (s32[]{:T(128)}, f32[32,16,64]{2,1,0:T(8,128)S(1)}, f32[32,16,64]{2,1,0:T(8,128)S(1)}, f32[32,16,64]{2,1,0:T(8,128)S(1)}, s32[]{:T(128)}, /*index=5*...) while((s32[]{:T(128)}, f32[32,16,64]{2,1,0:T(8,128)S(1)}, ...), condition=%wide.region_22.23_spmd, body=%wide.region_11.22_spmd.sunk | while | flops 3309583 | bytes 6816232 | solution.py:177
  78.2 14.7 %collective-permute-start = (f32[32,16,64]{2,1,0:T(8,128)S(1)}, f32[32,16,64]{2,1,0:T(8,128)S(1)}, u32[]{:S(2)}, u32[]{:S(2)}) collective-permute-start(f32[32,16,64]{2,1,0:T(8,128)S(1)} %get-tuple-element.1046), channel_id=1, source_target_pairs={{0,32},{32,64},{64,96},{96,128},{128,160},{160,192},{192,224},{224... | collective-permute-start | bytes 393224 | tf_op jit(solution)/shard_map/while/body/eval_jaxpr/ppermute | solution.py:48
  104.1 14.7 %collective-permute-start = (f32[32,16,64]{2,1,0:T(8,128)S(1)}, f32[32,16,64]{2,1,0:T(8,128)S(1)}, u32[]{:S(2)}, u32[]{:S(2)}) collective-permute-start(f32[32,16,64]{2,1,0:T(8,128)S(1)} %get-tuple-element.1046), channel_id=1, source_target_pairs={{0,32},{32,64},{64,96},{96,128},{128,160},{160,192},{192,224},{224... | collective-permute-start | bytes 393224 | tf_op jit(solution)/shard_map/while/body/eval_jaxpr/ppermute | solution.py:48
  128.9 15.1 %collective-permute-start = (f32[32,16,64]{2,1,0:T(8,128)S(1)}, f32[32,16,64]{2,1,0:T(8,128)S(1)}, u32[]{:S(2)}, u32[]{:S(2)}) collective-permute-start(f32[32,16,64]{2,1,0:T(8,128)S(1)} %get-tuple-element.1046), channel_id=1, source_target_pairs={{0,32},{32,64},{64,96},{96,128},{128,160},{160,192},{192,224},{224... | collective-permute-start | bytes 393224 | tf_op jit(solution)/shard_map/while/body/eval_jaxpr/ppermute | solution.py:48
  144.1 51.8 %collective-permute-done = f32[32,16,64]{2,1,0:T(8,128)S(1)} collective-permute-done((f32[32,16,64]{2,1,0:T(8,128)S(1)}, f32[32,16,64]{2,1,0:T(8,128)S(1)}, u32[]{:S(2)}, u32[]{:S(2)}) %collective-permute-start) | collective-permute-done | bytes 131104 | tf_op jit(solution)/shard_map/while/body/eval_jaxpr/ppermute | solution.py:48
  196.0 15.3 %conditional.6 = (f32[32,16,64]{2,1,0:T(8,128)S(1)}) conditional(s32[]{:T(128)} %convert_element_type.62, f32[32,16,64]{2,1,0:T(8,128)S(1)} %get-tuple-element.956, (f32[32,16,64]{2,1,0:T(8,128)S(1)}, f32[32,16,64]{2,1,0:T(8,128)S(1)}, f32[32,16,64]{2,1,0:T(8,128)S(1)}) %tuple.216), branch_computations={%region_12.12_spmd, %region_13.21_spmd} | conditional | flops 3211263 | bytes 5243060 | solution.py:168
  250.2 16.6 %all_to_all.58 = f32[32,1,2]{2,1,0:T(1,128)S(1)} all-to-all(f32[32,1,2]{2,1,0:T(1,128)S(1)} %broadcast_in_dim.135), channel_id=1, replica_groups=mesh['tm'=8,'space'=32] {'space'}, dimensions={0} | all-to-all | bytes 512 | tf_op jit(solution)/shard_map/all_to_all | solution.py:29
  280.7 14.5 %all_to_all.59 = f32[32,1,2]{2,1,0:T(1,128)S(1)} all-to-all(f32[32,1,2]{2,1,0:T(1,128)S(1)} %broadcast_in_dim.136), channel_id=1, replica_groups=mesh['tm'=8,'space'=32] {'space'}, dimensions={0} | all-to-all | bytes 512 | tf_op jit(solution)/shard_map/all_to_all | solution.py:29
  325.8 16.4 %all_to_all.60 = f32[32,1,2]{2,1,0:T(1,128)S(1)} all-to-all(f32[32,1,2]{2,1,0:T(1,128)S(1)} %broadcast_in_dim.137), channel_id=1, replica_groups=mesh['tm'=8,'space'=32] {'space'}, dimensions={0} | all-to-all | bytes 512 | tf_op jit(solution)/shard_map/all_to_all | solution.py:29
  401.5 163.7 %while.65 = (s32[]{:T(128)}, f32[32,16,64]{2,1,0:T(8,128)S(1)}, f32[32,16,64]{2,1,0:T(8,128)S(1)}, f32[32,16,64]{2,1,0:T(8,128)S(1)}, s32[]{:T(128)}, /*index=5*...) while((s32[]{:T(128)}, f32[32,16,64]{2,1,0:T(8,128)S(1)}, ...), condition=%wide.region_48.49_spmd, body=%wide.region_37.48_spmd.sunk | while | flops 3342351 | bytes 7078384 | solution.py:177
  401.7 15.7 %collective-permute-start.1 = (f32[32,16,64]{2,1,0:T(8,128)S(1)}, f32[32,16,64]{2,1,0:T(8,128)S(1)}, u32[]{:S(2)}, u32[]{:S(2)}) collective-permute-start(f32[32,16,64]{2,1,0:T(8,128)S(1)} %get-tuple-element.931), channel_id=1, source_target_pairs={{0,32},{32,64},{64,96},{96,128},{128,160},{160,192},{192,224},{224... | collective-permute-start | bytes 393224 | tf_op jit(solution)/shard_map/while/body/eval_jaxpr/ppermute | solution.py:48
  495.2 49.6 %collective-permute-done.1 = f32[32,16,64]{2,1,0:T(8,128)S(1)} collective-permute-done((f32[32,16,64]{2,1,0:T(8,128)S(1)}, f32[32,16,64]{2,1,0:T(8,128)S(1)}, u32[]{:S(2)}, u32[]{:S(2)}) %collective-permute-start.1) | collective-permute-done | bytes 131104 | tf_op jit(solution)/shard_map/while/body/eval_jaxpr/ppermute | solution.py:48
  544.9 14.7 %conditional.7 = (f32[32,16,64]{2,1,0:T(8,128)S(1)}) conditional(s32[]{:T(128)} %convert_element_type.63, f32[32,16,64]{2,1,0:T(8,128)S(1)} %get-tuple-element.990, (f32[32,16,64]{2,1,0:T(8,128)S(1)}, f32[32,16,64]{2,1,0:T(8,128)S(1)}, f32[32,16,64]{2,1,0:T(8,128)S(1)}) %tuple.220), branch_computations={%region_38.38_spmd, %region_39.47_spmd} | conditional | flops 3211263 | bytes 5243060 | solution.py:168
  598.9 15.9 %all_to_all.61 = f32[32,1,2]{2,1,0:T(1,128)S(1)} all-to-all(f32[32,1,2]{2,1,0:T(1,128)S(1)} %broadcast_in_dim.147), channel_id=1, replica_groups=mesh['tm'=8,'space'=32] {'space'}, dimensions={0} | all-to-all | bytes 512 | tf_op jit(solution)/shard_map/all_to_all | solution.py:29
  628.8 14.3 %all_to_all.62 = f32[32,1,2]{2,1,0:T(1,128)S(1)} all-to-all(f32[32,1,2]{2,1,0:T(1,128)S(1)} %broadcast_in_dim.148), channel_id=1, replica_groups=mesh['tm'=8,'space'=32] {'space'}, dimensions={0} | all-to-all | bytes 512 | tf_op jit(solution)/shard_map/all_to_all | solution.py:29
  672.1 16.4 %all_to_all.63 = f32[32,1,2]{2,1,0:T(1,128)S(1)} all-to-all(f32[32,1,2]{2,1,0:T(1,128)S(1)} %broadcast_in_dim.149), channel_id=1, replica_groups=mesh['tm'=8,'space'=32] {'space'}, dimensions={0} | all-to-all | bytes 512 | tf_op jit(solution)/shard_map/all_to_all | solution.py:29
  746.6 169.7 %while.66 = (s32[]{:T(128)}, f32[32,16,64]{2,1,0:T(8,128)S(1)}, f32[32,16,64]{2,1,0:T(8,128)S(1)}, s32[]{:T(128)}, f32[32,16,64]{2,1,0:T(8,128)S(1)}, /*index=5*...) while((s32[]{:T(128)}, f32[32,16,64]{2,1,0:T(8,128)S(1)}, ...), condition=%wide.region_74.75_spmd, body=%wide.region_63.74_spmd.sunk | while | flops 3309583 | bytes 6816231 | solution.py:177
  746.7 14.8 %collective-permute-start.2 = (f32[32,16,64]{2,1,0:T(8,128)S(1)}, f32[32,16,64]{2,1,0:T(8,128)S(1)}, u32[]{:S(2)}, u32[]{:S(2)}) collective-permute-start(f32[32,16,64]{2,1,0:T(8,128)S(1)} %add.2433), channel_id=1, source_target_pairs={{0,32},{32,64},{64,96},{96,128},{128,160},{160,192},{192,224},{224... | collective-permute-start | bytes 393224 | tf_op jit(solution)/shard_map/while/body/eval_jaxpr/ppermute | solution.py:48
  775.1 15.1 %collective-permute-start.2 = (f32[32,16,64]{2,1,0:T(8,128)S(1)}, f32[32,16,64]{2,1,0:T(8,128)S(1)}, u32[]{:S(2)}, u32[]{:S(2)}) collective-permute-start(f32[32,16,64]{2,1,0:T(8,128)S(1)} %add.2433), channel_id=1, source_target_pairs={{0,32},{32,64},{64,96},{96,128},{128,160},{160,192},{192,224},{224... | collective-permute-start | bytes 393224 | tf_op jit(solution)/shard_map/while/body/eval_jaxpr/ppermute | solution.py:48
  801.3 15.1 %collective-permute-start.2 = (f32[32,16,64]{2,1,0:T(8,128)S(1)}, f32[32,16,64]{2,1,0:T(8,128)S(1)}, u32[]{:S(2)}, u32[]{:S(2)}) collective-permute-start(f32[32,16,64]{2,1,0:T(8,128)S(1)} %add.2433), channel_id=1, source_target_pairs={{0,32},{32,64},{64,96},{96,128},{128,160},{160,192},{192,224},{224... | collective-permute-start | bytes 393224 | tf_op jit(solution)/shard_map/while/body/eval_jaxpr/ppermute | solution.py:48
  826.7 15.4 %collective-permute-start.2 = (f32[32,16,64]{2,1,0:T(8,128)S(1)}, f32[32,16,64]{2,1,0:T(8,128)S(1)}, u32[]{:S(2)}, u32[]{:S(2)}) collective-permute-start(f32[32,16,64]{2,1,0:T(8,128)S(1)} %add.2433), channel_id=1, source_target_pairs={{0,32},{32,64},{64,96},{96,128},{128,160},{160,192},{192,224},{224... | collective-permute-start | bytes 393224 | tf_op jit(solution)/shard_map/while/body/eval_jaxpr/ppermute | solution.py:48
  842.1 52.8 %collective-permute-done.2 = f32[32,16,64]{2,1,0:T(8,128)S(1)} collective-permute-done((f32[32,16,64]{2,1,0:T(8,128)S(1)}, f32[32,16,64]{2,1,0:T(8,128)S(1)}, u32[]{:S(2)}, u32[]{:S(2)}) %collective-permute-start.2) | collective-permute-done | bytes 131104 | tf_op jit(solution)/shard_map/while/body/eval_jaxpr/ppermute | solution.py:48
  895.0 15.8 %conditional.8 = (f32[32,16,64]{2,1,0:T(8,128)S(1)}) conditional(s32[]{:T(128)} %convert_element_type.64, f32[32,16,64]{2,1,0:T(8,128)S(1)} %get-tuple-element.1025, (f32[32,16,64]{2,1,0:T(8,128)S(1)}, f32[32,16,64]{2,1,0:T(8,128)S(1)}, f32[32,16,64]{2,1,0:T(8,128)S(1)}) %tuple.223), branch_computations={%region_64.64_spmd, %region_65.73_spmd} | conditional | flops 3211263 | bytes 5243060 | solution.py:168
  (393 shorter events, 471.6 us)
Async XLA Ops:
  51.8 17.9 %collective-permute-start = (f32[32,16,64]{2,1,0:T(8,128)S(1)}, f32[32,16,64]{2,1,0:T(8,128)S(1)}, u32[]{:S(2)}, u32[]{:S(2)}) collective-permute-start(f32[32,16,64]{2,1,0:T(8,128)S(1)} %get-tuple-element.1046), channel_id=1, source_target_pairs={{0,32},{32,64},{64,96},{96,128},{128,160},{160,192},{192,224},{224... | collective-permute-start | bytes 393224 | tf_op jit(solution)/shard_map/while/body/eval_jaxpr/ppermute | solution.py:48
  69.9 8.1 collective-permute-start
  78.2 18.7 %collective-permute-start = (f32[32,16,64]{2,1,0:T(8,128)S(1)}, f32[32,16,64]{2,1,0:T(8,128)S(1)}, u32[]{:S(2)}, u32[]{:S(2)}) collective-permute-start(f32[32,16,64]{2,1,0:T(8,128)S(1)} %get-tuple-element.1046), channel_id=1, source_target_pairs={{0,32},{32,64},{64,96},{96,128},{128,160},{160,192},{192,224},{224... | collective-permute-start | bytes 393224 | tf_op jit(solution)/shard_map/while/body/eval_jaxpr/ppermute | solution.py:48
  97.1 6.8 collective-permute-start
  104.1 18.0 %collective-permute-start = (f32[32,16,64]{2,1,0:T(8,128)S(1)}, f32[32,16,64]{2,1,0:T(8,128)S(1)}, u32[]{:S(2)}, u32[]{:S(2)}) collective-permute-start(f32[32,16,64]{2,1,0:T(8,128)S(1)} %get-tuple-element.1046), channel_id=1, source_target_pairs={{0,32},{32,64},{64,96},{96,128},{128,160},{160,192},{192,224},{224... | collective-permute-start | bytes 393224 | tf_op jit(solution)/shard_map/while/body/eval_jaxpr/ppermute | solution.py:48
  128.9 67.0 %collective-permute-start = (f32[32,16,64]{2,1,0:T(8,128)S(1)}, f32[32,16,64]{2,1,0:T(8,128)S(1)}, u32[]{:S(2)}, u32[]{:S(2)}) collective-permute-start(f32[32,16,64]{2,1,0:T(8,128)S(1)} %get-tuple-element.1046), channel_id=1, source_target_pairs={{0,32},{32,64},{64,96},{96,128},{128,160},{160,192},{192,224},{224... | collective-permute-start | bytes 393224 | tf_op jit(solution)/shard_map/while/body/eval_jaxpr/ppermute | solution.py:48
  219.8 11.2 %collective-permute-start.3 = (f32[1,64,256]{2,1,0:T(8,128)S(1)}, f32[1,64,256]{2,1,0:T(8,128)S(1)}, u32[]{:S(2)}, u32[]{:S(2)}) collective-permute-start(f32[1,64,256]{2,1,0:T(8,128)S(1)} %get-tuple-element.761), channel_id=1, source_target_pairs={{1,0},{2,1},{3,2},{4,3},{5,4},{6,5},{7,6},{8,7},{9,8},{10,9},{11,1... | collective-permute-start | bytes 196616 | tf_op jit(solution)/shard_map/ppermute | solution.py:22
  357.0 14.5 %all-to-all-start.3 = ((f32[32,1,2]{2,1,0:T(1,128)}), f32[32,1,2]{2,1,0:T(1,128)S(1)}, u32[]{:S(2)}, u32[]{:S(2)}) async-start(f32[32,1,2]{2,1,0:T(1,128)} %broadcast_in_dim.138), calls=%async_computation.3 | async-start | bytes 32768 | tf_op jit(solution)/shard_map/all_to_all | solution.py:29
  387.9 11.9 %all-to-all-start.4 = ((f32[32,1,1024]{2,1,0:T(1,128)}), f32[32,1,1024]{2,1,0:T(1,128)S(1)}, u32[]{:S(2)}, u32[]{:S(2)}) async-start(f32[32,1,1024]{2,1,0:T(1,128)} %reshape.357), calls=%async_computation.4 | async-start | bytes 262144 | tf_op jit(solution)/shard_map/all_to_all | solution.py:29
  392.8 177.4 %collective-permute-start.15 = (f32[4,64,256]{2,1,0:T(8,128)}, f32[4,64,256]{2,1,0:T(8,128)}, u32[]{:S(2)}, u32[]{:S(2)}) collective-permute-start(f32[4,64,256]{2,1,0:T(8,128)} %broadcast_subtract_fusion.1), channel_id=1, source_target_pairs={{0,32},{32,64},{64,96},{96,128},{128,160},{160,192},{192,224},{224... | collective-permute-start | bytes 786440 | tf_op jit(solution)/shard_map/ppermute | solution.py:48
  401.7 20.9 %collective-permute-start.1 = (f32[32,16,64]{2,1,0:T(8,128)S(1)}, f32[32,16,64]{2,1,0:T(8,128)S(1)}, u32[]{:S(2)}, u32[]{:S(2)}) collective-permute-start(f32[32,16,64]{2,1,0:T(8,128)S(1)} %get-tuple-element.931), channel_id=1, source_target_pairs={{0,32},{32,64},{64,96},{96,128},{128,160},{160,192},{192,224},{224... | collective-permute-start | bytes 393224 | tf_op jit(solution)/shard_map/while/body/eval_jaxpr/ppermute | solution.py:48
  422.9 7.9 collective-permute-start.1
  431.1 17.9 %collective-permute-start.1 = (f32[32,16,64]{2,1,0:T(8,128)S(1)}, f32[32,16,64]{2,1,0:T(8,128)S(1)}, u32[]{:S(2)}, u32[]{:S(2)}) collective-permute-start(f32[32,16,64]{2,1,0:T(8,128)S(1)} %get-tuple-element.931), channel_id=1, source_target_pairs={{0,32},{32,64},{64,96},{96,128},{128,160},{160,192},{192,224},{224... | collective-permute-start | bytes 393224 | tf_op jit(solution)/shard_map/while/body/eval_jaxpr/ppermute | solution.py:48
  456.4 17.4 %collective-permute-start.1 = (f32[32,16,64]{2,1,0:T(8,128)S(1)}, f32[32,16,64]{2,1,0:T(8,128)S(1)}, u32[]{:S(2)}, u32[]{:S(2)}) collective-permute-start(f32[32,16,64]{2,1,0:T(8,128)S(1)} %get-tuple-element.931), channel_id=1, source_target_pairs={{0,32},{32,64},{64,96},{96,128},{128,160},{160,192},{192,224},{224... | collective-permute-start | bytes 393224 | tf_op jit(solution)/shard_map/while/body/eval_jaxpr/ppermute | solution.py:48
  480.9 63.9 %collective-permute-start.1 = (f32[32,16,64]{2,1,0:T(8,128)S(1)}, f32[32,16,64]{2,1,0:T(8,128)S(1)}, u32[]{:S(2)}, u32[]{:S(2)}) collective-permute-start(f32[32,16,64]{2,1,0:T(8,128)S(1)} %get-tuple-element.931), channel_id=1, source_target_pairs={{0,32},{32,64},{64,96},{96,128},{128,160},{160,192},{192,224},{224... | collective-permute-start | bytes 393224 | tf_op jit(solution)/shard_map/while/body/eval_jaxpr/ppermute | solution.py:48
  571.1 10.7 %collective-permute-start.16 = (f32[1,64,256]{2,1,0:T(8,128)S(1)}, f32[1,64,256]{2,1,0:T(8,128)S(1)}, u32[]{:S(2)}, u32[]{:S(2)}) collective-permute-start(f32[1,64,256]{2,1,0:T(8,128)S(1)} %get-tuple-element.749), channel_id=1, source_target_pairs={{1,0},{2,1},{3,2},{4,3},{5,4},{6,5},{7,6},{8,7},{9,8},{10,9},{11,1... | collective-permute-start | bytes 196616 | tf_op jit(solution)/shard_map/ppermute | solution.py:22
  703.1 14.5 %all-to-all-start.8 = ((f32[32,1,2]{2,1,0:T(1,128)}), f32[32,1,2]{2,1,0:T(1,128)S(1)}, u32[]{:S(2)}, u32[]{:S(2)}) async-start(f32[32,1,2]{2,1,0:T(1,128)} %broadcast_in_dim.150), calls=%async_computation.8 | async-start | bytes 32768 | tf_op jit(solution)/shard_map/all_to_all | solution.py:29
  733.6 11.9 %all-to-all-start.9 = ((f32[32,1,1024]{2,1,0:T(1,128)}), f32[32,1,1024]{2,1,0:T(1,128)S(1)}, u32[]{:S(2)}, u32[]{:S(2)}) async-start(f32[32,1,1024]{2,1,0:T(1,128)} %reshape.359), calls=%async_computation.9 | async-start | bytes 262144 | tf_op jit(solution)/shard_map/all_to_all | solution.py:29
  738.5 179.8 %collective-permute-start.28 = (f32[4,64,256]{2,1,0:T(8,128)}, f32[4,64,256]{2,1,0:T(8,128)S(1)}, u32[]{:S(2)}, u32[]{:S(2)}) collective-permute-start(f32[4,64,256]{2,1,0:T(8,128)} %broadcast_subtract_fusion), channel_id=1, source_target_pairs={{0,32},{32,64},{64,96},{96,128},{128,160},{160,192},{192,224},{224... | collective-permute-start | bytes 786440 | tf_op jit(solution)/shard_map/ppermute | solution.py:48
  746.7 20.1 %collective-permute-start.2 = (f32[32,16,64]{2,1,0:T(8,128)S(1)}, f32[32,16,64]{2,1,0:T(8,128)S(1)}, u32[]{:S(2)}, u32[]{:S(2)}) collective-permute-start(f32[32,16,64]{2,1,0:T(8,128)S(1)} %add.2433), channel_id=1, source_target_pairs={{0,32},{32,64},{64,96},{96,128},{128,160},{160,192},{192,224},{224... | collective-permute-start | bytes 393224 | tf_op jit(solution)/shard_map/while/body/eval_jaxpr/ppermute | solution.py:48
  767.0 7.9 collective-permute-start.2
  775.1 19.0 %collective-permute-start.2 = (f32[32,16,64]{2,1,0:T(8,128)S(1)}, f32[32,16,64]{2,1,0:T(8,128)S(1)}, u32[]{:S(2)}, u32[]{:S(2)}) collective-permute-start(f32[32,16,64]{2,1,0:T(8,128)S(1)} %add.2433), channel_id=1, source_target_pairs={{0,32},{32,64},{64,96},{96,128},{128,160},{160,192},{192,224},{224... | collective-permute-start | bytes 393224 | tf_op jit(solution)/shard_map/while/body/eval_jaxpr/ppermute | solution.py:48
  801.3 18.5 %collective-permute-start.2 = (f32[32,16,64]{2,1,0:T(8,128)S(1)}, f32[32,16,64]{2,1,0:T(8,128)S(1)}, u32[]{:S(2)}, u32[]{:S(2)}) collective-permute-start(f32[32,16,64]{2,1,0:T(8,128)S(1)} %add.2433), channel_id=1, source_target_pairs={{0,32},{32,64},{64,96},{96,128},{128,160},{160,192},{192,224},{224... | collective-permute-start | bytes 393224 | tf_op jit(solution)/shard_map/while/body/eval_jaxpr/ppermute | solution.py:48
  826.7 68.2 %collective-permute-start.2 = (f32[32,16,64]{2,1,0:T(8,128)S(1)}, f32[32,16,64]{2,1,0:T(8,128)S(1)}, u32[]{:S(2)}, u32[]{:S(2)}) collective-permute-start(f32[32,16,64]{2,1,0:T(8,128)S(1)} %add.2433), channel_id=1, source_target_pairs={{0,32},{32,64},{64,96},{96,128},{128,160},{160,192},{192,224},{224... | collective-permute-start | bytes 393224 | tf_op jit(solution)/shard_map/while/body/eval_jaxpr/ppermute | solution.py:48
  (39 other events, 304.4 us)
where the time goes:
time: 938 us; the launch traced here: 919 us
  starting transfers between devices  310 us (33%)
  waiting for transfers between devices  282 us (30%)
  blocking collectives  120 us (13%)
  other arithmetic  99.7 us (11%)
  local copies, waits for them, and re-layouts  53.7 us (6%)
  loops' own time  28.7 us (3%)
  between operations  24.8 us (3%)
    ppermute x26, waiting for transfers between devices, from_behind(): return lax.ppermute(value, axis, pairs)  240 us
    ppermute x26, starting transfers between devices, from_behind(): return lax.ppermute(value, axis, pairs)  207 us
    all_to_all x6, blocking collectives, from_everyone(): return lax.all_to_all(copies, axis, split_axis=0, concat_axis=0, tiled=True)  94.2 us
    ppermute x12, starting transfers between devices, with_halo(): before = lax.ppermute(last, axis, up)  40.1 us
    ppermute x12, starting transfers between devices, with_halo(): after = lax.ppermute(initial, axis, down)  39.2 us
    reduce_sum x8, other arithmetic, paired_sums(): jnp.sum(residual * residual)  28.2 us
    another operation x24, loops' own time, one_turn(): stepped = lax.cond(active, advance, keep_same, current)  27.8 us
    all_to_all x4, waiting for transfers between devices, from_everyone(): return lax.all_to_all(copies, axis, split_axis=0, concat_axis=0, tiled=True)  26.6 us
  transfers between devices with their start and end apart: 54, of which 40 were waited for; matrix products, arithmetic and copies ran while one was open for 3% of the time, Pallas kernels for 0%

commit v1 on v0

v1 whole, which is shorter than its diff:
```python
import functools

import jax
import jax.numpy as jnp
from jax import lax
from jax.experimental import pallas as pl
from jax.experimental.pallas import tpu as pltpu
from jax.sharding import PartitionSpec as P

PHASES = 3
CG_COARSE = 4
F32 = jnp.float32
HIGHEST = lax.Precision.HIGHEST
VMEM = pltpu.MemorySpace.VMEM
SMEM = pltpu.MemorySpace.SMEM
INTERPRET = False
LIMIT = 20 << 20


def iota(shape, dim):
    return lax.broadcasted_iota(jnp.int32, shape, dim)


def dot(a, b):
    return lax.dot_general(a, b, (((1,), (0,)), ((), ())), precision=HIGHEST, preferred_element_type=F32)


def total(x):
    while x.ndim > 2:
        x = jnp.sum(x, axis=0)
    return jnp.sum(jnp.sum(x, axis=0, keepdims=True), axis=1, keepdims=True)


def restrict_packed(summed):
    columns = (iota((256, 128), 0) >> 2) == (iota((256, 128), 1) & 63)
    rows = (iota((16, 64), 1) >> 2) == iota((16, 64), 0)
    half = dot(summed, jnp.where(columns, 1.0 / 64.0, 0.0).astype(F32))
    both = dot(jnp.where(rows, 1.0, 0.0).astype(F32), half)
    return jnp.where(iota((8, 128), 1) < 64, both[:8], both[8:])


def widen(planes):
    columns = (iota((128, 256), 1) >> 2) == iota((128, 256), 0)
    rows = (iota((64, 16), 0) >> 2) == iota((64, 16), 1)
    wide = dot(planes, jnp.where(columns, 1.0, 0.0).astype(F32))
    lift = jnp.where(rows, 1.0, 0.0).astype(F32)
    return [dot(lift, wide[k : k + 16]) for k in range(0, planes.shape[0], 16)]


def unpack(low, high):
    axis = low.ndim - 1
    left = iota(low.shape, axis) < 64
    top = jnp.where(left, low, pltpu.roll(high, 64, axis))
    bottom = jnp.where(left, pltpu.roll(low, 64, axis), high)
    return jnp.concatenate([top, bottom], axis=axis - 1)


def coarse_beside(v):
    one = (1, 16, 128)
    lane, row = iota(one, 2), iota(one, 1)
    left = lane < 64
    first, last = pltpu.roll(v[:1], 64, 2), pltpu.roll(v[15:], 64, 2)
    after = jnp.concatenate([v[1:], jnp.where(left, first, 0.0)], axis=0)
    before = jnp.concatenate([jnp.where(left, 0.0, last), v[:15]], axis=0)
    out = after + before
    out = out + jnp.where(row == 0, 0.0, pltpu.roll(v, 1, 1)) + jnp.where(row == 15, 0.0, pltpu.roll(v, 15, 1))
    inner = lane & 63
    return out + jnp.where(inner == 0, 0.0, pltpu.roll(v, 1, 2)) + jnp.where(inner == 63, 0.0, pltpu.roll(v, 127, 2))


def coarse_solve(start, source, diagonal):
    def apply(v):
        return diagonal * v - 0.0625 * coarse_beside(v)

    x = start
    residual = source - 0.375 * start + 0.0625 * coarse_beside(start)
    image = apply(residual)
    norm, product = total(residual * residual), total(residual * image)
    step = norm / product
    direction, moved = residual, image
    for turn in range(CG_COARSE):
        x = x + step[None] * direction
        if turn + 1 < CG_COARSE:
            residual = residual - step[None] * moved
            image = apply(residual)
            new, product = total(residual * residual), total(residual * image)
            ratio = new / norm
            step = new / (product - ratio * new / step)
            direction = residual + ratio[None] * direction
            moved = image + ratio[None] * moved
            norm = new
    return x


def cut_planes(state, place, offsets):
    out = []
    lane = iota((16, 128), 1)
    for offset in offsets:
        at = place + offset
        inside = jnp.logical_and(at >= 0, at < 32).astype(jnp.int32)
        at = jnp.clip(at, 0, 31)
        plane = state[at & 15]
        plane = jnp.where((at >> 4) * jnp.ones_like(lane) == 1, pltpu.roll(plane, 64, 1), plane)
        out.append(jnp.where(lane < 64 * inside, plane, 0.0))
    return out


def call(body, outs, args, small=(), scratch=(), flops=0):
    specs = [pl.BlockSpec(memory_space=SMEM if k in small else VMEM) for k in range(len(args))]
    return pl.pallas_call(
        body,
        out_shape=tuple(jax.ShapeDtypeStruct(s, F32) for s in outs),
        in_specs=specs,
        out_specs=tuple(pl.BlockSpec(memory_space=VMEM) for _ in outs),
        scratch_shapes=tuple(pltpu.VMEM(s, F32) for s in scratch),
        cost_estimate=pl.CostEstimate(flops=flops, bytes_accessed=1 << 20, transcendentals=0) if flops else None,
        compiler_params=pltpu.CompilerParams(vmem_limit_bytes=LIMIT),
        interpret=INTERPRET,
    )(*args)


def setup_kernel(cond, cur, labels, coils, initial, sigma, sources, up, down, far, packed):
    region = labels[...]
    cell = jnp.where(region == 0, cond[0], 0.0)
    for k in range(1, 4):
        cell = cell + jnp.where(region == k, cond[k], 0.0)
    sigma[...] = cell
    pattern = [coils[p] for p in range(PHASES)]
    for step in range(2):
        source = cur[step, 0] * pattern[0]
        for p in range(1, PHASES):
            source = source + cur[step, p] * pattern[p]
        sources[step] = source
    up[0:2] = sigma[2:4]
    up[2:5] = sources[0, 1:4]
    up[5:6] = sources[1, 3:4]
    down[0:3] = sigma[0:3]
    down[3:7] = sources[0]
    down[7:9] = sources[1, 0:2]
    up[6:10] = initial[...]
    down[9:13] = initial[...]
    far[...] = initial[0:1]
    fields = [initial[...], cell, *pattern]
    rows = [restrict_packed(jnp.sum(f, axis=0)) for f in fields]
    rows = jnp.concatenate([*rows, jnp.zeros((8, 128), F32)], axis=0)
    packed[...] = jnp.broadcast_to(rows[None], packed.shape)


def unpack_all(whole, at):
    return unpack(whole[0:16, at : at + 8, :], whole[16:32, at : at + 8, :])


def sweep(where, cur, state, static, advanced, planes, correction, count):
    mine, place = where[0], where[1]
    diagonal = static[1] * 0.5 + 0.375

    def turn(n, carry):
        if planes is not None:

            @pl.when(n == mine)
            def _():
                for k, plane in enumerate(cut_planes(state, place, (-1, 0, 1, 2))):
                    planes[16 * k : 16 * k + 16] = plane

        source = jnp.zeros((16, 16, 128), F32)
        for p in range(PHASES):
            mean = 0.5 * (cur[n, p] + cur[n, PHASES + p])
            source = source + mean * static[2 + p]
        solved = coarse_solve(state[...], source, static[1] * 0.5 + 0.375)
        if advanced is not None:
            advanced[n] = solved
        state[...] = solved if correction is None else solved + correction[n]
        return carry

    lax.fori_loop(0, count, turn, 0)


def first_sweep_kernel(where, cur, whole, static, planes, advanced, state):
    for k in range(5):
        static[k] = unpack_all(whole, 8 * k)
    state[...] = static[0]
    sweep(where, cur, state, static, advanced, planes, None, 8)


def load_corrections(where, ends, before, correction):
    for end, offset in zip(ends, OFFSETS):
        n = (where[0] + offset) & 7
        correction[n] = unpack(end[0:16], end[16:32]) - before[n]


OFFSETS = (0, -1, 1, -2, 2, -3, 3, -4)


def next_sweep_kernel(where, cur, static, before, begin, *refs):
    ends, (planes, advanced, state, correction) = refs[:8], refs[8:]
    load_corrections(where, ends, before, correction)
    state[...] = begin[...]
    sweep(where, cur, state, static, advanced, planes, correction, 8)


def last_sweep_kernel(where, cur, static, before, begin, rest_first, rest_other, *refs):
    ends, (start, state, correction, planes) = refs[:8], refs[8:]
    load_corrections(where, ends, before, correction)
    state[...] = begin[...]

    def keep():
        (plane,) = cut_planes(state, where[1], (0,))
        planes[...] = plane

    mine = where[0]

    def turn(n, carry):
        source = jnp.zeros((16, 16, 128), F32)
        for p in range(PHASES):
            mean = 0.5 * (cur[n, p] + cur[n, PHASES + p])
            source = source + mean * static[2 + p]
        state[...] = coarse_solve(state[...], source, static[1] * 0.5 + 0.375) + correction[n]
        return carry

    lax.fori_loop(0, mine, turn, 0)
    keep()
    (own,) = widen(planes[...])
    first = (mine == 0).astype(F32)
    start[...] = own[None] + (first * rest_first[...] + (1.0 - first) * rest_other[...])


def fine_beside(v):
    rows, lanes = iota(v.shape, 0), iota(v.shape, 1)
    out = jnp.where(rows == 0, 0.0, pltpu.roll(v, 1, 0)) + jnp.where(rows == 63, 0.0, pltpu.roll(v, 63, 0))
    return out + jnp.where(lanes == 0, 0.0, pltpu.roll(v, 1, 1)) + jnp.where(lanes == 255, 0.0, pltpu.roll(v, 255, 1))


def inside(plane):
    return jnp.logical_and(plane >= 0, plane < 128).astype(F32)


def each(pieces, body):
    at = 0
    for read, count in pieces:

        def one(i, carry, read=read, at=at):
            body(at + i, read(i))
            return carry

        lax.fori_loop(0, count, one, 0)
        at += count


def residual_planes(field, source, out, first):
    def body(j, piece):
        v = field[j + 1]
        r = piece - 6.0 * v + (field[j] + field[j + 2]) + fine_beside(v)
        out[j] = inside(first + j) * r

    each(source, body)


def image_planes(field, weight, out, first):
    def body(j, piece):
        v = field[j + 1]
        w = (piece + 6.0) * v - (field[j] + field[j + 2]) - fine_beside(v)
        out[j] = inside(first + j) * w

    each(weight, body)


def moments(r, r_at, w, w_at, sigma):
    def body(i, sums):
        a, b, c = r[r_at + i], w[w_at + i], w[w_at + i + 1]
        cross = (sigma[i] + 6.0) * b - fine_beside(b) - 2.0 * c
        return (sums[0] + a * a, sums[1] + a * b, sums[2] + b * b, sums[3] + b * cross)

    zero = jnp.zeros((64, 256), F32)
    sums = lax.fori_loop(0, 4, body, (zero,) * 4)
    lane = iota((1, 128), 1)
    row = jnp.zeros((1, 128), F32)
    for k in range(4):
        row = jnp.where(lane == k, total(sums[k]), row)
    return row


def weights(row):
    lane = iota((1, 128), 1)
    m0, m1, m2, m3 = (jnp.sum(jnp.where(lane == k, row, 0.0), axis=1, keepdims=True) for k in range(4))
    step = m0 / m1
    new = step * step * m2 - m0
    product = m1 - 2.0 * step * m2 + step * step * m3
    ratio = new / m0
    second = new / (product - ratio * new / step)
    return step + second * (1.0 + ratio), -step * second


def fine_one_kernel(initial, where, planes, rest, rest_up, rest_down, rest_far, sigma, sources, up, down,
                    u_out, r_out, w_out, packed, u, r):
    first = 4 * where[1]
    zero = (where[0] == 0).astype(F32)
    scale = (1.0 - zero, zero) if initial else (1.0, 1.0 - zero)
    above, below = (6, 9) if initial else (0, 0)
    lifted = widen(planes[...])
    pieces = [(rest_up, above + k) for k in range(4)] + [(rest, k) for k in range(4)]
    pieces = pieces + [(rest_down, below + k) for k in range(4)] + [(rest_far, 0)]
    for j, (piece, k) in enumerate(pieces):
        u[j] = scale[0] * lifted[j // 4] + scale[1] * piece[k]
    source = ((lambda i: up[2 + i], 3), (lambda i: sources[0, i], 4), (lambda i: down[3 + i], 4))
    residual_planes(u, source, r, first - 3)
    weight = ((lambda i: up[i], 2), (lambda i: sigma[i], 4), (lambda i: down[i], 3))
    image_planes(r, weight, w_out, first - 2)
    u_out[...] = u[2:11]
    r_out[...] = r[1:10]
    packed[...] = jnp.broadcast_to(moments(r, 3, w_out, 2, sigma), packed.shape)


def fine_two_kernel(where, sums, u, r, w, sigma, sources, up, down, u_out, r_out, w_out, packed, u1, r1, w1):
    first = 4 * where[1]
    a, b = weights(jnp.sum(sums[...], axis=0, keepdims=True))

    def move(j, carry):
        u1[j] = u[j] + a * r[j] + b * w[j]
        return carry

    lax.fori_loop(0, 9, move, 0)
    source = ((lambda i: up[5 + i], 1), (lambda i: sources[1, i], 4), (lambda i: down[7 + i], 2))
    residual_planes(u1, source, r1, first - 1)
    weight = ((lambda i: sigma[i], 4), (lambda i: down[i], 1))
    image_planes(r1, weight, w1, first)
    u_out[...] = u1[2:6]
    r_out[...] = r1[1:5]
    w_out[...] = w1[0:4]
    row = moments(r1, 1, w1, 0, sigma)
    parts = [restrict_packed(jnp.sum(f[...], axis=0)) for f in (u_out, r_out, w_out)]
    rows = jnp.concatenate([*parts, jnp.broadcast_to(row, (8, 128))], axis=0)
    packed[...] = jnp.broadcast_to(rows[None], packed.shape)


def fine_three_kernel(where, whole, u, r, w, fine, rest, ends):
    a, b = weights(jnp.sum(whole[:, 24, :], axis=0, keepdims=True))
    ends[...] = whole[:, 0:8, :] + a[None] * whole[:, 8:16, :] + b[None] * whole[:, 16:24, :]
    own = ends[where[1]]
    left = iota((8, 128), 1) < 64
    plane = jnp.concatenate([jnp.where(left, own, 0.0), jnp.where(left, pltpu.roll(own, 64, 1), 0.0)], axis=0)
    (lifted,) = widen(plane)
    for i in range(4):
        value = u[i] + a * r[i] + b * w[i]
        fine[i] = value
        rest[i] = value - lifted


def shifted(x, axis, by, ring):
    n = lax.axis_size(axis)
    pairs = [(i, (i + by) % n) for i in range(n) if ring or 0 <= i + by < n]
    return lax.ppermute(x, axis, pairs)


def exchange(x, axis):
    return lax.all_to_all(x, axis, split_axis=0, concat_axis=0, tiled=True)


def around(x):
    ends, ahead, behind = [x], x, x
    for k in range(1, 5):
        ahead = shifted(ahead, "tm", 1, True)
        ends.append(ahead)
        if k < 4:
            behind = shifted(behind, "tm", -1, True)
            ends.append(behind)
    return ends


def halos(x):
    return (
        shifted(x, "space", 1, False),
        shifted(x, "space", -1, False),
        shifted(x[:1], "space", -2, False),
    )


def body(labels, conductivity, coil_pattern, currents, initial_state):
    tm, place = lax.axis_index("tm"), lax.axis_index("space")
    where = jnp.stack([tm, place]).astype(jnp.int32)
    block, field = (4, 64, 256), (16, 16, 128)

    slices, across = lax.axis_size("tm"), lax.axis_size("space")
    pairs = [
        (b * across + slices * a + t, t * across + slices * a + b)
        for t in range(slices)
        for b in range(slices)
        for a in range(across // slices)
    ]
    theirs = lax.ppermute(jnp.pad(currents.reshape(1, 6), ((0, 0), (0, 122))), ("tm", "space"), pairs)

    sigma, sources, up, down, far, packed = call(
        setup_kernel,
        (block, (2, *block), (10, 64, 256), (13, 64, 256), (1, 64, 256), (32, 48, 128)),
        (conductivity, currents[0], labels, coil_pattern, initial_state),
        small=(0, 1),
    )
    packed = lax.dynamic_update_slice(packed, jnp.broadcast_to(theirs[None], (32, 1, 128)), (0, 40, 0))
    whole = exchange(packed, "space")
    table = whole[:8, 40, :]
    up, down = shifted(up, "space", 1, False), shifted(down, "space", -1, False)
    far = shifted(far, "space", -2, False)
    static, planes, advanced, state = call(
        first_sweep_kernel,
        ((5, *field), (64, 128), (8, *field), field),
        (where, table, whole),
        small=(0, 1),
        flops=1 << 26,
    )

    def fine(initial, planes, rest, around_rest):
        u, r, w, sums = call(
            functools.partial(fine_one_kernel, initial),
            ((9, 64, 256), (9, 64, 256), (9, 64, 256), (32, 128)),
            (where, planes, rest, *around_rest, sigma, sources, up, down),
            small=(0,),
            scratch=((13, 64, 256), (11, 64, 256)),
        )
        u, r, w, packed = call(
            fine_two_kernel,
            (block, block, block, (32, 32, 128)),
            (where, exchange(sums, "space"), u, r, w, sigma, sources, up, down),
            small=(0,),
            scratch=((9, 64, 256), (7, 64, 256), (5, 64, 256)),
        )
        return call(
            fine_three_kernel,
            (block, block, (32, 8, 128)),
            (where, exchange(packed, "space"), u, r, w),
            small=(0,),
        )

    _, rest, ends = fine(True, planes, initial_state, (up, down, far))
    rest_first = shifted(rest, "tm", 1, True)
    planes, advanced_next, state_next = call(
        next_sweep_kernel,
        ((64, 128), (8, *field), field),
        (where, table, static, advanced, state, *around(ends)),
        small=(0, 1),
        scratch=((8, *field),),
        flops=1 << 26,
    )
    fine_state, rest, ends = fine(False, planes, rest_first, halos(rest_first))
    rest_other = shifted(rest, "tm", 1, False)
    (start,) = call(
        last_sweep_kernel,
        (block,),
        (where, table, static, advanced_next, state_next, rest_first, rest_other, *around(ends)),
        small=(0, 1),
        scratch=(field, (8, *field), (16, 128)),
        flops=1 << 26,
    )
    return (start[None], fine_state[None])


def solution(mesh):
    in_specs = (
        P("space", None, None),
        P(),
        P(None, "space", None, None),
        P("tm", None, None),
        P("space", None, None),
    )
    out_specs = (P("tm", "space", None, None), P("tm", "space", None, None))
    return jax.shard_map(body, mesh=mesh, in_specs=in_specs, out_specs=out_specs, check_vma=False)
```

time: 938 us -> 199 us (0.21)
  the two profiles are of different devices: /device:TPU:225 before, /device:TPU:128 now
where the time goes in v1:
time: 199 us
  blocking collectives  52.8 us (27%)
  waiting for transfers between devices  48.5 us (24%)
  Pallas kernels  46.5 us (23%)
  starting transfers between devices  43.7 us (22%)
  local copies, waits for them, and re-layouts  6.28 us (3%)
    all_to_all x4, blocking collectives, exchange(): return lax.all_to_all(x, axis, split_axis=0, concat_axis=0, tiled=True)  52.8 us
    pallas_call x10, Pallas kernels, call(): pl.pallas_call(body, out_shape=tuple((jax.ShapeDtypeStruct(s, F32) for s...  46.5 us
    ppermute x22, starting transfers between devices, shifted(): return lax.ppermute(x, axis, pairs)  32.3 us
    ppermute x22, waiting for transfers between devices, shifted(): return lax.ppermute(x, axis, pairs)  29.6 us
    all_to_all x1, waiting for transfers between devices, exchange(): return lax.all_to_all(x, axis, split_axis=0, concat_axis=0, tiled=True)  10.9 us
    ppermute x1, waiting for transfers between devices, body(): lax.ppermute(jnp.pad(currents.reshape(1, 6), ((0, 0), (0, 122))), ('tm',...  8.03 us
    all_to_all x1, starting transfers between devices, exchange(): return lax.all_to_all(x, axis, split_axis=0, concat_axis=0, tiled=True)  7.67 us
    unnamed x14, local copies, waits for them, and re-layouts  4.55 us
  transfers between devices with their start and end apart: 24, of which 11 were waited for; matrix products, arithmetic and copies ran while one was open for 1% of the time, Pallas kernels for 10%

profile of v1, /device:TPU:128, one launch (start us, length us, event | category | flops | bytes accessed | tf_op | source)
XLA Modules:
  0.0 198.8 jit_solution(6086256957843967489)
XLA Ops:
  9.6 3.7 %collective-permute-start = (f32[1,128]{1,0:T(1,128)S(1)}, f32[1,128]{1,0:T(1,128)S(1)}, u32[]{:S(2)}, u32[]{:S(2)}) collective-permute-start(f32[1,128]{1,0:T(1,128)S(1)} %pad.4), channel_id=1, source_target_pairs={{0,0},{8,8},{16,16},{24,24},{32,1},{40,9},{48,17},{56,25},{64,2},{... | collective-permute-start | bytes 1544 | tf_op jit(solution)/shard_map/ppermute | solution.py:389
  13.3 8.0 %collective-permute-done = f32[1,128]{1,0:T(1,128)S(1)} collective-permute-done((f32[1,128]{1,0:T(1,128)S(1)}, f32[1,128]{1,0:T(1,128)S(1)}, u32[]{:S(2)}, u32[]{:S(2)}) %collective-permute-start) | collective-permute-done | bytes 544 | tf_op jit(solution)/shard_map/ppermute | solution.py:389
  23.0 7.7 %all-to-all-start = ((f32[32,48,128]{2,1,0:T(8,128)}), f32[32,48,128]{2,1,0:T(8,128)S(1)}, u32[]{:S(2)}, u32[]{:S(2)}) async-start(f32[32,48,128]{2,1,0:T(8,128)} %dynamic_update_slice.3), calls=%async_computation | async-start | bytes 1572864 | tf_op jit(solution)/shard_map/all_to_all | solution.py:355
  34.3 10.9 %all-to-all-done.whole = f32[32,48,128]{2,1,0:T(8,128)S(1)} async-done(((f32[32,48,128]{2,1,0:T(8,128)}), f32[32,48,128]{2,1,0:T(8,128)S(1)}, u32[]{:S(2)}, u32[]{:S(2)}) %all-to-all-start) | async-done | bytes 786464 | tf_op jit(solution)/shard_map/all_to_all | solution.py:355
  45.2 9.5 %shard_map.69 = (f32[5,16,16,128]{3,2,1,0:T(8,128)S(1)}, f32[64,128]{1,0:T(8,128)S(1)}, f32[8,16,16,128]{3,2,1,0:T(8,128)S(1)}, f32[16,16,128]{2,1,0:T(8,128)S(1)}) custom-call(s32[2]{0:T(128)S(1)} %pad_add_fusion.where, f32[8,128]{1,0:T(8,128)S(1)} %bitcast.17, f32[32,48,128]{2,1,0:T(8,128)S(1)} %all-to-all-done.whole), custom_call_target="tpu_custom_call" | custom-call | flops 67108864 | bytes 1048576 | tf_op jit(solution)/shard_map/pallas_call | solution.py:110
  54.8 4.0 %shard_map.70 = (f32[9,64,256]{2,1,0:T(8,128)S(1)}, f32[9,64,256]{2,1,0:T(8,128)S(1)}, f32[9,64,256]{2,1,0:T(8,128)S(1)}, f32[32,128]{1,0:T(8,128)S(1)}) custom-call(s32[2]{0:T(128)S(1)} %pad_add_fusion.where, f32[64,128]{1,0:T(8,128)S(1)} %get-tuple-element.40.planes, f32[4,64,256]{2,1,0:T(8,128)S(1)} %copy-done.1, ...), custom_call_target="tpu_custom_call" | custom-call | tf_op jit(solution)/shard_map/pallas_call | solution.py:110
  58.8 11.5 %all_to_all.37 = f32[32,1,128]{2,1,0:T(1,128)S(1)} all-to-all(f32[32,1,128]{2,1,0:T(1,128)S(1)} %bitcast.23), channel_id=1, replica_groups=mesh['tm'=8,'space'=32] {'space'}, dimensions={0} | all-to-all | bytes 32768 | tf_op jit(solution)/shard_map/all_to_all | solution.py:355
  70.3 3.4 %shard_map.71 = (f32[4,64,256]{2,1,0:T(8,128)S(1)}, f32[4,64,256]{2,1,0:T(8,128)S(1)}, f32[4,64,256]{2,1,0:T(8,128)S(1)}, f32[32,32,128]{2,1,0:T(8,128)S(1)}) custom-call(s32[2]{0:T(128)S(1)} %pad_add_fusion.where, f32[32,128]{1,0:T(8,128)S(1)} %bitcast.21, f32[9,64,256]{2,1,0:T(8,128)S(1)} %get-tuple-element.47.u, f32[9,64,256]{2,1,0:T(8,128)S(1)} %get-tuple-element.48.r, ...), custom_call_target="tpu_custom_call" | custom-call | tf_op jit(solution)/shard_map/pallas_call | solution.py:110
  73.7 14.9 %all_to_all.38.whole = f32[32,32,128]{2,1,0:T(8,128)S(1)} all-to-all(f32[32,32,128]{2,1,0:T(8,128)S(1)} %get-tuple-element.50), channel_id=1, replica_groups=mesh['tm'=8,'space'=32] {'space'}, dimensions={0} | all-to-all | bytes 1048576 | tf_op jit(solution)/shard_map/all_to_all | solution.py:355
  93.3 4.3 %collective-permute-done.4.refs_1_ = f32[32,8,128]{2,1,0:T(8,128)S(1)} collective-permute-done((f32[32,8,128]{2,1,0:T(8,128)S(1)}, f32[32,8,128]{2,1,0:T(8,128)S(1)}, u32[]{:S(2)}, u32[]{:S(2)}) %collective-permute-start.4) | collective-permute-done | bytes 131104 | tf_op jit(solution)/shard_map/ppermute | solution.py:351
  97.6 3.2 %collective-permute-start.7 = (f32[32,8,128]{2,1,0:T(8,128)S(1)}, f32[32,8,128]{2,1,0:T(8,128)S(1)}, u32[]{:S(2)}, u32[]{:S(2)}) collective-permute-start(f32[32,8,128]{2,1,0:T(8,128)S(1)} %collective-permute-done.5.refs_2_), channel_id=1, source_target_pairs={{0,224},{32,0},{64,32},{96,64},{128,96},{160,128},{192,160},{224,1... | collective-permute-start | bytes 393224 | tf_op jit(solution)/shard_map/ppermute | solution.py:351
  100.9 4.3 %collective-permute-done.6.refs_3_ = f32[32,8,128]{2,1,0:T(8,128)S(1)} collective-permute-done((f32[32,8,128]{2,1,0:T(8,128)S(1)}, f32[32,8,128]{2,1,0:T(8,128)S(1)}, u32[]{:S(2)}, u32[]{:S(2)}) %collective-permute-start.6) | collective-permute-done | bytes 131104 | tf_op jit(solution)/shard_map/ppermute | solution.py:351
  109.5 3.3 %collective-permute-start.9 = (f32[32,8,128]{2,1,0:T(8,128)S(1)}, f32[32,8,128]{2,1,0:T(8,128)S(1)}, u32[]{:S(2)}, u32[]{:S(2)}) collective-permute-start(f32[32,8,128]{2,1,0:T(8,128)S(1)} %collective-permute-done.7.refs_4_), channel_id=1, source_target_pairs={{0,224},{32,0},{64,32},{96,64},{128,96},{160,128},{192,160},{224,1... | collective-permute-start | bytes 393224 | tf_op jit(solution)/shard_map/ppermute | solution.py:351
  116.3 3.4 %collective-permute-done.10.refs_7_ = f32[32,8,128]{2,1,0:T(8,128)S(1)} collective-permute-done((f32[32,8,128]{2,1,0:T(8,128)S(1)}, f32[32,8,128]{2,1,0:T(8,128)S(1)}, u32[]{:S(2)}, u32[]{:S(2)}) %collective-permute-start.10) | collective-permute-done | bytes 131104 | tf_op jit(solution)/shard_map/ppermute | solution.py:351
  119.7 9.6 %shard_map.73 = (f32[64,128]{1,0:T(8,128)S(1)}, f32[8,16,16,128]{3,2,1,0:T(8,128)S(1)}, f32[16,16,128]{2,1,0:T(8,128)S(1)}) custom-call(s32[2]{0:T(128)S(1)} %pad_add_fusion.where, f32[8,128]{1,0:T(8,128)S(1)} %bitcast.18, f32[5,16,16,128]{3,2,1,0:T(8,128)S(1)} %get-tuple-element.37.static, f32[8,16,16,128]{3,2,1,0:T(8,128)S(1)} %get-tuple-element.38.before, ...), custom_call_target="tpu_custom_call" | custom-call | flops 67108864 | bytes 1048576 | tf_op jit(solution)/shard_map/pallas_call | solution.py:110
  129.4 4.0 %shard_map.74 = (f32[9,64,256]{2,1,0:T(8,128)S(1)}, f32[9,64,256]{2,1,0:T(8,128)S(1)}, f32[9,64,256]{2,1,0:T(8,128)S(1)}, f32[32,128]{1,0:T(8,128)S(1)}) custom-call(s32[2]{0:T(128)S(1)} %pad_add_fusion.where, f32[64,128]{1,0:T(8,128)S(1)} %get-tuple-element.58.planes, f32[4,64,256]{2,1,0:T(8,128)S(1)} %collective-permute-done.11.rest.rest_first, ...), custom_call_target="tpu_custom_call" | custom-call | tf_op jit(solution)/shard_map/pallas_call | solution.py:110
  133.4 11.5 %all_to_all.39 = f32[32,1,128]{2,1,0:T(1,128)S(1)} all-to-all(f32[32,1,128]{2,1,0:T(1,128)S(1)} %bitcast.22), channel_id=1, replica_groups=mesh['tm'=8,'space'=32] {'space'}, dimensions={0} | all-to-all | bytes 32768 | tf_op jit(solution)/shard_map/all_to_all | solution.py:355
  145.0 3.4 %shard_map.75 = (f32[4,64,256]{2,1,0:T(8,128)S(1)}, f32[4,64,256]{2,1,0:T(8,128)S(1)}, f32[4,64,256]{2,1,0:T(8,128)S(1)}, f32[32,32,128]{2,1,0:T(8,128)S(1)}) custom-call(s32[2]{0:T(128)S(1)} %pad_add_fusion.where, f32[32,128]{1,0:T(8,128)S(1)} %bitcast.20, f32[9,64,256]{2,1,0:T(8,128)S(1)} %get-tuple-element.60.u, f32[9,64,256]{2,1,0:T(8,128)S(1)} %get-tuple-element.61.r, ...), custom_call_target="tpu_custom_call" | custom-call | tf_op jit(solution)/shard_map/pallas_call | solution.py:110
  148.4 14.9 %all_to_all.40.whole = f32[32,32,128]{2,1,0:T(8,128)S(1)} all-to-all(f32[32,32,128]{2,1,0:T(8,128)S(1)} %get-tuple-element.63), channel_id=1, replica_groups=mesh['tm'=8,'space'=32] {'space'}, dimensions={0} | all-to-all | bytes 1048576 | tf_op jit(solution)/shard_map/all_to_all | solution.py:355
  168.0 3.5 %collective-permute-done.16.refs_1_ = f32[32,8,128]{2,1,0:T(8,128)S(1)} collective-permute-done((f32[32,8,128]{2,1,0:T(8,128)S(1)}, f32[32,8,128]{2,1,0:T(8,128)S(1)}, u32[]{:S(2)}, u32[]{:S(2)}) %collective-permute-start.16) | collective-permute-done | bytes 131104 | tf_op jit(solution)/shard_map/ppermute | solution.py:351
  173.4 3.3 %collective-permute-start.19 = (f32[32,8,128]{2,1,0:T(8,128)S(1)}, f32[32,8,128]{2,1,0:T(8,128)S(1)}, u32[]{:S(2)}, u32[]{:S(2)}) collective-permute-start(f32[32,8,128]{2,1,0:T(8,128)S(1)} %collective-permute-done.17.refs_2_), channel_id=1, source_target_pairs={{0,224},{32,0},{64,32},{96,64},{128,96},{160,128},{192,160},{224,1... | collective-permute-start | bytes 393224 | tf_op jit(solution)/shard_map/ppermute | solution.py:351
  179.2 3.7 %collective-permute-start.21 = (f32[32,8,128]{2,1,0:T(8,128)S(1)}, f32[32,8,128]{2,1,0:T(8,128)S(1)}, u32[]{:S(2)}, u32[]{:S(2)}) collective-permute-start(f32[32,8,128]{2,1,0:T(8,128)S(1)} %collective-permute-done.19.refs_4_), channel_id=1, source_target_pairs={{0,224},{32,0},{64,32},{96,64},{128,96},{160,128},{192,160},{224,1... | collective-permute-start | bytes 393224 | tf_op jit(solution)/shard_map/ppermute | solution.py:351
  186.1 6.2 %collective-permute-done.22.refs_7_ = f32[32,8,128]{2,1,0:T(8,128)S(1)} collective-permute-done((f32[32,8,128]{2,1,0:T(8,128)S(1)}, f32[32,8,128]{2,1,0:T(8,128)S(1)}, u32[]{:S(2)}, u32[]{:S(2)}) %collective-permute-start.22) | collective-permute-done | bytes 131104 | tf_op jit(solution)/shard_map/ppermute | solution.py:351
  192.3 6.5 %shard_map.77 = f32[4,64,256]{2,1,0:T(8,128)} custom-call(s32[2]{0:T(128)S(1)} %pad_add_fusion.where, f32[8,128]{1,0:T(8,128)S(1)} %bitcast.19, f32[5,16,16,128]{3,2,1,0:T(8,128)S(1)} %get-tuple-element.37.static, f32[8,16,16,128]{3,2,1,0:T(8,128)S(1)} %get-tuple-element.55.before, f32[16,16,128]{2,1,0:T(8,128)S(1)} %get-tuple-element.56.begin, ...), custom_call_target="tpu_custom_call" | custom-call | flops 67108864 | bytes 1048576 | tf_op jit(solution)/shard_map/pallas_call | solution.py:110
  (59 shorter events, 39.0 us)
Async XLA Ops:
  8.2 46.5 %collective-permute-start.2 = (f32[13,64,256]{2,1,0:T(8,128)}, f32[13,64,256]{2,1,0:T(8,128)S(1)}, u32[]{:S(2)}, u32[]{:S(2)}) collective-permute-start(f32[13,64,256]{2,1,0:T(8,128)} %get-tuple-element.42), channel_id=1, source_target_pairs={{1,0},{2,1},{3,2},{4,3},{5,4},{6,5},{7,6},{8,7},{9,8},{10,9},{11,1... | collective-permute-start | bytes 2555912 | tf_op jit(solution)/shard_map/ppermute | solution.py:351
  9.6 11.8 %collective-permute-start = (f32[1,128]{1,0:T(1,128)S(1)}, f32[1,128]{1,0:T(1,128)S(1)}, u32[]{:S(2)}, u32[]{:S(2)}) collective-permute-start(f32[1,128]{1,0:T(1,128)S(1)} %pad.4), channel_id=1, source_target_pairs={{0,0},{8,8},{16,16},{24,24},{32,1},{40,9},{48,17},{56,25},{64,2},{... | collective-permute-start | bytes 1544 | tf_op jit(solution)/shard_map/ppermute | solution.py:389
  23.0 22.2 %all-to-all-start = ((f32[32,48,128]{2,1,0:T(8,128)}), f32[32,48,128]{2,1,0:T(8,128)S(1)}, u32[]{:S(2)}, u32[]{:S(2)}) async-start(f32[32,48,128]{2,1,0:T(8,128)} %dynamic_update_slice.3), calls=%async_computation | async-start | bytes 1572864 | tf_op jit(solution)/shard_map/all_to_all | solution.py:355
  30.6 24.1 %collective-permute-start.1 = (f32[10,64,256]{2,1,0:T(8,128)}, f32[10,64,256]{2,1,0:T(8,128)S(1)}, u32[]{:S(2)}, u32[]{:S(2)}) collective-permute-start(f32[10,64,256]{2,1,0:T(8,128)} %copy-done.6), channel_id=1, source_target_pairs={{0,1},{1,2},{2,3},{3,4},{4,5},{5,6},{6,7},{7,8},{8,9},{9,10},{10,1... | collective-permute-start | bytes 1966088 | tf_op jit(solution)/shard_map/ppermute | solution.py:351
  32.9 21.8 %collective-permute-start.3 = (f32[1,64,256]{2,1,0:T(8,128)S(1)}, f32[1,64,256]{2,1,0:T(8,128)S(1)}, u32[]{:S(2)}, u32[]{:S(2)}) collective-permute-start(f32[1,64,256]{2,1,0:T(8,128)S(1)} %get-tuple-element.43), channel_id=1, source_target_pairs={{2,0},{3,1},{4,2},{5,3},{6,4},{7,5},{8,6},{9,7},{10,8},{11,9},{12,... | collective-permute-start | bytes 196616 | tf_op jit(solution)/shard_map/ppermute | solution.py:351
  90.0 7.6 %collective-permute-start.4 = (f32[32,8,128]{2,1,0:T(8,128)S(1)}, f32[32,8,128]{2,1,0:T(8,128)S(1)}, u32[]{:S(2)}, u32[]{:S(2)}) collective-permute-start(f32[32,8,128]{2,1,0:T(8,128)S(1)} %get-tuple-element.54.refs_0_), channel_id=1, source_target_pairs={{0,32},{32,64},{64,96},{96,128},{128,160},{160,192},{192,224},{224... | collective-permute-start | bytes 393224 | tf_op jit(solution)/shard_map/ppermute | solution.py:351
  90.0 15.2 %collective-permute-start.11 = (f32[4,64,256]{2,1,0:T(8,128)S(1)}, f32[4,64,256]{2,1,0:T(8,128)S(1)}, u32[]{:S(2)}, u32[]{:S(2)}) collective-permute-start(f32[4,64,256]{2,1,0:T(8,128)S(1)} %get-tuple-element.57), channel_id=1, source_target_pairs={{0,32},{32,64},{64,96},{96,128},{128,160},{160,192},{192,224},{224... | collective-permute-start | bytes 786440 | tf_op jit(solution)/shard_map/ppermute | solution.py:351
  90.8 6.8 %collective-permute-start.5 = (f32[32,8,128]{2,1,0:T(8,128)S(1)}, f32[32,8,128]{2,1,0:T(8,128)S(1)}, u32[]{:S(2)}, u32[]{:S(2)}) collective-permute-start(f32[32,8,128]{2,1,0:T(8,128)S(1)} %get-tuple-element.54.refs_0_), channel_id=1, source_target_pairs={{0,224},{32,0},{64,32},{96,64},{128,96},{160,128},{192,160},{224,1... | collective-permute-start | bytes 393224 | tf_op jit(solution)/shard_map/ppermute | solution.py:351
  97.6 7.6 %collective-permute-start.6 = (f32[32,8,128]{2,1,0:T(8,128)S(1)}, f32[32,8,128]{2,1,0:T(8,128)S(1)}, u32[]{:S(2)}, u32[]{:S(2)}) collective-permute-start(f32[32,8,128]{2,1,0:T(8,128)S(1)} %collective-permute-done.4.refs_1_), channel_id=1, source_target_pairs={{0,32},{32,64},{64,96},{96,128},{128,160},{160,192},{192,224},{224... | collective-permute-start | bytes 393224 | tf_op jit(solution)/shard_map/ppermute | solution.py:351
  97.6 11.9 %collective-permute-start.7 = (f32[32,8,128]{2,1,0:T(8,128)S(1)}, f32[32,8,128]{2,1,0:T(8,128)S(1)}, u32[]{:S(2)}, u32[]{:S(2)}) collective-permute-start(f32[32,8,128]{2,1,0:T(8,128)S(1)} %collective-permute-done.5.refs_2_), channel_id=1, source_target_pairs={{0,224},{32,0},{64,32},{96,64},{128,96},{160,128},{192,160},{224,1... | collective-permute-start | bytes 393224 | tf_op jit(solution)/shard_map/ppermute | solution.py:351
  105.2 7.7 %collective-permute-start.8 = (f32[32,8,128]{2,1,0:T(8,128)S(1)}, f32[32,8,128]{2,1,0:T(8,128)S(1)}, u32[]{:S(2)}, u32[]{:S(2)}) collective-permute-start(f32[32,8,128]{2,1,0:T(8,128)S(1)} %collective-permute-done.6.refs_3_), channel_id=1, source_target_pairs={{0,32},{32,64},{64,96},{96,128},{128,160},{160,192},{192,224},{224... | collective-permute-start | bytes 393224 | tf_op jit(solution)/shard_map/ppermute | solution.py:351
  105.2 24.2 %collective-permute-start.13 = (f32[4,64,256]{2,1,0:T(8,128)S(1)}, f32[4,64,256]{2,1,0:T(8,128)S(1)}, u32[]{:S(2)}, u32[]{:S(2)}) collective-permute-start(f32[4,64,256]{2,1,0:T(8,128)S(1)} %collective-permute-done.11.rest.rest_first), channel_id=1, source_target_pairs={{1,0},{2,1},{3,2},{4,3},{5,4},{6,5},{7,6},{8,7},{9,8},{10,9},{11,1... | collective-permute-start | bytes 786440 | tf_op jit(solution)/shard_map/ppermute | solution.py:351
  106.5 22.9 %collective-permute-start.12 = (f32[4,64,256]{2,1,0:T(8,128)S(1)}, f32[4,64,256]{2,1,0:T(8,128)S(1)}, u32[]{:S(2)}, u32[]{:S(2)}) collective-permute-start(f32[4,64,256]{2,1,0:T(8,128)S(1)} %collective-permute-done.11.rest.rest_first), channel_id=1, source_target_pairs={{0,1},{1,2},{2,3},{3,4},{4,5},{5,6},{6,7},{7,8},{8,9},{9,10},{10,1... | collective-permute-start | bytes 786440 | tf_op jit(solution)/shard_map/ppermute | solution.py:351
  109.5 6.8 %collective-permute-start.9 = (f32[32,8,128]{2,1,0:T(8,128)S(1)}, f32[32,8,128]{2,1,0:T(8,128)S(1)}, u32[]{:S(2)}, u32[]{:S(2)}) collective-permute-start(f32[32,8,128]{2,1,0:T(8,128)S(1)} %collective-permute-done.7.refs_4_), channel_id=1, source_target_pairs={{0,224},{32,0},{64,32},{96,64},{128,96},{160,128},{192,160},{224,1... | collective-permute-start | bytes 393224 | tf_op jit(solution)/shard_map/ppermute | solution.py:351
  112.9 6.9 %collective-permute-start.10 = (f32[32,8,128]{2,1,0:T(8,128)S(1)}, f32[32,8,128]{2,1,0:T(8,128)S(1)}, u32[]{:S(2)}, u32[]{:S(2)}) collective-permute-start(f32[32,8,128]{2,1,0:T(8,128)S(1)} %collective-permute-done.8.refs_5_), channel_id=1, source_target_pairs={{0,32},{32,64},{64,96},{96,128},{128,160},{160,192},{192,224},{224... | collective-permute-start | bytes 393224 | tf_op jit(solution)/shard_map/ppermute | solution.py:351
  112.9 16.5 %collective-permute-start.14 = (f32[1,64,256]{2,1,0:T(8,128)S(1)}, f32[1,64,256]{2,1,0:T(8,128)S(1)}, u32[]{:S(2)}, u32[]{:S(2)}) collective-permute-start(f32[1,64,256]{2,1,0:T(8,128)S(1)} %slice.9), channel_id=1, source_target_pairs={{2,0},{3,1},{4,2},{5,3},{6,4},{7,5},{8,6},{9,7},{10,8},{11,9},{12,... | collective-permute-start | bytes 196616 | tf_op jit(solution)/shard_map/ppermute | solution.py:351
  164.7 6.7 %collective-permute-start.16 = (f32[32,8,128]{2,1,0:T(8,128)S(1)}, f32[32,8,128]{2,1,0:T(8,128)S(1)}, u32[]{:S(2)}, u32[]{:S(2)}) collective-permute-start(f32[32,8,128]{2,1,0:T(8,128)S(1)} %get-tuple-element.68.refs_0_), channel_id=1, source_target_pairs={{0,32},{32,64},{64,96},{96,128},{128,160},{160,192},{192,224},{224... | collective-permute-start | bytes 393224 | tf_op jit(solution)/shard_map/ppermute | solution.py:351
  164.8 8.6 %collective-permute-start.17 = (f32[32,8,128]{2,1,0:T(8,128)S(1)}, f32[32,8,128]{2,1,0:T(8,128)S(1)}, u32[]{:S(2)}, u32[]{:S(2)}) collective-permute-start(f32[32,8,128]{2,1,0:T(8,128)S(1)} %get-tuple-element.68.refs_0_), channel_id=1, source_target_pairs={{0,224},{32,0},{64,32},{96,64},{128,96},{160,128},{192,160},{224,1... | collective-permute-start | bytes 393224 | tf_op jit(solution)/shard_map/ppermute | solution.py:351
  171.5 7.4 %collective-permute-start.18 = (f32[32,8,128]{2,1,0:T(8,128)S(1)}, f32[32,8,128]{2,1,0:T(8,128)S(1)}, u32[]{:S(2)}, u32[]{:S(2)}) collective-permute-start(f32[32,8,128]{2,1,0:T(8,128)S(1)} %collective-permute-done.16.refs_1_), channel_id=1, source_target_pairs={{0,32},{32,64},{64,96},{96,128},{128,160},{160,192},{192,224},{224... | collective-permute-start | bytes 393224 | tf_op jit(solution)/shard_map/ppermute | solution.py:351
  171.5 14.6 %collective-permute-start.15 = (f32[4,64,256]{2,1,0:T(8,128)S(1)}, f32[4,64,256]{2,1,0:T(8,128)S(1)}, u32[]{:S(2)}, u32[]{:S(2)}) collective-permute-start(f32[4,64,256]{2,1,0:T(8,128)S(1)} %get-tuple-element.67), channel_id=1, source_target_pairs={{0,32},{32,64},{64,96},{96,128},{128,160},{160,192},{192,224},{1,3... | collective-permute-start | bytes 786440 | tf_op jit(solution)/shard_map/ppermute | solution.py:351
  173.4 5.8 %collective-permute-start.19 = (f32[32,8,128]{2,1,0:T(8,128)S(1)}, f32[32,8,128]{2,1,0:T(8,128)S(1)}, u32[]{:S(2)}, u32[]{:S(2)}) collective-permute-start(f32[32,8,128]{2,1,0:T(8,128)S(1)} %collective-permute-done.17.refs_2_), channel_id=1, source_target_pairs={{0,224},{32,0},{64,32},{96,64},{128,96},{160,128},{192,160},{224,1... | collective-permute-start | bytes 393224 | tf_op jit(solution)/shard_map/ppermute | solution.py:351
  178.9 7.2 %collective-permute-start.20 = (f32[32,8,128]{2,1,0:T(8,128)S(1)}, f32[32,8,128]{2,1,0:T(8,128)S(1)}, u32[]{:S(2)}, u32[]{:S(2)}) collective-permute-start(f32[32,8,128]{2,1,0:T(8,128)S(1)} %collective-permute-done.18.refs_3_), channel_id=1, source_target_pairs={{0,32},{32,64},{64,96},{96,128},{128,160},{160,192},{192,224},{224... | collective-permute-start | bytes 393224 | tf_op jit(solution)/shard_map/ppermute | solution.py:351
  179.2 6.9 %collective-permute-start.21 = (f32[32,8,128]{2,1,0:T(8,128)S(1)}, f32[32,8,128]{2,1,0:T(8,128)S(1)}, u32[]{:S(2)}, u32[]{:S(2)}) collective-permute-start(f32[32,8,128]{2,1,0:T(8,128)S(1)} %collective-permute-done.19.refs_4_), channel_id=1, source_target_pairs={{0,224},{32,0},{64,32},{96,64},{128,96},{160,128},{192,160},{224,1... | collective-permute-start | bytes 393224 | tf_op jit(solution)/shard_map/ppermute | solution.py:351
  186.1 6.2 %collective-permute-start.22 = (f32[32,8,128]{2,1,0:T(8,128)S(1)}, f32[32,8,128]{2,1,0:T(8,128)S(1)}, u32[]{:S(2)}, u32[]{:S(2)}) collective-permute-start(f32[32,8,128]{2,1,0:T(8,128)S(1)} %collective-permute-done.20.refs_5_), channel_id=1, source_target_pairs={{0,32},{32,64},{64,96},{96,128},{128,160},{160,192},{192,224},{224... | collective-permute-start | bytes 393224 | tf_op jit(solution)/shard_map/ppermute | solution.py:351
  (7 other events, 14.8 us)

commit v2 on v1

--- a/solution.py
+++ b/solution.py
@@ -79,13 +79,15 @@
     step = norm / product
     direction, moved = residual, image
     for turn in range(CG_COARSE):
+        inverse = 1.0 / norm
+        scaled = inverse / step
         x = x + step[None] * direction
         if turn + 1 < CG_COARSE:
             residual = residual - step[None] * moved
             image = apply(residual)
             new, product = total(residual * residual), total(residual * image)
-            ratio = new / norm
-            step = new / (product - ratio * new / step)
+            ratio = new * inverse
+            step = new / (product - new * (new * scaled))
             direction = residual + ratio[None] * direction
             moved = image + ratio[None] * moved
             norm = new
@@ -119,7 +121,7 @@
     )(*args)
 
 
-def setup_kernel(cond, cur, labels, coils, initial, sigma, sources, up, down, far, packed):
+def setup_kernel(cond, cur, theirs, labels, coils, initial, sigma, sources, up, down, far, packed):
     region = labels[...]
     cell = jnp.where(region == 0, cond[0], 0.0)
     for k in range(1, 4):
@@ -142,7 +144,7 @@
     far[...] = initial[0:1]
     fields = [initial[...], cell, *pattern]
     rows = [restrict_packed(jnp.sum(f, axis=0)) for f in fields]
-    rows = jnp.concatenate([*rows, jnp.zeros((8, 128), F32)], axis=0)
+    rows = jnp.concatenate([*rows, jnp.broadcast_to(theirs[...], (8, 128))], axis=0)
     packed[...] = jnp.broadcast_to(rows[None], packed.shape)
 
 
@@ -182,25 +184,20 @@
     sweep(where, cur, state, static, advanced, planes, None, 8)
 
 
-def load_corrections(where, ends, before, correction):
-    for end, offset in zip(ends, OFFSETS):
-        n = (where[0] + offset) & 7
-        correction[n] = unpack(end[0:16], end[16:32]) - before[n]
-
-
-OFFSETS = (0, -1, 1, -2, 2, -3, 3, -4)
-
-
-def next_sweep_kernel(where, cur, static, before, begin, *refs):
-    ends, (planes, advanced, state, correction) = refs[:8], refs[8:]
-    load_corrections(where, ends, before, correction)
+def load_corrections(ends, before, correction):
+    for n in range(8):
+        correction[n] = unpack_all(ends, 8 * n) - before[n]
+
+
+def next_sweep_kernel(where, cur, static, before, begin, ends, planes, advanced, state, correction):
+    load_corrections(ends, before, correction)
     state[...] = begin[...]
     sweep(where, cur, state, static, advanced, planes, correction, 8)
 
 
-def last_sweep_kernel(where, cur, static, before, begin, rest_first, rest_other, *refs):
-    ends, (start, state, correction, planes) = refs[:8], refs[8:]
-    load_corrections(where, ends, before, correction)
+def last_sweep_kernel(where, cur, static, before, begin, rest_first, rest_other, ends,
+                      start, state, correction, planes):
+    load_corrections(ends, before, correction)
     state[...] = begin[...]
 
     def keep():
@@ -234,64 +231,17 @@
     return jnp.logical_and(plane >= 0, plane < 128).astype(F32)
 
 
-def each(pieces, body):
-    at = 0
-    for read, count in pieces:
-
-        def one(i, carry, read=read, at=at):
-            body(at + i, read(i))
-            return carry
-
-        lax.fori_loop(0, count, one, 0)
-        at += count
-
-
-def residual_planes(field, source, out, first):
-    def body(j, piece):
-        v = field[j + 1]
-        r = piece - 6.0 * v + (field[j] + field[j + 2]) + fine_beside(v)
-        out[j] = inside(first + j) * r
-
-    each(source, body)
-
-
-def image_planes(field, weight, out, first):
-    def body(j, piece):
-        v = field[j + 1]
-        w = (piece + 6.0) * v - (field[j] + field[j + 2]) - fine_beside(v)
-        out[j] = inside(first + j) * w
-
-    each(weight, body)
-
-
-def moments(r, r_at, w, w_at, sigma):
-    def body(i, sums):
-        a, b, c = r[r_at + i], w[w_at + i], w[w_at + i + 1]
-        cross = (sigma[i] + 6.0) * b - fine_beside(b) - 2.0 * c
-        return (sums[0] + a * a, sums[1] + a * b, sums[2] + b * b, sums[3] + b * cross)
-
-    zero = jnp.zeros((64, 256), F32)
-    sums = lax.fori_loop(0, 4, body, (zero,) * 4)
-    lane = iota((1, 128), 1)
-    row = jnp.zeros((1, 128), F32)
-    for k in range(4):
-        row = jnp.where(lane == k, total(sums[k]), row)
-    return row
-
-
-def weights(row):
-    lane = iota((1, 128), 1)
-    m0, m1, m2, m3 = (jnp.sum(jnp.where(lane == k, row, 0.0), axis=1, keepdims=True) for k in range(4))
-    step = m0 / m1
-    new = step * step * m2 - m0
-    product = m1 - 2.0 * step * m2 + step * step * m3
-    ratio = new / m0
-    second = new / (product - ratio * new / step)
-    return step + second * (1.0 + ratio), -step * second
-
-
-def fine_one_kernel(initial, where, planes, rest, rest_up, rest_down, rest_far, sigma, sources, up, down,
-                    u_out, r_out, w_out, packed, u, r):
+def guarded(value, plane, first):
+    return value if 0 <= plane < 4 else inside(first + plane) * value
+
+
+def part(value):
+    folded = jnp.sum(value.reshape(8, 8, 256), axis=0)
+    return folded[:, :128] + folded[:, 128:]
+
+
+def fine_kernel(initial, where, planes, rest, rest_up, rest_down, rest_far, sigma, sources, up, down,
+                fields, packed, u, r, w, q, a):
     first = 4 * where[1]
     zero = (where[0] == 0).astype(F32)
     scale = (1.0 - zero, zero) if initial else (1.0, 1.0 - zero)
@@ -301,48 +251,100 @@
     pieces = pieces + [(rest_down, below + k) for k in range(4)] + [(rest_far, 0)]
     for j, (piece, k) in enumerate(pieces):
         u[j] = scale[0] * lifted[j // 4] + scale[1] * piece[k]
-    source = ((lambda i: up[2 + i], 3), (lambda i: sources[0, i], 4), (lambda i: down[3 + i], 4))
-    residual_planes(u, source, r, first - 3)
-    weight = ((lambda i: up[i], 2), (lambda i: sigma[i], 4), (lambda i: down[i], 3))
-    image_planes(r, weight, w_out, first - 2)
-    u_out[...] = u[2:11]
-    r_out[...] = r[1:10]
-    packed[...] = jnp.broadcast_to(moments(r, 3, w_out, 2, sigma), packed.shape)
-
-
-def fine_two_kernel(where, sums, u, r, w, sigma, sources, up, down, u_out, r_out, w_out, packed, u1, r1, w1):
-    first = 4 * where[1]
-    a, b = weights(jnp.sum(sums[...], axis=0, keepdims=True))
-
-    def move(j, carry):
-        u1[j] = u[j] + a * r[j] + b * w[j]
-        return carry
-
-    lax.fori_loop(0, 9, move, 0)
-    source = ((lambda i: up[5 + i], 1), (lambda i: sources[1, i], 4), (lambda i: down[7 + i], 2))
-    residual_planes(u1, source, r1, first - 1)
-    weight = ((lambda i: sigma[i], 4), (lambda i: down[i], 1))
-    image_planes(r1, weight, w1, first)
-    u_out[...] = u1[2:6]
-    r_out[...] = r1[1:5]
-    w_out[...] = w1[0:4]
-    row = moments(r1, 1, w1, 0, sigma)
-    parts = [restrict_packed(jnp.sum(f[...], axis=0)) for f in (u_out, r_out, w_out)]
-    rows = jnp.concatenate([*parts, jnp.broadcast_to(row, (8, 128))], axis=0)
-    packed[...] = jnp.broadcast_to(rows[None], packed.shape)
-
-
-def fine_three_kernel(where, whole, u, r, w, fine, rest, ends):
-    a, b = weights(jnp.sum(whole[:, 24, :], axis=0, keepdims=True))
-    ends[...] = whole[:, 0:8, :] + a[None] * whole[:, 8:16, :] + b[None] * whole[:, 16:24, :]
-    own = ends[where[1]]
+
+    def weight(plane):
+        return up[2 + plane] if plane < 0 else sigma[plane] if plane < 4 else down[plane - 4]
+
+    def source(step, plane):
+        before, after = ((5, 3), (6, 7))[step]
+        return up[before + plane] if plane < 0 else sources[step, plane] if plane < 4 else down[after + plane - 4]
+
+    def spread(field, low, plane):
+        j = plane - low
+        v = field[j]
+        return field[j - 1] + field[j + 1] + fine_beside(v) - 6.0 * v
+
+    for plane in range(-3, 8):
+        r[plane + 3] = guarded(source(0, plane) + spread(u, -4, plane), plane, first)
+    for plane in range(-2, 7):
+        w[plane + 2] = guarded(weight(plane) * r[plane + 3] - spread(r, -3, plane), plane, first)
+    for plane in range(-1, 6):
+        q[0, plane + 1] = guarded(source(1, plane) + spread(u, -4, plane), plane, first)
+        q[1, plane + 1] = guarded(spread(r, -3, plane), plane, first)
+        q[2, plane + 1] = guarded(spread(w, -2, plane), plane, first)
+    for plane in range(5):
+        for k in range(3):
+            image = weight(plane) * q[k, plane + 1] - spread(q.at[k], -1, plane)
+            a[k, plane] = guarded(image, plane, first)
+    sums = [jnp.zeros((8, 128), F32)] * 28
+    for plane in range(4):
+        terms = []
+        rv, wv = r[plane + 3], w[plane + 2]
+        heavy = weight(plane) + 6.0
+        terms += [rv * rv, rv * wv, wv * wv]
+        terms += [wv * (heavy * wv - fine_beside(wv) - 2.0 * w[plane + 3])]
+        qs = [q[k, plane + 1] for k in range(3)]
+        images = [a[k, plane] for k in range(3)]
+        twice = []
+        for k in range(3):
+            value = heavy * images[k] - fine_beside(images[k]) - a[k, plane + 1]
+            twice.append(value - a[k, plane - 1] if plane else value)
+        for i, j in PAIRS:
+            last = images[i] * twice[j]
+            if plane == 3:
+                last = last - a[i, 4] * images[j]
+            terms += [qs[i] * qs[j], qs[i] * images[j], images[i] * images[j], last]
+        sums = [s + part(v) for s, v in zip(sums, terms)]
+    lane = iota((1, 128), 1)
+    row = jnp.zeros((1, 128), F32)
+    for k in range(28):
+        row = jnp.where(lane == k, total(sums[k]), row)
+    packed[...] = jnp.broadcast_to(row, packed.shape)
+    fields[0] = u[4:8]
+    fields[1] = r[3:7]
+    fields[2] = w[2:6]
+    for k in range(3):
+        fields[3 + k] = q[k, 1:5]
+        fields[6 + k] = a[k, 0:4]
+
+
+PAIRS = ((0, 0), (0, 1), (0, 2), (1, 1), (1, 2), (2, 2))
+
+
+def weights(m0, m1, m2, m3):
+    step = m0 / m1
+    new = step * step * m2 - m0
+    product = m1 - 2.0 * step * m2 + step * step * m3
+    ratio = new / m0
+    second = new / (product - ratio * new / step)
+    return step + second * (1.0 + ratio), -step * second
+
+
+def finish_kernel(sums, fields, fine, rest, ends):
+    row = jnp.sum(sums[...], axis=0, keepdims=True)
+    lane = iota((1, 128), 1)
+    m = [jnp.sum(jnp.where(lane == k, row, 0.0), axis=1, keepdims=True) for k in range(28)]
+    a, b = weights(*m[:4])
+    factor = {(0, 0): 1.0, (0, 1): 2.0 * a, (0, 2): 2.0 * b, (1, 1): a * a, (1, 2): 2.0 * (a * b), (2, 2): b * b}
+    after = [sum(factor[pair] * m[4 + 4 * p + k] for p, pair in enumerate(PAIRS)) for k in range(4)]
+    c, d = weights(*after)
+    scales = (None, a, b, c, c * a, c * b, d, d * a, d * b)
+    for i in range(4):
+        value = fields[0, i]
+        for k in range(1, 9):
+            value = value + scales[k] * fields[k, i]
+        fine[i] = value
+    own = restrict_packed(jnp.sum(fine[...], axis=0))
+    ends[...] = jnp.broadcast_to(own[None], ends.shape)
     left = iota((8, 128), 1) < 64
     plane = jnp.concatenate([jnp.where(left, own, 0.0), jnp.where(left, pltpu.roll(own, 64, 1), 0.0)], axis=0)
     (lifted,) = widen(plane)
     for i in range(4):
-        value = u[i] + a * r[i] + b * w[i]
-        fine[i] = value
-        rest[i] = value - lifted
+        rest[i] = fine[i] - lifted
+
+
+def spread_kernel(ends, packed):
+    packed[...] = jnp.broadcast_to(ends[...].reshape(1, 64, 128), packed.shape)
 
 
 def shifted(x, axis, by, ring):
@@ -355,15 +357,9 @@
     return lax.all_to_all(x, axis, split_axis=0, concat_axis=0, tiled=True)
 
 
-def around(x):
-    ends, ahead, behind = [x], x, x
-    for k in range(1, 5):
-        ahead = shifted(ahead, "tm", 1, True)
-        ends.append(ahead)
-        if k < 4:
-            behind = shifted(behind, "tm", -1, True)
-            ends.append(behind)
-    return ends
+def everywhere(ends):
+    (packed,) = call(spread_kernel, ((32, 64, 128),), (exchange(ends, "tm"),))
+    return exchange(packed, "space")
 
 
 def halos(x):
@@ -391,10 +387,9 @@
     sigma, sources, up, down, far, packed = call(
         setup_kernel,
         (block, (2, *block), (10, 64, 256), (13, 64, 256), (1, 64, 256), (32, 48, 128)),
-        (conductivity, currents[0], labels, coil_pattern, initial_state),
+        (conductivity, currents[0], theirs, labels, coil_pattern, initial_state),
         small=(0, 1),
     )
-    packed = lax.dynamic_update_slice(packed, jnp.broadcast_to(theirs[None], (32, 1, 128)), (0, 40, 0))
     whole = exchange(packed, "space")
     table = whole[:8, 40, :]
     up, down = shifted(up, "space", 1, False), shifted(down, "space", -1, False)
@@ -408,25 +403,17 @@
     )
 
     def fine(initial, planes, rest, around_rest):
-        u, r, w, sums = call(
-            functools.partial(fine_one_kernel, initial),
-            ((9, 64, 256), (9, 64, 256), (9, 64, 256), (32, 128)),
+        fields, sums = call(
+            functools.partial(fine_kernel, initial),
+            ((9, *block), (32, 128)),
             (where, planes, rest, *around_rest, sigma, sources, up, down),
             small=(0,),
-            scratch=((13, 64, 256), (11, 64, 256)),
-        )
-        u, r, w, packed = call(
-            fine_two_kernel,
-            (block, block, block, (32, 32, 128)),
-            (where, exchange(sums, "space"), u, r, w, sigma, sources, up, down),
-            small=(0,),
-            scratch=((9, 64, 256), (7, 64, 256), (5, 64, 256)),
+            scratch=((13, 64, 256), (11, 64, 256), (9, 64, 256), (3, 7, 64, 256), (3, 5, 64, 256)),
         )
         return call(
-            fine_three_kernel,
-            (block, block, (32, 8, 128)),
-            (where, exchange(packed, "space"), u, r, w),
-            small=(0,),
+            finish_kernel,
+            (block, block, (8, 8, 128)),
+            (exchange(sums, "space"), fields),
         )
 
     _, rest, ends = fine(True, planes, initial_state, (up, down, far))
@@ -434,7 +421,7 @@
     planes, advanced_next, state_next = call(
         next_sweep_kernel,
         ((64, 128), (8, *field), field),
-        (where, table, static, advanced, state, *around(ends)),
+        (where, table, static, advanced, state, everywhere(ends)),
         small=(0, 1),
         scratch=((8, *field),),
         flops=1 << 26,
@@ -444,7 +431,7 @@
     (start,) = call(
         last_sweep_kernel,
         (block,),
-        (where, table, static, advanced_next, state_next, rest_first, rest_other, *around(ends)),
+        (where, table, static, advanced_next, state_next, rest_first, rest_other, everywhere(ends)),
         small=(0, 1),
         scratch=(field, (8, *field), (16, 128)),
         flops=1 << 26,

time: 199 us -> 189 us (0.950)
  the two profiles are of different devices: /device:TPU:128 before, /device:TPU:225 now
where the time goes in v2:
time: 189 us; the launch traced here: 188 us
  blocking collectives  49.3 us (26%)
  Pallas kernels  45 us (24%)
  starting transfers between devices  41.5 us (22%)
  waiting for transfers between devices  37.5 us (20%)
  local copies, waits for them, and re-layouts  14.1 us (7%)
    all_to_all x4, blocking collectives, exchange(): return lax.all_to_all(x, axis, split_axis=0, concat_axis=0, tiled=True)  49.3 us
    pallas_call x10, Pallas kernels, call(): pl.pallas_call(body, out_shape=tuple((jax.ShapeDtypeStruct(s, F32) for s...  45 us
    all_to_all x3, starting transfers between devices, exchange(): return lax.all_to_all(x, axis, split_axis=0, concat_axis=0, tiled=True)  20.2 us
    ppermute x8, starting transfers between devices, shifted(): return lax.ppermute(x, axis, pairs)  18.8 us
    all_to_all x3, waiting for transfers between devices, exchange(): return lax.all_to_all(x, axis, split_axis=0, concat_axis=0, tiled=True)  17.5 us
    ppermute x8, waiting for transfers between devices, shifted(): return lax.ppermute(x, axis, pairs)  14 us
    unnamed x46, local copies, waits for them, and re-layouts  12.7 us
    ppermute x1, waiting for transfers between devices, body(): lax.ppermute(jnp.pad(currents.reshape(1, 6), ((0, 0), (0, 122))), ('tm',...  5.97 us
  transfers between devices with their start and end apart: 12, of which 6 were waited for; matrix products, arithmetic and copies ran while one was open for 0% of the time, Pallas kernels for 10%

profile of v2, /device:TPU:225, one launch (start us, length us, event | category | flops | bytes accessed | tf_op | source)
XLA Modules:
  0.0 188.3 jit_solution(11209708683386947696)
XLA Ops:
  1.4 2.5 %collective-permute-start = (f32[1,128]{1,0:T(1,128)S(1)}, f32[1,128]{1,0:T(1,128)S(1)}, u32[]{:S(2)}, u32[]{:S(2)}) collective-permute-start(f32[1,128]{1,0:T(1,128)S(1)} %pad.4), channel_id=1, source_target_pairs={{0,0},{8,8},{16,16},{24,24},{32,1},{40,9},{48,17},{56,25},{64,2},{... | collective-permute-start | bytes 1544 | tf_op jit(solution)/shard_map/ppermute | solution.py:385
  4.0 6.0 %collective-permute-done.theirs = f32[1,128]{1,0:T(1,128)S(1)} collective-permute-done((f32[1,128]{1,0:T(1,128)S(1)}, f32[1,128]{1,0:T(1,128)S(1)}, u32[]{:S(2)}, u32[]{:S(2)}) %collective-permute-start) | collective-permute-done | bytes 544 | tf_op jit(solution)/shard_map/ppermute | solution.py:385
  14.3 2.9 %shard_map.68 = (f32[4,64,256]{2,1,0:T(8,128)S(1)}, f32[2,4,64,256]{3,2,1,0:T(8,128)S(1)}, f32[10,64,256]{2,1,0:T(8,128)}, f32[13,64,256]{2,1,0:T(8,128)}, f32[1...) custom-call(f32[4]{0:T(128)S(1)} %copy-done.20, f32[2,3]{1,0:T(2,128)S(1)} %bitcast.23, ...), custom_call_target="tpu_custom_call" | custom-call | tf_op jit(solution)/shard_map/pallas_call | solution.py:112
  18.0 2.2 %collective-permute-start.2 = (f32[13,64,256]{2,1,0:T(8,128)}, f32[13,64,256]{2,1,0:T(8,128)S(1)}, u32[]{:S(2)}, u32[]{:S(2)}) collective-permute-start(f32[13,64,256]{2,1,0:T(8,128)} %get-tuple-element.30), channel_id=1, source_target_pairs={{1,0},{2,1},{3,2},{4,3},{5,4},{6,5},{7,6},{8,7},{9,8},{10,9},{11,1... | collective-permute-start | bytes 2555912 | tf_op jit(solution)/shard_map/ppermute | solution.py:353
  20.3 9.5 %all-to-all-start = ((f32[32,48,128]{2,1,0:T(8,128)}), f32[32,48,128]{2,1,0:T(8,128)S(1)}, u32[]{:S(2)}, u32[]{:S(2)}) async-start(f32[32,48,128]{2,1,0:T(8,128)} %copy-done.13), calls=%async_computation | async-start | bytes 1572864 | tf_op jit(solution)/shard_map/all_to_all | solution.py:357
  29.8 3.5 %collective-permute-start.1 = (f32[10,64,256]{2,1,0:T(8,128)}, f32[10,64,256]{2,1,0:T(8,128)S(1)}, u32[]{:S(2)}, u32[]{:S(2)}) collective-permute-start(f32[10,64,256]{2,1,0:T(8,128)} %get-tuple-element.29), channel_id=1, source_target_pairs={{0,1},{1,2},{2,3},{3,4},{4,5},{5,6},{6,7},{7,8},{8,9},{9,10},{10,1... | collective-permute-start | bytes 1966088 | tf_op jit(solution)/shard_map/ppermute | solution.py:353
  34.7 9.5 %all-to-all-done.whole = f32[32,48,128]{2,1,0:T(8,128)S(1)} async-done(((f32[32,48,128]{2,1,0:T(8,128)}), f32[32,48,128]{2,1,0:T(8,128)S(1)}, u32[]{:S(2)}, u32[]{:S(2)}) %all-to-all-start) | async-done | bytes 786464 | tf_op jit(solution)/shard_map/all_to_all | solution.py:357
  44.2 9.5 %shard_map.69 = (f32[5,16,16,128]{3,2,1,0:T(8,128)S(1)}, f32[64,128]{1,0:T(8,128)S(1)}, f32[8,16,16,128]{3,2,1,0:T(8,128)S(1)}, f32[16,16,128]{2,1,0:T(8,128)S(1)}) custom-call(s32[2]{0:T(128)S(1)} %pad_add_fusion.where, f32[8,128]{1,0:T(8,128)S(1)} %bitcast.16, f32[32,48,128]{2,1,0:T(8,128)S(1)} %all-to-all-done.whole), custom_call_target="tpu_custom_call" | custom-call | flops 67108864 | bytes 1048576 | tf_op jit(solution)/shard_map/pallas_call | solution.py:112
  56.4 4.4 %shard_map.70 = (f32[9,4,64,256]{3,2,1,0:T(8,128)S(1)}, f32[32,128]{1,0:T(8,128)S(1)}) custom-call(s32[2]{0:T(128)S(1)} %pad_add_fusion.where, f32[64,128]{1,0:T(8,128)S(1)} %get-tuple-element.28.planes, f32[4,64,256]{2,1,0:T(8,128)S(1)} %copy-done.7, f32[10,64,256]{2,1,0:T(8,128)S(1)} %collective-permute-done.1.rest_up.up, ...), custom_call_target="tpu_custom_call" | custom-call | tf_op jit(solution)/shard_map/pallas_call | solution.py:112
  60.9 13.1 %all_to_all.47 = f32[32,1,128]{2,1,0:T(1,128)S(1)} all-to-all(f32[32,1,128]{2,1,0:T(1,128)S(1)} %bitcast.22), channel_id=1, replica_groups=mesh['tm'=8,'space'=32] {'space'}, dimensions={0} | all-to-all | bytes 32768 | tf_op jit(solution)/shard_map/all_to_all | solution.py:357
  75.3 10.4 %all_to_all.48.ends = f32[8,8,128]{2,1,0:T(8,128)S(1)} all-to-all(f32[8,8,128]{2,1,0:T(8,128)S(1)} %get-tuple-element.36), channel_id=1, replica_groups=mesh['tm'=8,'space'=32] {'tm'}, dimensions={0} | all-to-all | bytes 65536 | tf_op jit(solution)/shard_map/all_to_all | solution.py:357
  86.8 5.5 %all-to-all-start.3 = ((f32[32,64,128]{2,1,0:T(8,128)}), f32[32,64,128]{2,1,0:T(8,128)S(1)}, u32[]{:S(2)}, u32[]{:S(2)}) async-start(f32[32,64,128]{2,1,0:T(8,128)} %copy-done), calls=%async_computation.3 | async-start | bytes 2097152 | tf_op jit(solution)/shard_map/all_to_all | solution.py:357
  92.4 2.6 %collective-permute-start.4 = (f32[4,64,256]{2,1,0:T(8,128)}, f32[4,64,256]{2,1,0:T(8,128)S(1)}, u32[]{:S(2)}, u32[]{:S(2)}) collective-permute-start(f32[4,64,256]{2,1,0:T(8,128)} %copy-done.21), channel_id=1, source_target_pairs={{0,32},{32,64},{64,96},{96,128},{128,160},{160,192},{192,224},{224... | collective-permute-start | bytes 786440 | tf_op jit(solution)/shard_map/ppermute | solution.py:353
  95.0 5.6 %collective-permute-done.4.rest.rest_first = f32[4,64,256]{2,1,0:T(8,128)S(1)} collective-permute-done((f32[4,64,256]{2,1,0:T(8,128)}, f32[4,64,256]{2,1,0:T(8,128)S(1)}, u32[]{:S(2)}, u32[]{:S(2)}) %collective-permute-start.4) | collective-permute-done | bytes 262176 | tf_op jit(solution)/shard_map/ppermute | solution.py:353
  100.6 4.4 %collective-permute-start.5 = (f32[4,64,256]{2,1,0:T(8,128)S(1)}, f32[4,64,256]{2,1,0:T(8,128)}, u32[]{:S(2)}, u32[]{:S(2)}) collective-permute-start(f32[4,64,256]{2,1,0:T(8,128)S(1)} %collective-permute-done.4.rest.rest_first), channel_id=1, source_target_pairs={{0,1},{1,2},{2,3},{3,4},{4,5},{5,6},{6,7},{7,8},{8,9},{9,10},{10,1... | collective-permute-start | bytes 786440 | tf_op jit(solution)/shard_map/ppermute | solution.py:353
  105.0 1.9 %collective-permute-start.6 = (f32[4,64,256]{2,1,0:T(8,128)S(1)}, f32[4,64,256]{2,1,0:T(8,128)}, u32[]{:S(2)}, u32[]{:S(2)}) collective-permute-start(f32[4,64,256]{2,1,0:T(8,128)S(1)} %collective-permute-done.4.rest.rest_first), channel_id=1, source_target_pairs={{1,0},{2,1},{3,2},{4,3},{5,4},{6,5},{7,6},{8,7},{9,8},{10,9},{11,1... | collective-permute-start | bytes 786440 | tf_op jit(solution)/shard_map/ppermute | solution.py:353
  111.7 9.6 %shard_map.73 = (f32[64,128]{1,0:T(8,128)S(1)}, f32[8,16,16,128]{3,2,1,0:T(8,128)S(1)}, f32[16,16,128]{2,1,0:T(8,128)S(1)}) custom-call(s32[2]{0:T(128)S(1)} %pad_add_fusion.where, f32[8,128]{1,0:T(8,128)S(1)} %bitcast.17, f32[5,16,16,128]{3,2,1,0:T(8,128)S(1)} %get-tuple-element.25.static, f32[8,16,16,128]{3,2,1,0:T(8,128)S(1)} %copy-done.9, ...), custom_call_target="tpu_custom_call" | custom-call | flops 67108864 | bytes 1048576 | tf_op jit(solution)/shard_map/pallas_call | solution.py:112
  123.0 4.9 %shard_map.74 = (f32[9,4,64,256]{3,2,1,0:T(8,128)S(1)}, f32[32,128]{1,0:T(8,128)S(1)}) custom-call(s32[2]{0:T(128)S(1)} %pad_add_fusion.where, f32[64,128]{1,0:T(8,128)S(1)} %get-tuple-element.40.planes, f32[4,64,256]{2,1,0:T(8,128)S(1)} %collective-permute-done.4.rest.rest_first, f32[4,64,256]{2,1,0:T(8,128)} %collective-permute-done.5.rest_up, ...), custom_call_target="tpu_custom_call" | custom-call | tf_op jit(solution)/shard_map/pallas_call | solution.py:112
  128.0 15.7 %all_to_all.49 = f32[32,1,128]{2,1,0:T(1,128)S(1)} all-to-all(f32[32,1,128]{2,1,0:T(1,128)S(1)} %bitcast.21), channel_id=1, replica_groups=mesh['tm'=8,'space'=32] {'space'}, dimensions={0} | all-to-all | bytes 32768 | tf_op jit(solution)/shard_map/all_to_all | solution.py:357
  145.0 10.1 %all_to_all.50.ends = f32[8,8,128]{2,1,0:T(8,128)S(1)} all-to-all(f32[8,8,128]{2,1,0:T(8,128)S(1)} %get-tuple-element.44), channel_id=1, replica_groups=mesh['tm'=8,'space'=32] {'tm'}, dimensions={0} | all-to-all | bytes 65536 | tf_op jit(solution)/shard_map/all_to_all | solution.py:357
  156.3 5.2 %all-to-all-start.6 = ((f32[32,64,128]{2,1,0:T(8,128)}), f32[32,64,128]{2,1,0:T(8,128)S(1)}, u32[]{:S(2)}, u32[]{:S(2)}) async-start(f32[32,64,128]{2,1,0:T(8,128)} %shard_map.76), calls=%async_computation.6 | async-start | bytes 2097152 | tf_op jit(solution)/shard_map/all_to_all | solution.py:357
  162.8 8.3 %collective-permute-done.8.rest_other = f32[4,64,256]{2,1,0:T(8,128)S(1)} collective-permute-done((f32[4,64,256]{2,1,0:T(8,128)}, f32[4,64,256]{2,1,0:T(8,128)S(1)}, u32[]{:S(2)}, u32[]{:S(2)}) %collective-permute-start.8) | collective-permute-done | bytes 262176 | tf_op jit(solution)/shard_map/ppermute | solution.py:353
  171.1 7.5 %all-to-all-done.6.ends = f32[32,64,128]{2,1,0:T(8,128)S(1)} async-done(((f32[32,64,128]{2,1,0:T(8,128)}), f32[32,64,128]{2,1,0:T(8,128)S(1)}, u32[]{:S(2)}, u32[]{:S(2)}) %all-to-all-start.6) | async-done | bytes 1048608 | tf_op jit(solution)/shard_map/all_to_all | solution.py:357
  178.6 9.7 %shard_map.77 = f32[4,64,256]{2,1,0:T(8,128)} custom-call(s32[2]{0:T(128)S(1)} %pad_add_fusion.where, f32[8,128]{1,0:T(8,128)S(1)} %bitcast.18, f32[5,16,16,128]{3,2,1,0:T(8,128)S(1)} %get-tuple-element.25.static, f32[8,16,16,128]{3,2,1,0:T(8,128)S(1)} %copy-done.5, f32[16,16,128]{2,1,0:T(8,128)S(1)} %copy-done.18, ...), custom_call_target="tpu_custom_call" | custom-call | flops 67108864 | bytes 1048576 | tf_op jit(solution)/shard_map/pallas_call | solution.py:112
  (65 shorter events, 22.7 us)
Async XLA Ops:
  1.4 8.5 %collective-permute-start = (f32[1,128]{1,0:T(1,128)S(1)}, f32[1,128]{1,0:T(1,128)S(1)}, u32[]{:S(2)}, u32[]{:S(2)}) collective-permute-start(f32[1,128]{1,0:T(1,128)S(1)} %pad.4), channel_id=1, source_target_pairs={{0,0},{8,8},{16,16},{24,24},{32,1},{40,9},{48,17},{56,25},{64,2},{... | collective-permute-start | bytes 1544 | tf_op jit(solution)/shard_map/ppermute | solution.py:385
  10.9 1.1 copy-start.12
  14.3 41.1 %copy-start.7 = (f32[4,64,256]{2,1,0:T(8,128)S(1)}, f32[4,64,256]{2,1,0:T(8,128)}, u32[]{:S(2)}) copy-start(f32[4,64,256]{2,1,0:T(8,128)} %rest.1) | copy-start | bytes 786436
  18.0 2.3 %copy-start.13 = (f32[32,48,128]{2,1,0:T(8,128)}, f32[32,48,128]{2,1,0:T(8,128)S(1)}, u32[]{:S(2)}) copy-start(f32[32,48,128]{2,1,0:T(8,128)S(1)} %get-tuple-element.24) | copy-start | bytes 2359300
  18.0 42.8 %copy-start.10 = (f32[4,64,256]{2,1,0:T(8,128)}, f32[4,64,256]{2,1,0:T(8,128)S(1)}, u32[]{:S(2)}) copy-start(f32[4,64,256]{2,1,0:T(8,128)S(1)} %get-tuple-element.32.sigma) | copy-start | bytes 786436
  18.0 37.4 %collective-permute-start.2 = (f32[13,64,256]{2,1,0:T(8,128)}, f32[13,64,256]{2,1,0:T(8,128)S(1)}, u32[]{:S(2)}, u32[]{:S(2)}) collective-permute-start(f32[13,64,256]{2,1,0:T(8,128)} %get-tuple-element.30), channel_id=1, source_target_pairs={{1,0},{2,1},{3,2},{4,3},{5,4},{6,5},{7,6},{8,7},{9,8},{10,9},{11,1... | collective-permute-start | bytes 2555912 | tf_op jit(solution)/shard_map/ppermute | solution.py:353
  20.3 23.9 %all-to-all-start = ((f32[32,48,128]{2,1,0:T(8,128)}), f32[32,48,128]{2,1,0:T(8,128)S(1)}, u32[]{:S(2)}, u32[]{:S(2)}) async-start(f32[32,48,128]{2,1,0:T(8,128)} %copy-done.13), calls=%async_computation | async-start | bytes 1572864 | tf_op jit(solution)/shard_map/all_to_all | solution.py:357
  29.8 25.6 %collective-permute-start.1 = (f32[10,64,256]{2,1,0:T(8,128)}, f32[10,64,256]{2,1,0:T(8,128)S(1)}, u32[]{:S(2)}, u32[]{:S(2)}) collective-permute-start(f32[10,64,256]{2,1,0:T(8,128)} %get-tuple-element.29), channel_id=1, source_target_pairs={{0,1},{1,2},{2,3},{3,4},{4,5},{5,6},{6,7},{7,8},{8,9},{9,10},{10,1... | collective-permute-start | bytes 1966088 | tf_op jit(solution)/shard_map/ppermute | solution.py:353
  33.3 22.1 %collective-permute-start.3 = (f32[1,64,256]{2,1,0:T(8,128)}, f32[1,64,256]{2,1,0:T(8,128)S(1)}, u32[]{:S(2)}, u32[]{:S(2)}) collective-permute-start(f32[1,64,256]{2,1,0:T(8,128)} %get-tuple-element.31), channel_id=1, source_target_pairs={{2,0},{3,1},{4,2},{5,3},{6,4},{7,5},{8,6},{9,7},{10,8},{11,9},{12,... | collective-permute-start | bytes 196616 | tf_op jit(solution)/shard_map/ppermute | solution.py:353
  55.4 1.0 copy-start.2
  75.3 17.1 %copy-start.21 = (f32[4,64,256]{2,1,0:T(8,128)}, f32[4,64,256]{2,1,0:T(8,128)S(1)}, u32[]{:S(2)}) copy-start(f32[4,64,256]{2,1,0:T(8,128)S(1)} %get-tuple-element.39) | copy-start | bytes 786436
  86.8 22.7 %all-to-all-start.3 = ((f32[32,64,128]{2,1,0:T(8,128)}), f32[32,64,128]{2,1,0:T(8,128)S(1)}, u32[]{:S(2)}, u32[]{:S(2)}) async-start(f32[32,64,128]{2,1,0:T(8,128)} %copy-done), calls=%async_computation.3 | async-start | bytes 2097152 | tf_op jit(solution)/shard_map/all_to_all | solution.py:357
  92.4 8.3 %collective-permute-start.4 = (f32[4,64,256]{2,1,0:T(8,128)}, f32[4,64,256]{2,1,0:T(8,128)S(1)}, u32[]{:S(2)}, u32[]{:S(2)}) collective-permute-start(f32[4,64,256]{2,1,0:T(8,128)} %copy-done.21), channel_id=1, source_target_pairs={{0,32},{32,64},{64,96},{96,128},{128,160},{160,192},{192,224},{224... | collective-permute-start | bytes 786440 | tf_op jit(solution)/shard_map/ppermute | solution.py:353
  100.6 22.4 %collective-permute-start.5 = (f32[4,64,256]{2,1,0:T(8,128)S(1)}, f32[4,64,256]{2,1,0:T(8,128)}, u32[]{:S(2)}, u32[]{:S(2)}) collective-permute-start(f32[4,64,256]{2,1,0:T(8,128)S(1)} %collective-permute-done.4.rest.rest_first), channel_id=1, source_target_pairs={{0,1},{1,2},{2,3},{3,4},{4,5},{5,6},{6,7},{7,8},{8,9},{9,10},{10,1... | collective-permute-start | bytes 786440 | tf_op jit(solution)/shard_map/ppermute | solution.py:353
  105.0 18.0 %collective-permute-start.6 = (f32[4,64,256]{2,1,0:T(8,128)S(1)}, f32[4,64,256]{2,1,0:T(8,128)}, u32[]{:S(2)}, u32[]{:S(2)}) collective-permute-start(f32[4,64,256]{2,1,0:T(8,128)S(1)} %collective-permute-done.4.rest.rest_first), channel_id=1, source_target_pairs={{1,0},{2,1},{3,2},{4,3},{5,4},{6,5},{7,6},{8,7},{9,8},{10,9},{11,1... | collective-permute-start | bytes 786440 | tf_op jit(solution)/shard_map/ppermute | solution.py:353
  107.6 15.4 %collective-permute-start.7 = (f32[1,64,256]{2,1,0:T(8,128)}, f32[1,64,256]{2,1,0:T(8,128)S(1)}, u32[]{:S(2)}, u32[]{:S(2)}) collective-permute-start(f32[1,64,256]{2,1,0:T(8,128)} %slice.9), channel_id=1, source_target_pairs={{2,0},{3,1},{4,2},{5,3},{6,4},{7,5},{8,6},{9,7},{10,8},{11,9},{12,... | collective-permute-start | bytes 196616 | tf_op jit(solution)/shard_map/ppermute | solution.py:353
  109.5 13.5 %copy-start.3 = (f32[2,4,64,256]{3,2,1,0:T(8,128)S(1)}, f32[2,4,64,256]{3,2,1,0:T(8,128)}, u32[]{:S(2)}) copy-start(f32[2,4,64,256]{3,2,1,0:T(8,128)} %copy-done.1) | copy-start | bytes 1572868
  109.5 1.3 copy-start.9
  111.7 11.3 %copy-start.11 = (f32[4,64,256]{2,1,0:T(8,128)S(1)}, f32[4,64,256]{2,1,0:T(8,128)}, u32[]{:S(2)}) copy-start(f32[4,64,256]{2,1,0:T(8,128)} %copy-done.10) | copy-start | bytes 786436
  143.6 35.0 %copy-start.5 = (f32[8,16,16,128]{3,2,1,0:T(8,128)S(1)}, f32[8,16,16,128]{3,2,1,0:T(8,128)}, u32[]{:S(2)}) copy-start(f32[8,16,16,128]{3,2,1,0:T(8,128)} %copy-done.4) | copy-start | bytes 3145732
  143.6 35.0 %copy-start.18 = (f32[16,16,128]{2,1,0:T(8,128)S(1)}, f32[16,16,128]{2,1,0:T(8,128)}, u32[]{:S(2)}) copy-start(f32[16,16,128]{2,1,0:T(8,128)} %copy-done.17) | copy-start | bytes 393220
  145.0 16.5 %copy-start.22 = (f32[4,64,256]{2,1,0:T(8,128)}, f32[4,64,256]{2,1,0:T(8,128)S(1)}, u32[]{:S(2)}) copy-start(f32[4,64,256]{2,1,0:T(8,128)S(1)} %get-tuple-element.43) | copy-start | bytes 786436
  156.3 22.4 %all-to-all-start.6 = ((f32[32,64,128]{2,1,0:T(8,128)}), f32[32,64,128]{2,1,0:T(8,128)S(1)}, u32[]{:S(2)}, u32[]{:S(2)}) async-start(f32[32,64,128]{2,1,0:T(8,128)} %shard_map.76), calls=%async_computation.6 | async-start | bytes 2097152 | tf_op jit(solution)/shard_map/all_to_all | solution.py:357
  161.5 9.6 %collective-permute-start.8 = (f32[4,64,256]{2,1,0:T(8,128)}, f32[4,64,256]{2,1,0:T(8,128)S(1)}, u32[]{:S(2)}, u32[]{:S(2)}) collective-permute-start(f32[4,64,256]{2,1,0:T(8,128)} %copy-done.22), channel_id=1, source_target_pairs={{0,32},{32,64},{64,96},{96,128},{128,160},{160,192},{192,224},{1,3... | collective-permute-start | bytes 786440 | tf_op jit(solution)/shard_map/ppermute | solution.py:353
  (11 other events, 9.2 us)

commit v3 on v2

--- a/solution.py
+++ b/solution.py
@@ -14,7 +14,7 @@
 VMEM = pltpu.MemorySpace.VMEM
 SMEM = pltpu.MemorySpace.SMEM
 INTERPRET = False
-LIMIT = 20 << 20
+LIMIT = 12 << 20
 
 
 def iota(shape, dim):
@@ -107,21 +107,35 @@
     return out
 
 
-def call(body, outs, args, small=(), scratch=(), flops=0):
-    specs = [pl.BlockSpec(memory_space=SMEM if k in small else VMEM) for k in range(len(args))]
+def call(body, outs, args, small=(), far=(), scratch=(), flops=0, copies=0, limit=LIMIT):
+    spaces = [SMEM if k in small else pltpu.MemorySpace.HBM if k in far else VMEM for k in range(len(args))]
+    specs = [pl.BlockSpec(memory_space=space) for space in spaces]
     return pl.pallas_call(
         body,
         out_shape=tuple(jax.ShapeDtypeStruct(s, F32) for s in outs),
         in_specs=specs,
         out_specs=tuple(pl.BlockSpec(memory_space=VMEM) for _ in outs),
-        scratch_shapes=tuple(pltpu.VMEM(s, F32) for s in scratch),
+        scratch_shapes=(
+            *(pltpu.VMEM(s, F32) if isinstance(s, tuple) else s for s in scratch),
+            *(pltpu.SemaphoreType.DMA for _ in range(copies)),
+        ),
         cost_estimate=pl.CostEstimate(flops=flops, bytes_accessed=1 << 20, transcendentals=0) if flops else None,
-        compiler_params=pltpu.CompilerParams(vmem_limit_bytes=LIMIT),
+        compiler_params=pltpu.CompilerParams(vmem_limit_bytes=limit),
         interpret=INTERPRET,
     )(*args)
 
 
-def setup_kernel(cond, cur, theirs, labels, coils, initial, sigma, sources, up, down, far, packed):
+def setup_kernel(cond, cur, theirs, labels_far, coils_far, initial_far, sigma, sources, up, down, far, packed,
+                 labels, coils, initial, labels_sem, coils_sem, initial_sem):
+    copies = [
+        pltpu.make_async_copy(labels_far, labels, labels_sem),
+        pltpu.make_async_copy(coils_far, coils, coils_sem),
+        pltpu.make_async_copy(initial_far, initial, initial_sem),
+    ]
+    for copy in copies:
+        copy.start()
+    for copy in copies:
+        copy.wait()
     region = labels[...]
     cell = jnp.where(region == 0, cond[0], 0.0)
     for k in range(1, 4):
@@ -144,7 +158,11 @@
     far[...] = initial[0:1]
     fields = [initial[...], cell, *pattern]
     rows = [restrict_packed(jnp.sum(f, axis=0)) for f in fields]
-    rows = jnp.concatenate([*rows, jnp.broadcast_to(theirs[...], (8, 128))], axis=0)
+    lane = iota((8, 128), 1)
+    row = jnp.zeros((8, 128), F32)
+    for k in range(6):
+        row = jnp.where(lane == k, theirs[k // 3, k % 3], row)
+    rows = jnp.concatenate([*rows, row], axis=0)
     packed[...] = jnp.broadcast_to(rows[None], packed.shape)
 
 
@@ -152,52 +170,57 @@
     return unpack(whole[0:16, at : at + 8, :], whole[16:32, at : at + 8, :])
 
 
-def sweep(where, cur, state, static, advanced, planes, correction, count):
+def slice_source(cur, static, n):
+    source = jnp.zeros((16, 16, 128), F32)
+    for p in range(PHASES):
+        source = source + 0.5 * (cur[n, p] + cur[n, PHASES + p]) * static[2 + p]
+    return source
+
+
+def sweep(where, cur, state, static, advanced, planes, correction):
     mine, place = where[0], where[1]
-    diagonal = static[1] * 0.5 + 0.375
 
     def turn(n, carry):
-        if planes is not None:
-
-            @pl.when(n == mine)
-            def _():
-                for k, plane in enumerate(cut_planes(state, place, (-1, 0, 1, 2))):
-                    planes[16 * k : 16 * k + 16] = plane
-
-        source = jnp.zeros((16, 16, 128), F32)
-        for p in range(PHASES):
-            mean = 0.5 * (cur[n, p] + cur[n, PHASES + p])
-            source = source + mean * static[2 + p]
-        solved = coarse_solve(state[...], source, static[1] * 0.5 + 0.375)
-        if advanced is not None:
-            advanced[n] = solved
-        state[...] = solved if correction is None else solved + correction[n]
+        @pl.when(n == mine)
+        def _():
+            for k, plane in enumerate(cut_planes(state, place, (-1, 0, 1, 2))):
+                planes[16 * k : 16 * k + 16] = plane
+
+        state[...] = coarse_solve(state[...], slice_source(cur, static, n), static[1] * 0.5 + 0.375)
+
+        @pl.when(n == mine)
+        def _():
+            (plane,) = cut_planes(state, place, (0,))
+            advanced[...] = plane[:8] + pltpu.roll(plane[8:], 64, 1)
+
+        if correction is not None:
+            state[...] = state[...] + correction[n]
         return carry
 
-    lax.fori_loop(0, count, turn, 0)
+    lax.fori_loop(0, 8, turn, 0)
 
 
 def first_sweep_kernel(where, cur, whole, static, planes, advanced, state):
     for k in range(5):
         static[k] = unpack_all(whole, 8 * k)
     state[...] = static[0]
-    sweep(where, cur, state, static, advanced, planes, None, 8)
-
-
-def load_corrections(ends, before, correction):
+    sweep(where, cur, state, static, advanced, planes, None)
+
+
+def load_corrections(ends, correction):
     for n in range(8):
-        correction[n] = unpack_all(ends, 8 * n) - before[n]
-
-
-def next_sweep_kernel(where, cur, static, before, begin, ends, planes, advanced, state, correction):
-    load_corrections(ends, before, correction)
+        correction[n] = unpack_all(ends, 8 * n)
+
+
+def next_sweep_kernel(where, cur, static, begin, ends, planes, advanced, state, correction):
+    load_corrections(ends, correction)
     state[...] = begin[...]
-    sweep(where, cur, state, static, advanced, planes, correction, 8)
-
-
-def last_sweep_kernel(where, cur, static, before, begin, rest_first, rest_other, ends,
+    sweep(where, cur, state, static, advanced, planes, correction)
+
+
+def last_sweep_kernel(where, cur, static, begin, rest_first, rest_other, ends,
                       start, state, correction, planes):
-    load_corrections(ends, before, correction)
+    load_corrections(ends, correction)
     state[...] = begin[...]
 
     def keep():
@@ -207,11 +230,8 @@
     mine = where[0]
 
     def turn(n, carry):
-        source = jnp.zeros((16, 16, 128), F32)
-        for p in range(PHASES):
-            mean = 0.5 * (cur[n, p] + cur[n, PHASES + p])
-            source = source + mean * static[2 + p]
-        state[...] = coarse_solve(state[...], source, static[1] * 0.5 + 0.375) + correction[n]
+        solved = coarse_solve(state[...], slice_source(cur, static, n), static[1] * 0.5 + 0.375)
+        state[...] = solved + correction[n]
         return carry
 
     lax.fori_loop(0, mine, turn, 0)
@@ -259,22 +279,24 @@
         before, after = ((5, 3), (6, 7))[step]
         return up[before + plane] if plane < 0 else sources[step, plane] if plane < 4 else down[after + plane - 4]
 
+    def beside(field, low, plane):
+        j = plane - low
+        return field[j - 1] + field[j + 1] + fine_beside(field[j])
+
     def spread(field, low, plane):
-        j = plane - low
-        v = field[j]
-        return field[j - 1] + field[j + 1] + fine_beside(v) - 6.0 * v
+        return beside(field, low, plane) - 6.0 * field[plane - low]
 
     for plane in range(-3, 8):
         r[plane + 3] = guarded(source(0, plane) + spread(u, -4, plane), plane, first)
     for plane in range(-2, 7):
-        w[plane + 2] = guarded(weight(plane) * r[plane + 3] - spread(r, -3, plane), plane, first)
+        w[plane + 2] = guarded(weight(plane) * r[plane + 3] - beside(r, -3, plane), plane, first)
     for plane in range(-1, 6):
         q[0, plane + 1] = guarded(source(1, plane) + spread(u, -4, plane), plane, first)
         q[1, plane + 1] = guarded(spread(r, -3, plane), plane, first)
         q[2, plane + 1] = guarded(spread(w, -2, plane), plane, first)
     for plane in range(5):
         for k in range(3):
-            image = weight(plane) * q[k, plane + 1] - spread(q.at[k], -1, plane)
+            image = weight(plane) * q[k, plane + 1] - beside(q.at[k], -1, plane)
             a[k, plane] = guarded(image, plane, first)
     sums = [jnp.zeros((8, 128), F32)] * 28
     for plane in range(4):
@@ -311,16 +333,18 @@
 PAIRS = ((0, 0), (0, 1), (0, 2), (1, 1), (1, 2), (2, 2))
 
 
-def weights(m0, m1, m2, m3):
-    step = m0 / m1
-    new = step * step * m2 - m0
-    product = m1 - 2.0 * step * m2 + step * step * m3
-    ratio = new / m0
-    second = new / (product - ratio * new / step)
-    return step + second * (1.0 + ratio), -step * second
-
-
-def finish_kernel(sums, fields, fine, rest, ends):
+def weights(norm, cross, square, product):
+    first = cross + 6.0 * norm
+    step = norm / first
+    keep = 1.0 - 6.0 * step
+    new = keep * keep * norm - 2.0 * keep * step * cross + step * step * square
+    second = keep * keep * first - 2.0 * keep * step * (square + 6.0 * cross) + step * step * product
+    ratio = new / norm
+    second = new / (second - ratio * new / step)
+    return step + second * (keep + ratio), -second * step
+
+
+def finish_kernel(sums, fields, advanced, fine, rest, ends):
     row = jnp.sum(sums[...], axis=0, keepdims=True)
     lane = iota((1, 128), 1)
     m = [jnp.sum(jnp.where(lane == k, row, 0.0), axis=1, keepdims=True) for k in range(28)]
@@ -335,7 +359,7 @@
             value = value + scales[k] * fields[k, i]
         fine[i] = value
     own = restrict_packed(jnp.sum(fine[...], axis=0))
-    ends[...] = jnp.broadcast_to(own[None], ends.shape)
+    ends[...] = jnp.broadcast_to((own - advanced[...])[None], ends.shape)
     left = iota((8, 128), 1) < 64
     plane = jnp.concatenate([jnp.where(left, own, 0.0), jnp.where(left, pltpu.roll(own, 64, 1), 0.0)], axis=0)
     (lifted,) = widen(plane)
@@ -343,7 +367,7 @@
         rest[i] = fine[i] - lifted
 
 
-def spread_kernel(ends, packed):
+def spread_kernel(ends, rest, packed):
     packed[...] = jnp.broadcast_to(ends[...].reshape(1, 64, 128), packed.shape)
 
 
@@ -357,8 +381,8 @@
     return lax.all_to_all(x, axis, split_axis=0, concat_axis=0, tiled=True)
 
 
-def everywhere(ends):
-    (packed,) = call(spread_kernel, ((32, 64, 128),), (exchange(ends, "tm"),))
+def everywhere(ends, rest):
+    (packed,) = call(spread_kernel, ((32, 64, 128),), (exchange(ends, "tm"), rest), far=(1,))
     return exchange(packed, "space")
 
 
@@ -382,13 +406,17 @@
         for b in range(slices)
         for a in range(across // slices)
     ]
-    theirs = lax.ppermute(jnp.pad(currents.reshape(1, 6), ((0, 0), (0, 122))), ("tm", "space"), pairs)
+    theirs = lax.ppermute(currents[0], ("tm", "space"), pairs)
 
     sigma, sources, up, down, far, packed = call(
         setup_kernel,
         (block, (2, *block), (10, 64, 256), (13, 64, 256), (1, 64, 256), (32, 48, 128)),
         (conductivity, currents[0], theirs, labels, coil_pattern, initial_state),
-        small=(0, 1),
+        small=(0, 1, 2),
+        far=(3, 4, 5),
+        scratch=(pltpu.VMEM(block, jnp.int32), (3, *block), block),
+        copies=3,
+        limit=60 << 20,
     )
     whole = exchange(packed, "space")
     table = whole[:8, 40, :]
@@ -396,13 +424,13 @@
     far = shifted(far, "space", -2, False)
     static, planes, advanced, state = call(
         first_sweep_kernel,
-        ((5, *field), (64, 128), (8, *field), field),
+        ((5, *field), (64, 128), (8, 128), field),
         (where, table, whole),
         small=(0, 1),
         flops=1 << 26,
     )
 
-    def fine(initial, planes, rest, around_rest):
+    def fine(initial, planes, advanced, rest, around_rest):
         fields, sums = call(
             functools.partial(fine_kernel, initial),
             ((9, *block), (32, 128)),
@@ -413,25 +441,25 @@
         return call(
             finish_kernel,
             (block, block, (8, 8, 128)),
-            (exchange(sums, "space"), fields),
+            (exchange(sums, "space"), fields, advanced),
         )
 
-    _, rest, ends = fine(True, planes, initial_state, (up, down, far))
+    _, rest, ends = fine(True, planes, advanced, initial_state, (up, down, far))
     rest_first = shifted(rest, "tm", 1, True)
     planes, advanced_next, state_next = call(
         next_sweep_kernel,
-        ((64, 128), (8, *field), field),
-        (where, table, static, advanced, state, everywhere(ends)),
+        ((64, 128), (8, 128), field),
+        (where, table, static, state, everywhere(ends, rest_first)),
         small=(0, 1),
         scratch=((8, *field),),
         flops=1 << 26,
     )
-    fine_state, rest, ends = fine(False, planes, rest_first, halos(rest_first))
+    fine_state, rest, ends = fine(False, planes, advanced_next, rest_first, halos(rest_first))
     rest_other = shifted(rest, "tm", 1, False)
     (start,) = call(
         last_sweep_kernel,
         (block,),
-        (where, table, static, advanced_next, state_next, rest_first, rest_other, everywhere(ends)),
+        (where, table, static, state_next, rest_first, rest_other, everywhere(ends, rest_other)),
         small=(0, 1),
         scratch=(field, (8, *field), (16, 128)),
         flops=1 << 26,

time: 189 us -> 183 us (0.968)
  blocking collectives: 49.3 us -> 68.4 us
  waiting for transfers between devices: 37.5 us -> 25.2 us
  starting transfers between devices: 41.5 us -> 33.4 us
  local copies, waits for them, and re-layouts: 14.1 us -> 7.61 us
    all_to_all x4 -> x5, blocking collectives: 49.3 us -> 68.4 us  [exchange(): return lax.all_to_all(x, axis, split_axis=0, concat_axis=0, tiled=True)]
    ppermute x8, waiting for transfers between devices: 14 us -> 0.02 us  [shifted(): return lax.ppermute(x, axis, pairs)]
    unnamed x46 -> x18, local copies, waits for them, and re-layouts: 12.7 us -> 6.98 us
    all_to_all x3 -> x2, starting transfers between devices: 20.2 us -> 15.3 us  [exchange(): return lax.all_to_all(x, axis, split_axis=0, concat_axis=0, tiled=True)]
    ppermute x8, starting transfers between devices: 18.8 us -> 15.5 us  [shifted(): return lax.ppermute(x, axis, pairs)]
    all_to_all x3 -> x2, waiting for transfers between devices: 17.5 us -> 19 us  [exchange(): return lax.all_to_all(x, axis, split_axis=0, concat_axis=0, tiled=True)]
  transfers between devices with their start and end apart: 12 -> 11, of which waited for: 6 -> 3; matrix products, arithmetic and copies ran while one was open for 0% -> 0% of each run, Pallas kernels for 10% -> 11%
where the time goes in v3:
time: 183 us; the launch traced here: 182 us
  blocking collectives  68.4 us (37%)
  Pallas kernels  46.7 us (26%)
  starting transfers between devices  33.4 us (18%)
  waiting for transfers between devices  25.2 us (14%)
  local copies, waits for them, and re-layouts  7.61 us (4%)
    all_to_all x5, blocking collectives, exchange(): return lax.all_to_all(x, axis, split_axis=0, concat_axis=0, tiled=True)  68.4 us
    pallas_call x10, Pallas kernels, call(): pl.pallas_call(body, out_shape=tuple((jax.ShapeDtypeStruct(s, F32) for s...  46.7 us
    all_to_all x2, waiting for transfers between devices, exchange(): return lax.all_to_all(x, axis, split_axis=0, concat_axis=0, tiled=True)  19 us
    ppermute x8, starting transfers between devices, shifted(): return lax.ppermute(x, axis, pairs)  15.5 us
    all_to_all x2, starting transfers between devices, exchange(): return lax.all_to_all(x, axis, split_axis=0, concat_axis=0, tiled=True)  15.3 us
    unnamed x18, local copies, waits for them, and re-layouts  6.98 us
    ppermute x1, waiting for transfers between devices, body(): theirs = lax.ppermute(currents[0], ('tm', 'space'), pairs)  6.18 us
  transfers between devices with their start and end apart: 11, of which 3 were waited for; matrix products, arithmetic and copies ran while one was open for 0% of the time, Pallas kernels for 11%

profile of v3, /device:TPU:225, one launch (start us, length us, event | category | flops | bytes accessed | tf_op | source)
XLA Modules:
  0.0 182.2 jit_solution(16777153910109962945)
XLA Ops:
  0.6 2.6 %collective-permute-start = (f32[2,3]{1,0:T(2,128)}, f32[2,3]{1,0:T(2,128)S(1)}, u32[]{:S(2)}, u32[]{:S(2)}) collective-permute-start(f32[2,3]{1,0:T(2,128)} %bitcast.24), channel_id=1, source_target_pairs={{0,0},{8,8},{16,16},{24,24},{32,1},{40,9},{48,17},{56,25},{64,2},{... | collective-permute-start | bytes 80 | tf_op jit(solution)/shard_map/ppermute | solution.py:409
  3.2 6.2 %collective-permute-done.theirs = f32[2,3]{1,0:T(2,128)S(1)} collective-permute-done((f32[2,3]{1,0:T(2,128)}, f32[2,3]{1,0:T(2,128)S(1)}, u32[]{:S(2)}, u32[]{:S(2)}) %collective-permute-start) | collective-permute-done | bytes 56 | tf_op jit(solution)/shard_map/ppermute | solution.py:409
  9.9 4.7 %shard_map.68 = (f32[4,64,256]{2,1,0:T(8,128)}, f32[2,4,64,256]{3,2,1,0:T(8,128)}, f32[10,64,256]{2,1,0:T(8,128)}, f32[13,64,256]{2,1,0:T(8,128)}, f32[1,64,256]{2,1,0:T(8,128)}, /*index=5*/f32[32,48,128]{2,1,0:T(8,128)}) custom-call(f32[4]{0:T(128)} %cond.1, f32[2,3]{1,0:T(2,128)} %bitcast.25, f32[2,3]{1,0:T(2,128)} %copy-done.8, s32[4,64,256]{2,1,0:T(8,128)} %labels_far.1, ...), custom_call_target="tpu_custom_call" | custom-call | tf_op jit(solution)/shard_map/pallas_call | solution.py:113
  14.6 2.4 %collective-permute-start.2 = (f32[13,64,256]{2,1,0:T(8,128)}, f32[13,64,256]{2,1,0:T(8,128)S(1)}, u32[]{:S(2)}, u32[]{:S(2)}) collective-permute-start(f32[13,64,256]{2,1,0:T(8,128)} %get-tuple-element.29), channel_id=1, source_target_pairs={{1,0},{2,1},{3,2},{4,3},{5,4},{6,5},{7,6},{8,7},{9,8},{10,9},{11,1... | collective-permute-start | bytes 2555912 | tf_op jit(solution)/shard_map/ppermute | solution.py:377
  17.0 9.5 %all-to-all-start = ((f32[32,48,128]{2,1,0:T(8,128)}), f32[32,48,128]{2,1,0:T(8,128)S(1)}, u32[]{:S(2)}, u32[]{:S(2)}) async-start(f32[32,48,128]{2,1,0:T(8,128)} %get-tuple-element.24), calls=%async_computation | async-start | bytes 1572864 | tf_op jit(solution)/shard_map/all_to_all | solution.py:381
  26.5 3.5 %collective-permute-start.1 = (f32[10,64,256]{2,1,0:T(8,128)}, f32[10,64,256]{2,1,0:T(8,128)S(1)}, u32[]{:S(2)}, u32[]{:S(2)}) collective-permute-start(f32[10,64,256]{2,1,0:T(8,128)} %get-tuple-element.28), channel_id=1, source_target_pairs={{0,1},{1,2},{2,3},{3,4},{4,5},{5,6},{6,7},{7,8},{8,9},{9,10},{10,1... | collective-permute-start | bytes 1966088 | tf_op jit(solution)/shard_map/ppermute | solution.py:377
  31.4 9.5 %all-to-all-done.whole = f32[32,48,128]{2,1,0:T(8,128)S(1)} async-done(((f32[32,48,128]{2,1,0:T(8,128)}), f32[32,48,128]{2,1,0:T(8,128)S(1)}, u32[]{:S(2)}, u32[]{:S(2)}) %all-to-all-start) | async-done | bytes 786464 | tf_op jit(solution)/shard_map/all_to_all | solution.py:381
  41.0 9.6 %shard_map.69 = (f32[5,16,16,128]{3,2,1,0:T(8,128)S(1)}, f32[64,128]{1,0:T(8,128)S(1)}, f32[8,128]{1,0:T(8,128)S(1)}, f32[16,16,128]{2,1,0:T(8,128)S(1)}) custom-call(s32[2]{0:T(128)S(1)} %pad_add_fusion.where, f32[8,128]{1,0:T(8,128)S(1)} %bitcast.16, f32[32,48,128]{2,1,0:T(8,128)S(1)} %all-to-all-done.whole), custom_call_target="tpu_custom_call" | custom-call | flops 67108864 | bytes 1048576 | tf_op jit(solution)/shard_map/pallas_call | solution.py:113
  53.2 4.7 %shard_map.70 = (f32[9,4,64,256]{3,2,1,0:T(8,128)S(1)}, f32[32,128]{1,0:T(8,128)S(1)}) custom-call(s32[2]{0:T(128)S(1)} %pad_add_fusion.where, f32[64,128]{1,0:T(8,128)S(1)} %get-tuple-element.27.planes, f32[4,64,256]{2,1,0:T(8,128)S(1)} %copy-done.3, f32[10,64,256]{2,1,0:T(8,128)S(1)} %collective-permute-done.1.rest_up.up, ...), custom_call_target="tpu_custom_call" | custom-call | tf_op jit(solution)/shard_map/pallas_call | solution.py:113
  57.8 13.0 %all_to_all.47 = f32[32,1,128]{2,1,0:T(1,128)S(1)} all-to-all(f32[32,1,128]{2,1,0:T(1,128)S(1)} %bitcast.22), channel_id=1, replica_groups=mesh['tm'=8,'space'=32] {'space'}, dimensions={0} | all-to-all | bytes 32768 | tf_op jit(solution)/shard_map/all_to_all | solution.py:381
  70.9 1.4 shard_map.71
  72.3 11.2 %all_to_all.48.ends = f32[8,8,128]{2,1,0:T(8,128)S(1)} all-to-all(f32[8,8,128]{2,1,0:T(8,128)S(1)} %get-tuple-element.36), channel_id=1, replica_groups=mesh['tm'=8,'space'=32] {'tm'}, dimensions={0} | all-to-all | bytes 65536 | tf_op jit(solution)/shard_map/all_to_all | solution.py:381
  84.7 5.9 %all-to-all-start.3 = ((f32[32,64,128]{2,1,0:T(8,128)}), f32[32,64,128]{2,1,0:T(8,128)S(1)}, u32[]{:S(2)}, u32[]{:S(2)}) async-start(f32[32,64,128]{2,1,0:T(8,128)} %copy-done), calls=%async_computation.3 | async-start | bytes 2097152 | tf_op jit(solution)/shard_map/all_to_all | solution.py:381
  90.5 2.3 %collective-permute-start.6 = (f32[4,64,256]{2,1,0:T(8,128)S(1)}, f32[4,64,256]{2,1,0:T(8,128)}, u32[]{:S(2)}, u32[]{:S(2)}) collective-permute-start(f32[4,64,256]{2,1,0:T(8,128)S(1)} %collective-permute-done.4.rest.rest_first), channel_id=1, source_target_pairs={{1,0},{2,1},{3,2},{4,3},{5,4},{6,5},{7,6},{8,7},{9,8},{10,9},{11,1... | collective-permute-start | bytes 786440 | tf_op jit(solution)/shard_map/ppermute | solution.py:377
  92.8 3.3 %collective-permute-start.5 = (f32[4,64,256]{2,1,0:T(8,128)S(1)}, f32[4,64,256]{2,1,0:T(8,128)}, u32[]{:S(2)}, u32[]{:S(2)}) collective-permute-start(f32[4,64,256]{2,1,0:T(8,128)S(1)} %collective-permute-done.4.rest.rest_first), channel_id=1, source_target_pairs={{0,1},{1,2},{2,3},{3,4},{4,5},{5,6},{6,7},{7,8},{8,9},{9,10},{10,1... | collective-permute-start | bytes 786440 | tf_op jit(solution)/shard_map/ppermute | solution.py:377
  96.7 1.5 collective-permute-start.7
  98.2 9.5 %all-to-all-done.3.ends = f32[32,64,128]{2,1,0:T(8,128)S(1)} async-done(((f32[32,64,128]{2,1,0:T(8,128)}), f32[32,64,128]{2,1,0:T(8,128)S(1)}, u32[]{:S(2)}, u32[]{:S(2)}) %all-to-all-start.3) | async-done | bytes 1048608 | tf_op jit(solution)/shard_map/all_to_all | solution.py:381
  108.6 9.8 %shard_map.73 = (f32[64,128]{1,0:T(8,128)S(1)}, f32[8,128]{1,0:T(8,128)S(1)}, f32[16,16,128]{2,1,0:T(8,128)S(1)}) custom-call(s32[2]{0:T(128)S(1)} %pad_add_fusion.where, f32[8,128]{1,0:T(8,128)S(1)} %bitcast.17, f32[5,16,16,128]{3,2,1,0:T(8,128)S(1)} %get-tuple-element.25.static, f32[16,16,128]{2,1,0:T(8,128)S(1)} %copy-done.7, ...), custom_call_target="tpu_custom_call" | custom-call | flops 67108864 | bytes 1048576 | tf_op jit(solution)/shard_map/pallas_call | solution.py:113
  120.4 5.2 %shard_map.74 = (f32[9,4,64,256]{3,2,1,0:T(8,128)S(1)}, f32[32,128]{1,0:T(8,128)S(1)}) custom-call(s32[2]{0:T(128)S(1)} %pad_add_fusion.where, f32[64,128]{1,0:T(8,128)S(1)} %get-tuple-element.39.planes, f32[4,64,256]{2,1,0:T(8,128)S(1)} %collective-permute-done.4.rest.rest_first, f32[4,64,256]{2,1,0:T(8,128)} %collective-permute-done.5.rest_up, ...), custom_call_target="tpu_custom_call" | custom-call | tf_op jit(solution)/shard_map/pallas_call | solution.py:113
  125.6 11.6 %all_to_all.49 = f32[32,1,128]{2,1,0:T(1,128)S(1)} all-to-all(f32[32,1,128]{2,1,0:T(1,128)S(1)} %bitcast.21), channel_id=1, replica_groups=mesh['tm'=8,'space'=32] {'space'}, dimensions={0} | all-to-all | bytes 32768 | tf_op jit(solution)/shard_map/all_to_all | solution.py:381
  137.2 1.4 shard_map.75
  139.9 10.4 %all_to_all.50.ends = f32[8,8,128]{2,1,0:T(8,128)S(1)} all-to-all(f32[8,8,128]{2,1,0:T(8,128)S(1)} %get-tuple-element.44), channel_id=1, replica_groups=mesh['tm'=8,'space'=32] {'tm'}, dimensions={0} | all-to-all | bytes 65536 | tf_op jit(solution)/shard_map/all_to_all | solution.py:381
  150.5 22.0 %all_to_all.51.ends = f32[32,64,128]{2,1,0:T(8,128)S(1)} all-to-all(f32[32,64,128]{2,1,0:T(8,128)S(1)} %shard_map.76), channel_id=1, replica_groups=mesh['tm'=8,'space'=32] {'space'}, dimensions={0} | all-to-all | bytes 2097152 | tf_op jit(solution)/shard_map/all_to_all | solution.py:381
  172.5 9.7 %shard_map.77 = f32[4,64,256]{2,1,0:T(8,128)} custom-call(s32[2]{0:T(128)S(1)} %pad_add_fusion.where, f32[8,128]{1,0:T(8,128)S(1)} %bitcast.18, f32[5,16,16,128]{3,2,1,0:T(8,128)S(1)} %get-tuple-element.25.static, f32[16,16,128]{2,1,0:T(8,128)S(1)} %get-tuple-element.38.begin, f32[4,64,256]{2,1,0:T(8,128)S(1)} %collective-permute-done.4.rest.rest_first, ...), custom_call_target="tpu_custom_call" | custom-call | flops 67108864 | bytes 1048576 | tf_op jit(solution)/shard_map/pallas_call | solution.py:113
  (34 shorter events, 10.5 us)
Async XLA Ops:
  0.6 8.7 %collective-permute-start = (f32[2,3]{1,0:T(2,128)}, f32[2,3]{1,0:T(2,128)S(1)}, u32[]{:S(2)}, u32[]{:S(2)}) collective-permute-start(f32[2,3]{1,0:T(2,128)} %bitcast.24), channel_id=1, source_target_pairs={{0,0},{8,8},{16,16},{24,24},{32,1},{40,9},{48,17},{56,25},{64,2},{... | collective-permute-start | bytes 80 | tf_op jit(solution)/shard_map/ppermute | solution.py:409
  9.4 0.5 copy-start.8
  14.6 36.7 %copy-start.1 = (f32[2,4,64,256]{3,2,1,0:T(8,128)S(1)}, f32[2,4,64,256]{3,2,1,0:T(8,128)}, u32[]{:S(2)}) copy-start(f32[2,4,64,256]{3,2,1,0:T(8,128)} %get-tuple-element.32.sources) | copy-start | bytes 1572868
  14.6 36.6 %collective-permute-start.2 = (f32[13,64,256]{2,1,0:T(8,128)}, f32[13,64,256]{2,1,0:T(8,128)S(1)}, u32[]{:S(2)}, u32[]{:S(2)}) collective-permute-start(f32[13,64,256]{2,1,0:T(8,128)} %get-tuple-element.29), channel_id=1, source_target_pairs={{1,0},{2,1},{3,2},{4,3},{5,4},{6,5},{7,6},{8,7},{9,8},{10,9},{11,1... | collective-permute-start | bytes 2555912 | tf_op jit(solution)/shard_map/ppermute | solution.py:377
  17.0 24.0 %all-to-all-start = ((f32[32,48,128]{2,1,0:T(8,128)}), f32[32,48,128]{2,1,0:T(8,128)S(1)}, u32[]{:S(2)}, u32[]{:S(2)}) async-start(f32[32,48,128]{2,1,0:T(8,128)} %get-tuple-element.24), calls=%async_computation | async-start | bytes 1572864 | tf_op jit(solution)/shard_map/all_to_all | solution.py:381
  26.5 24.7 %collective-permute-start.1 = (f32[10,64,256]{2,1,0:T(8,128)}, f32[10,64,256]{2,1,0:T(8,128)S(1)}, u32[]{:S(2)}, u32[]{:S(2)}) collective-permute-start(f32[10,64,256]{2,1,0:T(8,128)} %get-tuple-element.28), channel_id=1, source_target_pairs={{0,1},{1,2},{2,3},{3,4},{4,5},{5,6},{6,7},{7,8},{8,9},{9,10},{10,1... | collective-permute-start | bytes 1966088 | tf_op jit(solution)/shard_map/ppermute | solution.py:377
  30.1 21.2 %collective-permute-start.3 = (f32[1,64,256]{2,1,0:T(8,128)}, f32[1,64,256]{2,1,0:T(8,128)S(1)}, u32[]{:S(2)}, u32[]{:S(2)}) collective-permute-start(f32[1,64,256]{2,1,0:T(8,128)} %get-tuple-element.30), channel_id=1, source_target_pairs={{2,0},{3,1},{4,2},{5,3},{6,4},{7,5},{8,6},{9,7},{10,8},{11,9},{12,... | collective-permute-start | bytes 196616 | tf_op jit(solution)/shard_map/ppermute | solution.py:377
  50.6 0.6 copy-start.6
  51.3 1.0 copy-start.3
  52.2 0.9 copy-start.4
  72.3 11.2 %collective-permute-start.4 = (f32[4,64,256]{2,1,0:T(8,128)S(1)}, f32[4,64,256]{2,1,0:T(8,128)S(1)}, u32[]{:S(2)}, u32[]{:S(2)}) collective-permute-start(f32[4,64,256]{2,1,0:T(8,128)S(1)} %get-tuple-element.37), channel_id=1, source_target_pairs={{0,32},{32,64},{64,96},{96,128},{128,160},{160,192},{192,224},{224... | collective-permute-start | bytes 786440 | tf_op jit(solution)/shard_map/ppermute | solution.py:377
  83.6 1.0 copy-start
  84.7 23.0 %all-to-all-start.3 = ((f32[32,64,128]{2,1,0:T(8,128)}), f32[32,64,128]{2,1,0:T(8,128)S(1)}, u32[]{:S(2)}, u32[]{:S(2)}) async-start(f32[32,64,128]{2,1,0:T(8,128)} %copy-done), calls=%async_computation.3 | async-start | bytes 2097152 | tf_op jit(solution)/shard_map/all_to_all | solution.py:381
  90.5 27.9 %collective-permute-start.6 = (f32[4,64,256]{2,1,0:T(8,128)S(1)}, f32[4,64,256]{2,1,0:T(8,128)}, u32[]{:S(2)}, u32[]{:S(2)}) collective-permute-start(f32[4,64,256]{2,1,0:T(8,128)S(1)} %collective-permute-done.4.rest.rest_first), channel_id=1, source_target_pairs={{1,0},{2,1},{3,2},{4,3},{5,4},{6,5},{7,6},{8,7},{9,8},{10,9},{11,1... | collective-permute-start | bytes 786440 | tf_op jit(solution)/shard_map/ppermute | solution.py:377
  92.8 25.7 %collective-permute-start.5 = (f32[4,64,256]{2,1,0:T(8,128)S(1)}, f32[4,64,256]{2,1,0:T(8,128)}, u32[]{:S(2)}, u32[]{:S(2)}) collective-permute-start(f32[4,64,256]{2,1,0:T(8,128)S(1)} %collective-permute-done.4.rest.rest_first), channel_id=1, source_target_pairs={{0,1},{1,2},{2,3},{3,4},{4,5},{5,6},{6,7},{7,8},{8,9},{9,10},{10,1... | collective-permute-start | bytes 786440 | tf_op jit(solution)/shard_map/ppermute | solution.py:377
  96.7 21.7 %collective-permute-start.7 = (f32[1,64,256]{2,1,0:T(8,128)}, f32[1,64,256]{2,1,0:T(8,128)S(1)}, u32[]{:S(2)}, u32[]{:S(2)}) collective-permute-start(f32[1,64,256]{2,1,0:T(8,128)} %slice.9), channel_id=1, source_target_pairs={{2,0},{3,1},{4,2},{5,3},{6,4},{7,5},{8,6},{9,7},{10,8},{11,9},{12,... | collective-permute-start | bytes 196616 | tf_op jit(solution)/shard_map/ppermute | solution.py:377
  107.7 0.9 copy-start.7
  118.5 1.0 copy-start.2
  119.5 0.9 copy-start.5
  138.6 11.7 %collective-permute-start.8 = (f32[4,64,256]{2,1,0:T(8,128)S(1)}, f32[4,64,256]{2,1,0:T(8,128)S(1)}, u32[]{:S(2)}, u32[]{:S(2)}) collective-permute-start(f32[4,64,256]{2,1,0:T(8,128)S(1)} %get-tuple-element.43), channel_id=1, source_target_pairs={{0,32},{32,64},{64,96},{96,128},{128,160},{160,192},{192,224},{1,3... | collective-permute-start | bytes 786440 | tf_op jit(solution)/shard_map/ppermute | solution.py:377

commit v4 on v3

--- a/solution.py
+++ b/solution.py
@@ -125,7 +125,7 @@
     )(*args)
 
 
-def setup_kernel(cond, cur, theirs, labels_far, coils_far, initial_far, sigma, sources, up, down, far, packed,
+def setup_kernel(cond, cur, theirs, labels_far, coils_far, initial_far, own, up, down, far, packed,
                  labels, coils, initial, labels_sem, coils_sem, initial_sem):
     copies = [
         pltpu.make_async_copy(labels_far, labels, labels_sem),
@@ -140,19 +140,20 @@
     cell = jnp.where(region == 0, cond[0], 0.0)
     for k in range(1, 4):
         cell = cell + jnp.where(region == k, cond[k], 0.0)
-    sigma[...] = cell
+    own[0] = cell
+    own[3] = initial[...]
     pattern = [coils[p] for p in range(PHASES)]
     for step in range(2):
         source = cur[step, 0] * pattern[0]
         for p in range(1, PHASES):
             source = source + cur[step, p] * pattern[p]
-        sources[step] = source
-    up[0:2] = sigma[2:4]
-    up[2:5] = sources[0, 1:4]
-    up[5:6] = sources[1, 3:4]
-    down[0:3] = sigma[0:3]
-    down[3:7] = sources[0]
-    down[7:9] = sources[1, 0:2]
+        own[1 + step] = source
+    up[0:2] = own[0, 2:4]
+    up[2:5] = own[1, 1:4]
+    up[5:6] = own[2, 3:4]
+    down[0:3] = own[0, 0:3]
+    down[3:7] = own[1]
+    down[7:9] = own[2, 0:2]
     up[6:10] = initial[...]
     down[9:13] = initial[...]
     far[...] = initial[0:1]
@@ -207,20 +208,22 @@
     sweep(where, cur, state, static, advanced, planes, None)
 
 
-def load_corrections(ends, correction):
-    for n in range(8):
-        correction[n] = unpack_all(ends, 8 * n)
-
-
-def next_sweep_kernel(where, cur, static, begin, ends, planes, advanced, state, correction):
-    load_corrections(ends, correction)
+def load_corrections(where, ours, theirs, correction):
+    odd = where[1] & 1
+    for k in range(4):
+        correction[4 * odd + k] = unpack_all(ours, 8 * k)
+        correction[4 * (1 - odd) + k] = unpack_all(theirs, 8 * k)
+
+
+def next_sweep_kernel(where, cur, static, begin, ours, theirs, planes, advanced, state, correction):
+    load_corrections(where, ours, theirs, correction)
     state[...] = begin[...]
     sweep(where, cur, state, static, advanced, planes, correction)
 
 
-def last_sweep_kernel(where, cur, static, begin, rest_first, rest_other, ends,
+def last_sweep_kernel(where, cur, static, begin, rest_first, rest_other, ours, theirs,
                       start, state, correction, planes):
-    load_corrections(ends, correction)
+    load_corrections(where, ours, theirs, correction)
     state[...] = begin[...]
 
     def keep():
@@ -260,8 +263,13 @@
     return folded[:, :128] + folded[:, 128:]
 
 
-def fine_kernel(initial, where, planes, rest, rest_up, rest_down, rest_far, sigma, sources, up, down,
-                fields, packed, u, r, w, q, a):
+def fine_kernel(initial, where, planes, own, up, down, *refs):
+    if initial:
+        (rest_far,), refs = refs[:1], refs[1:]
+        rest, rest_up, rest_down = own.at[3], up, down
+    else:
+        (rest, rest_up, rest_down, rest_far), refs = refs[:4], refs[4:]
+    fields, packed, u, r, w, q, a = refs
     first = 4 * where[1]
     zero = (where[0] == 0).astype(F32)
     scale = (1.0 - zero, zero) if initial else (1.0, 1.0 - zero)
@@ -273,11 +281,11 @@
         u[j] = scale[0] * lifted[j // 4] + scale[1] * piece[k]
 
     def weight(plane):
-        return up[2 + plane] if plane < 0 else sigma[plane] if plane < 4 else down[plane - 4]
+        return up[2 + plane] if plane < 0 else own[0, plane] if plane < 4 else down[plane - 4]
 
     def source(step, plane):
         before, after = ((5, 3), (6, 7))[step]
-        return up[before + plane] if plane < 0 else sources[step, plane] if plane < 4 else down[after + plane - 4]
+        return up[before + plane] if plane < 0 else own[1 + step, plane] if plane < 4 else down[after + plane - 4]
 
     def beside(field, low, plane):
         j = plane - low
@@ -368,7 +376,10 @@
 
 
 def spread_kernel(ends, rest, packed):
-    packed[...] = jnp.broadcast_to(ends[...].reshape(1, 64, 128), packed.shape)
+    for half in range(2):
+        rows = ends[4 * half : 4 * half + 4].reshape(1, 32, 128)
+        for k in range(half, packed.shape[0], 2):
+            packed[k : k + 1] = rows
 
 
 def shifted(x, axis, by, ring):
@@ -382,8 +393,10 @@
 
 
 def everywhere(ends, rest):
-    (packed,) = call(spread_kernel, ((32, 64, 128),), (exchange(ends, "tm"), rest), far=(1,))
-    return exchange(packed, "space")
+    (packed,) = call(spread_kernel, ((32, 32, 128),), (exchange(ends, "tm"), rest), far=(1,))
+    half = exchange(packed, "space")
+    places = lax.axis_size("space")
+    return half, lax.ppermute(half, "space", [(i, i ^ 1) for i in range(places)])
 
 
 def halos(x):
@@ -408,9 +421,9 @@
     ]
     theirs = lax.ppermute(currents[0], ("tm", "space"), pairs)
 
-    sigma, sources, up, down, far, packed = call(
+    own, up, down, far, packed = call(
         setup_kernel,
-        (block, (2, *block), (10, 64, 256), (13, 64, 256), (1, 64, 256), (32, 48, 128)),
+        ((4, *block), (10, 64, 256), (13, 64, 256), (1, 64, 256), (32, 48, 128)),
         (conductivity, currents[0], theirs, labels, coil_pattern, initial_state),
         small=(0, 1, 2),
         far=(3, 4, 5),
@@ -420,6 +433,7 @@
     )
     whole = exchange(packed, "space")
     table = whole[:8, 40, :]
+    up, down, far, whole = lax.optimization_barrier((up, down, far, whole))
     up, down = shifted(up, "space", 1, False), shifted(down, "space", -1, False)
     far = shifted(far, "space", -2, False)
     static, planes, advanced, state = call(
@@ -430,11 +444,11 @@
         flops=1 << 26,
     )
 
-    def fine(initial, planes, advanced, rest, around_rest):
+    def fine(initial, planes, advanced, rest):
         fields, sums = call(
             functools.partial(fine_kernel, initial),
             ((9, *block), (32, 128)),
-            (where, planes, rest, *around_rest, sigma, sources, up, down),
+            (where, planes, own, up, down, *rest),
             small=(0,),
             scratch=((13, 64, 256), (11, 64, 256), (9, 64, 256), (3, 7, 64, 256), (3, 5, 64, 256)),
         )
@@ -444,22 +458,24 @@
             (exchange(sums, "space"), fields, advanced),
         )
 
-    _, rest, ends = fine(True, planes, advanced, initial_state, (up, down, far))
+    _, rest, ends = fine(True, planes, advanced, (far,))
     rest_first = shifted(rest, "tm", 1, True)
     planes, advanced_next, state_next = call(
         next_sweep_kernel,
         ((64, 128), (8, 128), field),
-        (where, table, static, state, everywhere(ends, rest_first)),
+        (where, table, static, state, *everywhere(ends, rest_first)),
         small=(0, 1),
         scratch=((8, *field),),
         flops=1 << 26,
     )
-    fine_state, rest, ends = fine(False, planes, advanced_next, rest_first, halos(rest_first))
+    fine_state, rest, ends = fine(
+        False, planes, advanced_next, (rest_first, *halos(rest_first))
+    )
     rest_other = shifted(rest, "tm", 1, False)
     (start,) = call(
         last_sweep_kernel,
         (block,),
-        (where, table, static, state_next, rest_first, rest_other, everywhere(ends, rest_other)),
+        (where, table, static, state_next, rest_first, rest_other, *everywhere(ends, rest_other)),
         small=(0, 1),
         scratch=(field, (8, *field), (16, 128)),
         flops=1 << 26,

time: 183 us -> 181 us (0.989)
  blocking collectives: 68.4 us -> 106 us
  waiting for transfers between devices: 25.2 us -> 7.74 us
  starting transfers between devices: 33.4 us -> 18.6 us
  local copies, waits for them, and re-layouts: 7.61 us -> 0.58 us
    all_to_all x5 -> x7, blocking collectives: 68.4 us -> 106 us  [exchange(): return lax.all_to_all(x, axis, split_axis=0, concat_axis=0, tiled=True)]
    all_to_all x2 -> x0, waiting for transfers between devices: 19 us -> none  [exchange(): return lax.all_to_all(x, axis, split_axis=0, concat_axis=0, tiled=True)]
    all_to_all x2 -> x0, starting transfers between devices: 15.3 us -> none  [exchange(): return lax.all_to_all(x, axis, split_axis=0, concat_axis=0, tiled=True)]
    unnamed x18 -> x4, local copies, waits for them, and re-layouts: 6.98 us -> 0.57 us
  transfers between devices with their start and end apart: 11 -> 11, of which waited for: 3 -> 2; matrix products, arithmetic and copies ran while one was open for 0% -> 0% of each run, Pallas kernels for 11% -> 11%
where the time goes in v4:
time: 181 us; the launch traced here: 180 us
  blocking collectives  106 us (59%)
  Pallas kernels  46.4 us (26%)
  starting transfers between devices  18.6 us (10%)
  waiting for transfers between devices  7.74 us (4%)
    all_to_all x7, blocking collectives, exchange(): return lax.all_to_all(x, axis, split_axis=0, concat_axis=0, tiled=True)  106 us
    pallas_call x10, Pallas kernels, call(): pl.pallas_call(body, out_shape=tuple((jax.ShapeDtypeStruct(s, F32) for s...  46.4 us
    ppermute x8, starting transfers between devices, shifted(): return lax.ppermute(x, axis, pairs)  15.3 us
    ppermute x1, waiting for transfers between devices, body(): theirs = lax.ppermute(currents[0], ('tm', 'space'), pairs)  6.18 us
  transfers between devices with their start and end apart: 11, of which 2 were waited for; matrix products, arithmetic and copies ran while one was open for 0% of the time, Pallas kernels for 11%

profile of v4, /device:TPU:225, one launch (start us, length us, event | category | flops | bytes accessed | tf_op | source)
XLA Modules:
  0.0 180.0 jit_solution(5385836610542775268)
XLA Ops:
  0.6 2.6 %collective-permute-start = (f32[2,3]{1,0:T(2,128)}, f32[2,3]{1,0:T(2,128)S(1)}, u32[]{:S(2)}, u32[]{:S(2)}) collective-permute-start(f32[2,3]{1,0:T(2,128)} %bitcast.24), channel_id=1, source_target_pairs={{0,0},{8,8},{16,16},{24,24},{32,1},{40,9},{48,17},{56,25},{64,2},{... | collective-permute-start | bytes 80 | tf_op jit(solution)/shard_map/ppermute | solution.py:422
  3.2 6.2 %collective-permute-done.theirs = f32[2,3]{1,0:T(2,128)S(1)} collective-permute-done((f32[2,3]{1,0:T(2,128)}, f32[2,3]{1,0:T(2,128)S(1)}, u32[]{:S(2)}, u32[]{:S(2)}) %collective-permute-start) | collective-permute-done | bytes 56 | tf_op jit(solution)/shard_map/ppermute | solution.py:422
  9.9 5.0 %shard_map.68 = (f32[4,4,64,256]{3,2,1,0:T(8,128)}, f32[10,64,256]{2,1,0:T(8,128)}, f32[13,64,256]{2,1,0:T(8,128)}, f32[1,64,256]{2,1,0:T(8,128)}, f32[32,48,128]{2,1,0:T(8,128)}) custom-call(f32[4]{0:T(128)} %cond.1, f32[2,3]{1,0:T(2,128)} %bitcast.25, f32[2,3]{1,0:T(2,128)} %copy-done.1, s32[4,64,256]{2,1,0:T(8,128)} %labels_far.1, ...), custom_call_target="tpu_custom_call" | custom-call | tf_op jit(solution)/shard_map/pallas_call | solution.py:113
  14.9 22.4 %all_to_all.47.whole = f32[32,48,128]{2,1,0:T(8,128)S(1)} all-to-all(f32[32,48,128]{2,1,0:T(8,128)} %get-tuple-element.27), channel_id=1, replica_groups=mesh['tm'=8,'space'=32] {'space'}, dimensions={0} | all-to-all | bytes 1572864 | tf_op jit(solution)/shard_map/all_to_all | solution.py:392
  37.3 2.4 %collective-permute-start.2 = (f32[13,64,256]{2,1,0:T(8,128)}, f32[13,64,256]{2,1,0:T(8,128)S(1)}, u32[]{:S(2)}, u32[]{:S(2)}) collective-permute-start(f32[13,64,256]{2,1,0:T(8,128)} %get-tuple-element.37), channel_id=1, source_target_pairs={{1,0},{2,1},{3,2},{4,3},{5,4},{6,5},{7,6},{8,7},{9,8},{10,9},{11,1... | collective-permute-start | bytes 2555912 | tf_op jit(solution)/shard_map/ppermute | solution.py:388
  39.7 3.1 %collective-permute-start.1 = (f32[10,64,256]{2,1,0:T(8,128)}, f32[10,64,256]{2,1,0:T(8,128)S(1)}, u32[]{:S(2)}, u32[]{:S(2)}) collective-permute-start(f32[10,64,256]{2,1,0:T(8,128)} %get-tuple-element.36), channel_id=1, source_target_pairs={{0,1},{1,2},{2,3},{3,4},{4,5},{5,6},{6,7},{7,8},{8,9},{9,10},{10,1... | collective-permute-start | bytes 1966088 | tf_op jit(solution)/shard_map/ppermute | solution.py:388
  42.9 1.3 collective-permute-start.3
  44.2 9.6 %shard_map.69 = (f32[5,16,16,128]{3,2,1,0:T(8,128)S(1)}, f32[64,128]{1,0:T(8,128)S(1)}, f32[8,128]{1,0:T(8,128)S(1)}, f32[16,16,128]{2,1,0:T(8,128)S(1)}) custom-call(s32[2]{0:T(128)S(1)} %pad_add_fusion.where, f32[8,128]{1,0:T(8,128)S(1)} %bitcast.16, f32[32,48,128]{2,1,0:T(8,128)S(1)} %all_to_all.47.whole), custom_call_target="tpu_custom_call" | custom-call | flops 67108864 | bytes 1048576 | tf_op jit(solution)/shard_map/pallas_call | solution.py:113
  53.9 4.6 %shard_map.70 = (f32[9,4,64,256]{3,2,1,0:T(8,128)S(1)}, f32[32,128]{1,0:T(8,128)S(1)}) custom-call(s32[2]{0:T(128)S(1)} %pad_add_fusion.where, f32[64,128]{1,0:T(8,128)S(1)} %get-tuple-element.34.planes, f32[4,4,64,256]{3,2,1,0:T(8,128)S(1)} %copy-done, f32[10,64,256]{2,1,0:T(8,128)S(1)} %collective-permute-done.1.up, ...), custom_call_target="tpu_custom_call" | custom-call | tf_op jit(solution)/shard_map/pallas_call | solution.py:113
  58.5 14.5 %all_to_all.48 = f32[32,1,128]{2,1,0:T(1,128)S(1)} all-to-all(f32[32,1,128]{2,1,0:T(1,128)S(1)} %bitcast.22), channel_id=1, replica_groups=mesh['tm'=8,'space'=32] {'space'}, dimensions={0} | all-to-all | bytes 32768 | tf_op jit(solution)/shard_map/all_to_all | solution.py:392
  73.1 1.4 shard_map.71
  74.6 11.1 %all_to_all.49.ends = f32[8,8,128]{2,1,0:T(8,128)S(1)} all-to-all(f32[8,8,128]{2,1,0:T(8,128)S(1)} %get-tuple-element.42), channel_id=1, replica_groups=mesh['tm'=8,'space'=32] {'tm'}, dimensions={0} | all-to-all | bytes 65536 | tf_op jit(solution)/shard_map/all_to_all | solution.py:392
  85.8 16.8 %all_to_all.50.ours = f32[32,32,128]{2,1,0:T(8,128)S(1)} all-to-all(f32[32,32,128]{2,1,0:T(8,128)S(1)} %shard_map.72), channel_id=1, replica_groups=mesh['tm'=8,'space'=32] {'space'}, dimensions={0} | all-to-all | bytes 1048576 | tf_op jit(solution)/shard_map/all_to_all | solution.py:392
  103.0 2.0 %collective-permute-start.7 = (f32[4,64,256]{2,1,0:T(8,128)S(1)}, f32[4,64,256]{2,1,0:T(8,128)S(1)}, u32[]{:S(2)}, u32[]{:S(2)}) collective-permute-start(f32[4,64,256]{2,1,0:T(8,128)S(1)} %collective-permute-done.4.rest.refs_0_.rest_first), channel_id=1, source_target_pairs={{1,0},{2,1},{3,2},{4,3},{5,4},{6,5},{7,6},{8,7},{9,8},{10,9},{11,1... | collective-permute-start | bytes 786440 | tf_op jit(solution)/shard_map/ppermute | solution.py:388
  105.0 3.5 %collective-permute-start.6 = (f32[4,64,256]{2,1,0:T(8,128)S(1)}, f32[4,64,256]{2,1,0:T(8,128)S(1)}, u32[]{:S(2)}, u32[]{:S(2)}) collective-permute-start(f32[4,64,256]{2,1,0:T(8,128)S(1)} %collective-permute-done.4.rest.refs_0_.rest_first), channel_id=1, source_target_pairs={{0,1},{1,2},{2,3},{3,4},{4,5},{5,6},{6,7},{7,8},{8,9},{9,10},{10,1... | collective-permute-start | bytes 786440 | tf_op jit(solution)/shard_map/ppermute | solution.py:388
  108.5 1.5 collective-permute-start.8
  110.0 9.9 %shard_map.73 = (f32[64,128]{1,0:T(8,128)S(1)}, f32[8,128]{1,0:T(8,128)S(1)}, f32[16,16,128]{2,1,0:T(8,128)S(1)}) custom-call(s32[2]{0:T(128)S(1)} %pad_add_fusion.where, f32[8,128]{1,0:T(8,128)S(1)} %bitcast.17, f32[5,16,16,128]{3,2,1,0:T(8,128)S(1)} %get-tuple-element.32.static, f32[16,16,128]{2,1,0:T(8,128)S(1)} %get-tuple-element.33.begin, ...), custom_call_target="tpu_custom_call" | custom-call | flops 67108864 | bytes 1048576 | tf_op jit(solution)/shard_map/pallas_call | solution.py:113
  119.9 4.7 %shard_map.74 = (f32[9,4,64,256]{3,2,1,0:T(8,128)S(1)}, f32[32,128]{1,0:T(8,128)S(1)}) custom-call(s32[2]{0:T(128)S(1)} %pad_add_fusion.where, f32[64,128]{1,0:T(8,128)S(1)} %get-tuple-element.45.planes, f32[4,4,64,256]{3,2,1,0:T(8,128)S(1)} %copy-done, f32[10,64,256]{2,1,0:T(8,128)S(1)} %collective-permute-done.1.up, ...), custom_call_target="tpu_custom_call" | custom-call | tf_op jit(solution)/shard_map/pallas_call | solution.py:113
  124.6 14.2 %all_to_all.51 = f32[32,1,128]{2,1,0:T(1,128)S(1)} all-to-all(f32[32,1,128]{2,1,0:T(1,128)S(1)} %bitcast.21), channel_id=1, replica_groups=mesh['tm'=8,'space'=32] {'space'}, dimensions={0} | all-to-all | bytes 32768 | tf_op jit(solution)/shard_map/all_to_all | solution.py:392
  138.7 1.4 shard_map.75
  141.4 10.4 %all_to_all.52.ends = f32[8,8,128]{2,1,0:T(8,128)S(1)} all-to-all(f32[8,8,128]{2,1,0:T(8,128)S(1)} %get-tuple-element.50), channel_id=1, replica_groups=mesh['tm'=8,'space'=32] {'tm'}, dimensions={0} | all-to-all | bytes 65536 | tf_op jit(solution)/shard_map/all_to_all | solution.py:392
  151.9 16.4 %all_to_all.53.ours = f32[32,32,128]{2,1,0:T(8,128)S(1)} all-to-all(f32[32,32,128]{2,1,0:T(8,128)S(1)} %shard_map.76), channel_id=1, replica_groups=mesh['tm'=8,'space'=32] {'space'}, dimensions={0} | all-to-all | bytes 1048576 | tf_op jit(solution)/shard_map/all_to_all | solution.py:392
  168.8 1.5 collective-permute-done.10.theirs
  170.3 9.7 %shard_map.77 = f32[4,64,256]{2,1,0:T(8,128)} custom-call(s32[2]{0:T(128)S(1)} %pad_add_fusion.where, f32[8,128]{1,0:T(8,128)S(1)} %bitcast.18, f32[5,16,16,128]{3,2,1,0:T(8,128)S(1)} %get-tuple-element.32.static, f32[16,16,128]{2,1,0:T(8,128)S(1)} %get-tuple-element.44.begin, f32[4,64,256]{2,1,0:T(8,128)S(1)} %collective-permute-done.4.rest.refs_0_.rest_first, ...), custom_call_target="tpu_custom_call" | custom-call | flops 67108864 | bytes 1048576 | tf_op jit(solution)/shard_map/pallas_call | solution.py:113
  (22 shorter events, 3.0 us)
Async XLA Ops:
  0.6 8.7 %collective-permute-start = (f32[2,3]{1,0:T(2,128)}, f32[2,3]{1,0:T(2,128)S(1)}, u32[]{:S(2)}, u32[]{:S(2)}) collective-permute-start(f32[2,3]{1,0:T(2,128)} %bitcast.24), channel_id=1, source_target_pairs={{0,0},{8,8},{16,16},{24,24},{32,1},{40,9},{48,17},{56,25},{64,2},{... | collective-permute-start | bytes 80 | tf_op jit(solution)/shard_map/ppermute | solution.py:422
  9.4 0.6 copy-start.1
  14.9 39.0 %copy-start = (f32[4,4,64,256]{3,2,1,0:T(8,128)S(1)}, f32[4,4,64,256]{3,2,1,0:T(8,128)}, u32[]{:S(2)}) copy-start(f32[4,4,64,256]{3,2,1,0:T(8,128)} %get-tuple-element.35.own) | copy-start | bytes 3145732
  37.3 16.6 %collective-permute-start.2 = (f32[13,64,256]{2,1,0:T(8,128)}, f32[13,64,256]{2,1,0:T(8,128)S(1)}, u32[]{:S(2)}, u32[]{:S(2)}) collective-permute-start(f32[13,64,256]{2,1,0:T(8,128)} %get-tuple-element.37), channel_id=1, source_target_pairs={{1,0},{2,1},{3,2},{4,3},{5,4},{6,5},{7,6},{8,7},{9,8},{10,9},{11,1... | collective-permute-start | bytes 2555912 | tf_op jit(solution)/shard_map/ppermute | solution.py:388
  39.7 14.1 %collective-permute-start.1 = (f32[10,64,256]{2,1,0:T(8,128)}, f32[10,64,256]{2,1,0:T(8,128)S(1)}, u32[]{:S(2)}, u32[]{:S(2)}) collective-permute-start(f32[10,64,256]{2,1,0:T(8,128)} %get-tuple-element.36), channel_id=1, source_target_pairs={{0,1},{1,2},{2,3},{3,4},{4,5},{5,6},{6,7},{7,8},{8,9},{9,10},{10,1... | collective-permute-start | bytes 1966088 | tf_op jit(solution)/shard_map/ppermute | solution.py:388
  42.9 11.0 %collective-permute-start.3 = (f32[1,64,256]{2,1,0:T(8,128)}, f32[1,64,256]{2,1,0:T(8,128)S(1)}, u32[]{:S(2)}, u32[]{:S(2)}) collective-permute-start(f32[1,64,256]{2,1,0:T(8,128)} %get-tuple-element.38), channel_id=1, source_target_pairs={{2,0},{3,1},{4,2},{5,3},{6,4},{7,5},{8,6},{9,7},{10,8},{11,9},{12,... | collective-permute-start | bytes 196616 | tf_op jit(solution)/shard_map/ppermute | solution.py:388
  74.5 11.2 %collective-permute-start.4 = (f32[4,64,256]{2,1,0:T(8,128)S(1)}, f32[4,64,256]{2,1,0:T(8,128)S(1)}, u32[]{:S(2)}, u32[]{:S(2)}) collective-permute-start(f32[4,64,256]{2,1,0:T(8,128)S(1)} %get-tuple-element.43), channel_id=1, source_target_pairs={{0,32},{32,64},{64,96},{96,128},{128,160},{160,192},{192,224},{224... | collective-permute-start | bytes 786440 | tf_op jit(solution)/shard_map/ppermute | solution.py:388
  102.6 7.5 %collective-permute-start.5 = (f32[32,32,128]{2,1,0:T(8,128)S(1)}, f32[32,32,128]{2,1,0:T(8,128)S(1)}, u32[]{:S(2)}, u32[]{:S(2)}) collective-permute-start(f32[32,32,128]{2,1,0:T(8,128)S(1)} %all_to_all.50.ours), channel_id=1, source_target_pairs={{0,1},{1,0},{2,3},{3,2},{4,5},{5,4},{6,7},{7,6},{8,9},{9,8},{10,11... | collective-permute-start | bytes 1572872 | tf_op jit(solution)/shard_map/ppermute | solution.py:399
  103.0 17.0 %collective-permute-start.7 = (f32[4,64,256]{2,1,0:T(8,128)S(1)}, f32[4,64,256]{2,1,0:T(8,128)S(1)}, u32[]{:S(2)}, u32[]{:S(2)}) collective-permute-start(f32[4,64,256]{2,1,0:T(8,128)S(1)} %collective-permute-done.4.rest.refs_0_.rest_first), channel_id=1, source_target_pairs={{1,0},{2,1},{3,2},{4,3},{5,4},{6,5},{7,6},{8,7},{9,8},{10,9},{11,1... | collective-permute-start | bytes 786440 | tf_op jit(solution)/shard_map/ppermute | solution.py:388
  105.0 15.0 %collective-permute-start.6 = (f32[4,64,256]{2,1,0:T(8,128)S(1)}, f32[4,64,256]{2,1,0:T(8,128)S(1)}, u32[]{:S(2)}, u32[]{:S(2)}) collective-permute-start(f32[4,64,256]{2,1,0:T(8,128)S(1)} %collective-permute-done.4.rest.refs_0_.rest_first), channel_id=1, source_target_pairs={{0,1},{1,2},{2,3},{3,4},{4,5},{5,6},{6,7},{7,8},{8,9},{9,10},{10,1... | collective-permute-start | bytes 786440 | tf_op jit(solution)/shard_map/ppermute | solution.py:388
  108.5 11.4 %collective-permute-start.8 = (f32[1,64,256]{2,1,0:T(8,128)S(1)}, f32[1,64,256]{2,1,0:T(8,128)S(1)}, u32[]{:S(2)}, u32[]{:S(2)}) collective-permute-start(f32[1,64,256]{2,1,0:T(8,128)S(1)} %slice.9), channel_id=1, source_target_pairs={{2,0},{3,1},{4,2},{5,3},{6,4},{7,5},{8,6},{9,7},{10,8},{11,9},{12,... | collective-permute-start | bytes 196616 | tf_op jit(solution)/shard_map/ppermute | solution.py:388
  140.1 11.7 %collective-permute-start.9 = (f32[4,64,256]{2,1,0:T(8,128)S(1)}, f32[4,64,256]{2,1,0:T(8,128)S(1)}, u32[]{:S(2)}, u32[]{:S(2)}) collective-permute-start(f32[4,64,256]{2,1,0:T(8,128)S(1)} %get-tuple-element.49), channel_id=1, source_target_pairs={{0,32},{32,64},{64,96},{96,128},{128,160},{160,192},{192,224},{1,3... | collective-permute-start | bytes 786440 | tf_op jit(solution)/shard_map/ppermute | solution.py:388
  168.4 1.9 %collective-permute-start.10 = (f32[32,32,128]{2,1,0:T(8,128)S(1)}, f32[32,32,128]{2,1,0:T(8,128)S(1)}, u32[]{:S(2)}, u32[]{:S(2)}) collective-permute-start(f32[32,32,128]{2,1,0:T(8,128)S(1)} %all_to_all.53.ours), channel_id=1, source_target_pairs={{0,1},{1,0},{2,3},{3,2},{4,5},{5,4},{6,7},{7,6},{8,9},{9,8},{10,11... | collective-permute-start | bytes 1572872 | tf_op jit(solution)/shard_map/ppermute | solution.py:399

commit v5 on v4

--- a/solution.py
+++ b/solution.py
@@ -8,7 +8,6 @@
 from jax.sharding import PartitionSpec as P
 
 PHASES = 3
-CG_COARSE = 4
 F32 = jnp.float32
 HIGHEST = lax.Precision.HIGHEST
 VMEM = pltpu.MemorySpace.VMEM
@@ -68,30 +67,40 @@
     return out + jnp.where(inner == 0, 0.0, pltpu.roll(v, 1, 2)) + jnp.where(inner == 63, 0.0, pltpu.roll(v, 127, 2))
 
 
-def coarse_solve(start, source, diagonal):
+def coarse_solve(start, source, scaled):
     def apply(v):
-        return diagonal * v - 0.0625 * coarse_beside(v)
-
-    x = start
-    residual = source - 0.375 * start + 0.0625 * coarse_beside(start)
-    image = apply(residual)
-    norm, product = total(residual * residual), total(residual * image)
-    step = norm / product
-    direction, moved = residual, image
-    for turn in range(CG_COARSE):
-        inverse = 1.0 / norm
-        scaled = inverse / step
-        x = x + step[None] * direction
-        if turn + 1 < CG_COARSE:
-            residual = residual - step[None] * moved
-            image = apply(residual)
-            new, product = total(residual * residual), total(residual * image)
-            ratio = new * inverse
-            step = new / (product - new * (new * scaled))
-            direction = residual + ratio[None] * direction
-            moved = image + ratio[None] * moved
-            norm = new
-    return x
+        return scaled * v - 0.1 * coarse_beside(v)
+
+    v0 = source - 0.375 * start + 0.0625 * coarse_beside(start)
+    v1 = apply(v0)
+    v2 = 2.0 * apply(v1) - v0
+    v3 = 2.0 * apply(v2) - v1
+    p = [total(a * b) for a, b in ((v0, v0), (v0, v1), (v1, v1), (v1, v2), (v2, v2), (v2, v3), (v3, v3))]
+    m = p[:2] + [2.0 * p[k] - p[k & 1] for k in range(2, 7)]
+    last = total(v3 * apply(v3))
+
+    def entry(i, j):
+        both = 0.5 * (m[i + j] + m[abs(i - j)])
+        if i == j == 3:
+            return both + last
+        return both + 0.25 * (m[i + j + 1] + m[abs(i + j - 1)] + m[abs(i - j + 1)] + m[abs(i - j - 1)])
+
+    right = m[:4]
+    rows = {(i, j): entry(i, j) for i in range(4) for j in range(i + 1)}
+    whole = [rows[k, k] for k in range(4)]
+    inverse = []
+    for k in range(4):
+        inverse.append(jnp.where(rows[k, k] > 1e-6 * whole[k], 1.0 / rows[k, k], 0.0))
+        for i in range(k + 1, 4):
+            factor = rows[i, k] * inverse[k]
+            right[i] = right[i] - factor * right[k]
+            for j in range(k + 1, i + 1):
+                rows[i, j] = rows[i, j] - factor * rows[j, k]
+    y = [None] * 4
+    for k in (3, 2, 1, 0):
+        y[k] = (right[k] - sum(rows[i, k] * y[i] for i in range(k + 1, 4))) * inverse[k]
+    y = [1.6 * value[None] for value in y]
+    return start + (y[0] * v0 + y[1] * v1) + (y[2] * v2 + y[3] * v3)
 
 
 def cut_planes(state, place, offsets):
@@ -178,34 +187,38 @@
     return source
 
 
-def sweep(where, cur, state, static, advanced, planes, correction):
+def solve_slice(cur, state, static, n):
+    state[...] = coarse_solve(state[...], slice_source(cur, static, n), 0.8 * static[1] - 0.4)
+
+
+AROUND = (-1, 0, 1, 2)
+
+
+def first_sweep_kernel(where, cur, whole, static, planes, advanced, state):
     mine, place = where[0], where[1]
+    for k in range(5):
+        static[k] = unpack_all(whole, 8 * k)
+    state[...] = static[0]
 
     def turn(n, carry):
         @pl.when(n == mine)
         def _():
-            for k, plane in enumerate(cut_planes(state, place, (-1, 0, 1, 2))):
+            for k, plane in enumerate(cut_planes(state, place, AROUND)):
                 planes[16 * k : 16 * k + 16] = plane
 
-        state[...] = coarse_solve(state[...], slice_source(cur, static, n), static[1] * 0.5 + 0.375)
+        solve_slice(cur, state, static, n)
 
         @pl.when(n == mine)
         def _():
-            (plane,) = cut_planes(state, place, (0,))
-            advanced[...] = plane[:8] + pltpu.roll(plane[8:], 64, 1)
-
-        if correction is not None:
-            state[...] = state[...] + correction[n]
+            advanced[...] = pack(*cut_planes(state, place, (0,)))
+
         return carry
 
     lax.fori_loop(0, 8, turn, 0)
 
 
-def first_sweep_kernel(where, cur, whole, static, planes, advanced, state):
-    for k in range(5):
-        static[k] = unpack_all(whole, 8 * k)
-    state[...] = static[0]
-    sweep(where, cur, state, static, advanced, planes, None)
+def pack(plane):
+    return plane[:8] + pltpu.roll(plane[8:], 64, 1)
 
 
 def load_corrections(where, ours, theirs, correction):
@@ -215,33 +228,63 @@
         correction[4 * (1 - odd) + k] = unpack_all(theirs, 8 * k)
 
 
-def next_sweep_kernel(where, cur, static, begin, ours, theirs, planes, advanced, state, correction):
+def next_sweep_kernel(where, cur, static, begin, old, ours, theirs, planes, advanced, state, kept, correction):
+    mine, place = where[0], where[1]
     load_corrections(where, ours, theirs, correction)
     state[...] = begin[...]
-    sweep(where, cur, state, static, advanced, planes, correction)
-
-
-def last_sweep_kernel(where, cur, static, begin, rest_first, rest_other, ours, theirs,
-                      start, state, correction, planes):
+
+    @pl.when(mine == 0)
+    def _():
+        for k, plane in enumerate(cut_planes(state, place, AROUND)):
+            planes[16 * k : 16 * k + 16] = plane
+
+    def turn(n, carry):
+        solve_slice(cur, state, static, n)
+
+        @pl.when(n == mine)
+        def _():
+            advanced[...] = pack(*cut_planes(state, place, (0,)))
+
+        @pl.when(n == mine - 1)
+        def _():
+            around = cut_planes(state, place, AROUND)
+            kept[...] = around[1]
+            for k, plane in enumerate(around):
+                planes[16 * k : 16 * k + 16] = plane - old[16 * k : 16 * k + 16]
+
+        @pl.when(jnp.logical_and(n == 7, mine == 0))
+        def _():
+            (new,), (before,) = cut_planes(state, place, (0,)), cut_planes(begin, place, (0,))
+            kept[...] = new - before
+
+        state[...] = state[...] + correction[n]
+        return carry
+
+    lax.fori_loop(0, 8, turn, 0)
+
+
+def last_sweep_kernel(where, cur, static, begin, kept, moved_first, moved_other, ours, theirs,
+                      start, state, correction, plane):
+    mine, place = where[0], where[1]
     load_corrections(where, ours, theirs, correction)
     state[...] = begin[...]
-
-    def keep():
-        (plane,) = cut_planes(state, where[1], (0,))
-        planes[...] = plane
-
-    mine = where[0]
+    plane[...] = kept[...]
 
     def turn(n, carry):
-        solved = coarse_solve(state[...], slice_source(cur, static, n), static[1] * 0.5 + 0.375)
-        state[...] = solved + correction[n]
+        solve_slice(cur, state, static, n)
+
+        @pl.when(n == mine - 1)
+        def _():
+            (new,) = cut_planes(state, place, (0,))
+            plane[...] = new - kept[...]
+
+        state[...] = state[...] + correction[n]
         return carry
 
     lax.fori_loop(0, mine, turn, 0)
-    keep()
-    (own,) = widen(planes[...])
+    (own,) = widen(plane[...])
     first = (mine == 0).astype(F32)
-    start[...] = own[None] + (first * rest_first[...] + (1.0 - first) * rest_other[...])
+    start[...] = own[None] + (first * moved_first[0:4] + (1.0 - first) * moved_other[0:4])
 
 
 def fine_beside(v):
@@ -268,7 +311,8 @@
         (rest_far,), refs = refs[:1], refs[1:]
         rest, rest_up, rest_down = own.at[3], up, down
     else:
-        (rest, rest_up, rest_down, rest_far), refs = refs[:4], refs[4:]
+        (rest, rest_up, rest_down), refs = refs[:3], refs[3:]
+        rest_far = rest_down.at[4:5]
     fields, packed, u, r, w, q, a = refs
     first = 4 * where[1]
     zero = (where[0] == 0).astype(F32)
@@ -330,12 +374,12 @@
     for k in range(28):
         row = jnp.where(lane == k, total(sums[k]), row)
     packed[...] = jnp.broadcast_to(row, packed.shape)
-    fields[0] = u[4:8]
-    fields[1] = r[3:7]
-    fields[2] = w[2:6]
+    fields[0] = u[4:9]
+    fields[1] = r[3:8]
+    fields[2] = w[2:7]
     for k in range(3):
-        fields[3 + k] = q[k, 1:5]
-        fields[6 + k] = a[k, 0:4]
+        fields[3 + k] = q[k, 1:6]
+        fields[6 + k] = a[k, 0:5]
 
 
 PAIRS = ((0, 0), (0, 1), (0, 2), (1, 1), (1, 2), (2, 2))
@@ -352,7 +396,7 @@
     return step + second * (keep + ratio), -second * step
 
 
-def finish_kernel(sums, fields, advanced, fine, rest, ends):
+def finish_kernel(sums, fields, advanced, fine, moved, ends):
     row = jnp.sum(sums[...], axis=0, keepdims=True)
     lane = iota((1, 128), 1)
     m = [jnp.sum(jnp.where(lane == k, row, 0.0), axis=1, keepdims=True) for k in range(28)]
@@ -361,18 +405,15 @@
     after = [sum(factor[pair] * m[4 + 4 * p + k] for p, pair in enumerate(PAIRS)) for k in range(4)]
     c, d = weights(*after)
     scales = (None, a, b, c, c * a, c * b, d, d * a, d * b)
-    for i in range(4):
+    for i in range(5):
         value = fields[0, i]
         for k in range(1, 9):
             value = value + scales[k] * fields[k, i]
-        fine[i] = value
-    own = restrict_packed(jnp.sum(fine[...], axis=0))
+        moved[i] = value
+        if i < 4:
+            fine[i] = value
+    own = restrict_packed(jnp.sum(moved[0:4], axis=0))
     ends[...] = jnp.broadcast_to((own - advanced[...])[None], ends.shape)
-    left = iota((8, 128), 1) < 64
-    plane = jnp.concatenate([jnp.where(left, own, 0.0), jnp.where(left, pltpu.roll(own, 64, 1), 0.0)], axis=0)
-    (lifted,) = widen(plane)
-    for i in range(4):
-        rest[i] = fine[i] - lifted
 
 
 def spread_kernel(ends, rest, packed):
@@ -397,14 +438,6 @@
     half = exchange(packed, "space")
     places = lax.axis_size("space")
     return half, lax.ppermute(half, "space", [(i, i ^ 1) for i in range(places)])
-
-
-def halos(x):
-    return (
-        shifted(x, "space", 1, False),
-        shifted(x, "space", -1, False),
-        shifted(x[:1], "space", -2, False),
-    )
 
 
 def body(labels, conductivity, coil_pattern, currents, initial_state):
@@ -447,35 +480,34 @@
     def fine(initial, planes, advanced, rest):
         fields, sums = call(
             functools.partial(fine_kernel, initial),
-            ((9, *block), (32, 128)),
+            ((9, 5, 64, 256), (32, 128)),
             (where, planes, own, up, down, *rest),
             small=(0,),
             scratch=((13, 64, 256), (11, 64, 256), (9, 64, 256), (3, 7, 64, 256), (3, 5, 64, 256)),
         )
         return call(
             finish_kernel,
-            (block, block, (8, 8, 128)),
+            (block, (5, 64, 256), (8, 8, 128)),
             (exchange(sums, "space"), fields, advanced),
         )
 
-    _, rest, ends = fine(True, planes, advanced, (far,))
-    rest_first = shifted(rest, "tm", 1, True)
-    planes, advanced_next, state_next = call(
+    _, moved, ends = fine(True, planes, advanced, (far,))
+    moved_first = shifted(moved, "tm", 1, True)
+    planes, advanced, state, kept = call(
         next_sweep_kernel,
-        ((64, 128), (8, 128), field),
-        (where, table, static, state, *everywhere(ends, rest_first)),
+        ((64, 128), (8, 128), field, (16, 128)),
+        (where, table, static, state, planes, *everywhere(ends, moved_first)),
         small=(0, 1),
         scratch=((8, *field),),
         flops=1 << 26,
     )
-    fine_state, rest, ends = fine(
-        False, planes, advanced_next, (rest_first, *halos(rest_first))
-    )
-    rest_other = shifted(rest, "tm", 1, False)
+    around = (shifted(moved_first, "space", 1, False), shifted(moved_first, "space", -1, False))
+    fine_state, moved, ends = fine(False, planes, advanced, (moved_first, *around))
+    moved_other = shifted(moved, "tm", 1, False)
     (start,) = call(
         last_sweep_kernel,
         (block,),
-        (where, table, static, state_next, rest_first, rest_other, *everywhere(ends, rest_other)),
+        (where, table, static, state, kept, moved_first, moved_other, *everywhere(ends, moved_other)),
         small=(0, 1),
         scratch=(field, (8, *field), (16, 128)),
         flops=1 << 26,

time: 181 us -> 171 us (0.945)
  Pallas kernels: 46.4 us -> 39.1 us
  blocking collectives: 106 us -> 103 us
    pallas_call x10, Pallas kernels: 46.4 us -> 39.1 us  [call(): pl.pallas_call(body, out_shape=tuple((jax.ShapeDtypeStruct(s, F32) for s...]
    all_to_all x7, blocking collectives: 106 us -> 103 us  [exchange(): return lax.all_to_all(x, axis, split_axis=0, concat_axis=0, tiled=True)]
    ppermute x8 -> x7, starting transfers between devices: 15.3 us -> 13.8 us  [shifted(): return lax.ppermute(x, axis, pairs)]
  transfers between devices with their start and end apart: 11 -> 10, of which waited for: 2 -> 3; matrix products, arithmetic and copies ran while one was open for 0% -> 0% of each run, Pallas kernels for 11% -> 9%
where the time goes in v5:
time: 171 us; the launch traced here: 169 us
  blocking collectives  103 us (60%)
  Pallas kernels  39.1 us (23%)
  starting transfers between devices  17.2 us (10%)
  waiting for transfers between devices  8.49 us (5%)
    all_to_all x7, blocking collectives, exchange(): return lax.all_to_all(x, axis, split_axis=0, concat_axis=0, tiled=True)  103 us
    pallas_call x10, Pallas kernels, call(): pl.pallas_call(body, out_shape=tuple((jax.ShapeDtypeStruct(s, F32) for s...  39.1 us
    ppermute x7, starting transfers between devices, shifted(): return lax.ppermute(x, axis, pairs)  13.8 us
    ppermute x1, waiting for transfers between devices, body(): theirs = lax.ppermute(currents[0], ('tm', 'space'), pairs)  6.18 us
  transfers between devices with their start and end apart: 10, of which 3 were waited for; matrix products, arithmetic and copies ran while one was open for 0% of the time, Pallas kernels for 9%

profile of v5, /device:TPU:225, one launch (start us, length us, event | category | flops | bytes accessed | tf_op | source)
XLA Modules:
  0.0 169.4 jit_solution(7709942325334688125)
XLA Ops:
  0.6 2.6 %collective-permute-start = (f32[2,3]{1,0:T(2,128)}, f32[2,3]{1,0:T(2,128)S(1)}, u32[]{:S(2)}, u32[]{:S(2)}) collective-permute-start(f32[2,3]{1,0:T(2,128)} %bitcast.24), channel_id=1, source_target_pairs={{0,0},{8,8},{16,16},{24,24},{32,1},{40,9},{48,17},{56,25},{64,2},{... | collective-permute-start | bytes 80 | tf_op jit(solution)/shard_map/ppermute | solution.py:455
  3.2 6.2 %collective-permute-done.theirs = f32[2,3]{1,0:T(2,128)S(1)} collective-permute-done((f32[2,3]{1,0:T(2,128)}, f32[2,3]{1,0:T(2,128)S(1)}, u32[]{:S(2)}, u32[]{:S(2)}) %collective-permute-start) | collective-permute-done | bytes 56 | tf_op jit(solution)/shard_map/ppermute | solution.py:455
  9.9 5.0 %shard_map.68 = (f32[4,4,64,256]{3,2,1,0:T(8,128)}, f32[10,64,256]{2,1,0:T(8,128)}, f32[13,64,256]{2,1,0:T(8,128)}, f32[1,64,256]{2,1,0:T(8,128)}, f32[32,48,128]{2,1,0:T(8,128)}) custom-call(f32[4]{0:T(128)} %cond.1, f32[2,3]{1,0:T(2,128)} %bitcast.25, f32[2,3]{1,0:T(2,128)} %copy-done.1, s32[4,64,256]{2,1,0:T(8,128)} %labels_far.1, ...), custom_call_target="tpu_custom_call" | custom-call | tf_op jit(solution)/shard_map/pallas_call | solution.py:122
  14.9 22.4 %all_to_all.47.whole = f32[32,48,128]{2,1,0:T(8,128)S(1)} all-to-all(f32[32,48,128]{2,1,0:T(8,128)} %get-tuple-element.28), channel_id=1, replica_groups=mesh['tm'=8,'space'=32] {'space'}, dimensions={0} | all-to-all | bytes 1572864 | tf_op jit(solution)/shard_map/all_to_all | solution.py:433
  37.3 2.4 %collective-permute-start.2 = (f32[13,64,256]{2,1,0:T(8,128)}, f32[13,64,256]{2,1,0:T(8,128)S(1)}, u32[]{:S(2)}, u32[]{:S(2)}) collective-permute-start(f32[13,64,256]{2,1,0:T(8,128)} %get-tuple-element.38), channel_id=1, source_target_pairs={{1,0},{2,1},{3,2},{4,3},{5,4},{6,5},{7,6},{8,7},{9,8},{10,9},{11,1... | collective-permute-start | bytes 2555912 | tf_op jit(solution)/shard_map/ppermute | solution.py:429
  39.7 3.1 %collective-permute-start.1 = (f32[10,64,256]{2,1,0:T(8,128)}, f32[10,64,256]{2,1,0:T(8,128)S(1)}, u32[]{:S(2)}, u32[]{:S(2)}) collective-permute-start(f32[10,64,256]{2,1,0:T(8,128)} %get-tuple-element.37), channel_id=1, source_target_pairs={{0,1},{1,2},{2,3},{3,4},{4,5},{5,6},{6,7},{7,8},{8,9},{9,10},{10,1... | collective-permute-start | bytes 1966088 | tf_op jit(solution)/shard_map/ppermute | solution.py:429
  42.9 1.3 collective-permute-start.3
  44.3 7.2 %shard_map.69 = (f32[5,16,16,128]{3,2,1,0:T(8,128)S(1)}, f32[64,128]{1,0:T(8,128)S(1)}, f32[8,128]{1,0:T(8,128)S(1)}, f32[16,16,128]{2,1,0:T(8,128)S(1)}) custom-call(s32[2]{0:T(128)S(1)} %pad_add_fusion.where, f32[8,128]{1,0:T(8,128)S(1)} %bitcast.16, f32[32,48,128]{2,1,0:T(8,128)S(1)} %all_to_all.47.whole), custom_call_target="tpu_custom_call" | custom-call | flops 67108864 | bytes 1048576 | tf_op jit(solution)/shard_map/pallas_call | solution.py:122
  52.2 4.7 %shard_map.70 = (f32[9,5,64,256]{3,2,1,0:T(8,128)S(1)}, f32[32,128]{1,0:T(8,128)S(1)}) custom-call(s32[2]{0:T(128)S(1)} %pad_add_fusion.where, f32[64,128]{1,0:T(8,128)S(1)} %get-tuple-element.35.planes.old, f32[4,4,64,256]{3,2,1,0:T(8,128)S(1)} %copy-done, f32[10,64,256]{2,1,0:T(8,128)S(1)} %collective-permute-done.1.up, ...), custom_call_target="tpu_custom_call" | custom-call | tf_op jit(solution)/shard_map/pallas_call | solution.py:122
  56.9 13.8 %all_to_all.48 = f32[32,1,128]{2,1,0:T(1,128)S(1)} all-to-all(f32[32,1,128]{2,1,0:T(1,128)S(1)} %bitcast.22), channel_id=1, replica_groups=mesh['tm'=8,'space'=32] {'space'}, dimensions={0} | all-to-all | bytes 32768 | tf_op jit(solution)/shard_map/all_to_all | solution.py:433
  70.7 1.1 shard_map.71
  72.0 11.1 %all_to_all.49.ends = f32[8,8,128]{2,1,0:T(8,128)S(1)} all-to-all(f32[8,8,128]{2,1,0:T(8,128)S(1)} %get-tuple-element.43), channel_id=1, replica_groups=mesh['tm'=8,'space'=32] {'tm'}, dimensions={0} | all-to-all | bytes 65536 | tf_op jit(solution)/shard_map/all_to_all | solution.py:433
  83.1 16.8 %all_to_all.50.ours = f32[32,32,128]{2,1,0:T(8,128)S(1)} all-to-all(f32[32,32,128]{2,1,0:T(8,128)S(1)} %shard_map.72), channel_id=1, replica_groups=mesh['tm'=8,'space'=32] {'space'}, dimensions={0} | all-to-all | bytes 1048576 | tf_op jit(solution)/shard_map/all_to_all | solution.py:433
  100.3 2.0 %collective-permute-start.7 = (f32[5,64,256]{2,1,0:T(8,128)S(1)}, f32[5,64,256]{2,1,0:T(8,128)S(1)}, u32[]{:S(2)}, u32[]{:S(2)}) collective-permute-start(f32[5,64,256]{2,1,0:T(8,128)S(1)} %collective-permute-done.4.rest.refs_0_.moved_first), channel_id=1, source_target_pairs={{1,0},{2,1},{3,2},{4,3},{5,4},{6,5},{7,6},{8,7},{9,8},{10,9},{11,1... | collective-permute-start | bytes 983048 | tf_op jit(solution)/shard_map/ppermute | solution.py:429
  102.3 3.5 %collective-permute-start.6 = (f32[5,64,256]{2,1,0:T(8,128)S(1)}, f32[5,64,256]{2,1,0:T(8,128)S(1)}, u32[]{:S(2)}, u32[]{:S(2)}) collective-permute-start(f32[5,64,256]{2,1,0:T(8,128)S(1)} %collective-permute-done.4.rest.refs_0_.moved_first), channel_id=1, source_target_pairs={{0,1},{1,2},{2,3},{3,4},{4,5},{5,6},{6,7},{7,8},{8,9},{9,10},{10,1... | collective-permute-start | bytes 983048 | tf_op jit(solution)/shard_map/ppermute | solution.py:429
  105.9 7.6 %shard_map.73 = (f32[64,128]{1,0:T(8,128)S(1)}, f32[8,128]{1,0:T(8,128)S(1)}, f32[16,16,128]{2,1,0:T(8,128)S(1)}, f32[16,128]{1,0:T(8,128)S(1)}) custom-call(s32[2]{0:T(128)S(1)} %pad_add_fusion.where, f32[8,128]{1,0:T(8,128)S(1)} %bitcast.17, f32[5,16,16,128]{3,2,1,0:T(8,128)S(1)} %get-tuple-element.33.static, f32[16,16,128]{2,1,0:T(8,128)S(1)} %get-tuple-element.34.begin, ...), custom_call_target="tpu_custom_call" | custom-call | flops 67108864 | bytes 1048576 | tf_op jit(solution)/shard_map/pallas_call | solution.py:122
  113.6 4.7 %shard_map.74 = (f32[9,5,64,256]{3,2,1,0:T(8,128)S(1)}, f32[32,128]{1,0:T(8,128)S(1)}) custom-call(s32[2]{0:T(128)S(1)} %pad_add_fusion.where, f32[64,128]{1,0:T(8,128)S(1)} %get-tuple-element.47.planes, f32[4,4,64,256]{3,2,1,0:T(8,128)S(1)} %copy-done, f32[10,64,256]{2,1,0:T(8,128)S(1)} %collective-permute-done.1.up, ...), custom_call_target="tpu_custom_call" | custom-call | tf_op jit(solution)/shard_map/pallas_call | solution.py:122
  118.2 12.1 %all_to_all.51 = f32[32,1,128]{2,1,0:T(1,128)S(1)} all-to-all(f32[32,1,128]{2,1,0:T(1,128)S(1)} %bitcast.21), channel_id=1, replica_groups=mesh['tm'=8,'space'=32] {'space'}, dimensions={0} | all-to-all | bytes 32768 | tf_op jit(solution)/shard_map/all_to_all | solution.py:433
  130.3 1.1 shard_map.75
  131.5 1.3 collective-permute-start.8
  132.8 10.3 %all_to_all.52.ends = f32[8,8,128]{2,1,0:T(8,128)S(1)} all-to-all(f32[8,8,128]{2,1,0:T(8,128)S(1)} %get-tuple-element.52), channel_id=1, replica_groups=mesh['tm'=8,'space'=32] {'tm'}, dimensions={0} | all-to-all | bytes 65536 | tf_op jit(solution)/shard_map/all_to_all | solution.py:433
  143.1 16.8 %all_to_all.53.ours = f32[32,32,128]{2,1,0:T(8,128)S(1)} all-to-all(f32[32,32,128]{2,1,0:T(8,128)S(1)} %shard_map.76), channel_id=1, replica_groups=mesh['tm'=8,'space'=32] {'space'}, dimensions={0} | all-to-all | bytes 1048576 | tf_op jit(solution)/shard_map/all_to_all | solution.py:433
  160.3 1.5 collective-permute-done.9.theirs
  161.8 7.6 %shard_map.77 = f32[4,64,256]{2,1,0:T(8,128)} custom-call(s32[2]{0:T(128)S(1)} %pad_add_fusion.where, f32[8,128]{1,0:T(8,128)S(1)} %bitcast.18, f32[5,16,16,128]{3,2,1,0:T(8,128)S(1)} %get-tuple-element.33.static, f32[16,16,128]{2,1,0:T(8,128)S(1)} %get-tuple-element.45.begin, f32[16,128]{1,0:T(8,128)S(1)} %get-tuple-element.46.kept, ...), custom_call_target="tpu_custom_call" | custom-call | flops 67108864 | bytes 1048576 | tf_op jit(solution)/shard_map/pallas_call | solution.py:122
  (19 shorter events, 2.4 us)
Async XLA Ops:
  0.6 8.7 %collective-permute-start = (f32[2,3]{1,0:T(2,128)}, f32[2,3]{1,0:T(2,128)S(1)}, u32[]{:S(2)}, u32[]{:S(2)}) collective-permute-start(f32[2,3]{1,0:T(2,128)} %bitcast.24), channel_id=1, source_target_pairs={{0,0},{8,8},{16,16},{24,24},{32,1},{40,9},{48,17},{56,25},{64,2},{... | collective-permute-start | bytes 80 | tf_op jit(solution)/shard_map/ppermute | solution.py:455
  9.4 0.6 copy-start.1
  14.9 37.3 %copy-start = (f32[4,4,64,256]{3,2,1,0:T(8,128)S(1)}, f32[4,4,64,256]{3,2,1,0:T(8,128)}, u32[]{:S(2)}) copy-start(f32[4,4,64,256]{3,2,1,0:T(8,128)} %get-tuple-element.36.own) | copy-start | bytes 3145732
  37.3 14.9 %collective-permute-start.2 = (f32[13,64,256]{2,1,0:T(8,128)}, f32[13,64,256]{2,1,0:T(8,128)S(1)}, u32[]{:S(2)}, u32[]{:S(2)}) collective-permute-start(f32[13,64,256]{2,1,0:T(8,128)} %get-tuple-element.38), channel_id=1, source_target_pairs={{1,0},{2,1},{3,2},{4,3},{5,4},{6,5},{7,6},{8,7},{9,8},{10,9},{11,1... | collective-permute-start | bytes 2555912 | tf_op jit(solution)/shard_map/ppermute | solution.py:429
  39.7 11.7 %collective-permute-start.1 = (f32[10,64,256]{2,1,0:T(8,128)}, f32[10,64,256]{2,1,0:T(8,128)S(1)}, u32[]{:S(2)}, u32[]{:S(2)}) collective-permute-start(f32[10,64,256]{2,1,0:T(8,128)} %get-tuple-element.37), channel_id=1, source_target_pairs={{0,1},{1,2},{2,3},{3,4},{4,5},{5,6},{6,7},{7,8},{8,9},{9,10},{10,1... | collective-permute-start | bytes 1966088 | tf_op jit(solution)/shard_map/ppermute | solution.py:429
  42.9 8.6 %collective-permute-start.3 = (f32[1,64,256]{2,1,0:T(8,128)}, f32[1,64,256]{2,1,0:T(8,128)S(1)}, u32[]{:S(2)}, u32[]{:S(2)}) collective-permute-start(f32[1,64,256]{2,1,0:T(8,128)} %get-tuple-element.39), channel_id=1, source_target_pairs={{2,0},{3,1},{4,2},{5,3},{6,4},{7,5},{8,6},{9,7},{10,8},{11,9},{12,... | collective-permute-start | bytes 196616 | tf_op jit(solution)/shard_map/ppermute | solution.py:429
  71.8 11.2 %collective-permute-start.4 = (f32[5,64,256]{2,1,0:T(8,128)S(1)}, f32[5,64,256]{2,1,0:T(8,128)S(1)}, u32[]{:S(2)}, u32[]{:S(2)}) collective-permute-start(f32[5,64,256]{2,1,0:T(8,128)S(1)} %get-tuple-element.44), channel_id=1, source_target_pairs={{0,32},{32,64},{64,96},{96,128},{128,160},{160,192},{192,224},{224... | collective-permute-start | bytes 983048 | tf_op jit(solution)/shard_map/ppermute | solution.py:429
  99.9 6.0 %collective-permute-start.5 = (f32[32,32,128]{2,1,0:T(8,128)S(1)}, f32[32,32,128]{2,1,0:T(8,128)S(1)}, u32[]{:S(2)}, u32[]{:S(2)}) collective-permute-start(f32[32,32,128]{2,1,0:T(8,128)S(1)} %all_to_all.50.ours), channel_id=1, source_target_pairs={{0,1},{1,0},{2,3},{3,2},{4,5},{5,4},{6,7},{7,6},{8,9},{9,8},{10,11... | collective-permute-start | bytes 1572872 | tf_op jit(solution)/shard_map/ppermute | solution.py:440
  100.3 13.2 %collective-permute-start.7 = (f32[5,64,256]{2,1,0:T(8,128)S(1)}, f32[5,64,256]{2,1,0:T(8,128)S(1)}, u32[]{:S(2)}, u32[]{:S(2)}) collective-permute-start(f32[5,64,256]{2,1,0:T(8,128)S(1)} %collective-permute-done.4.rest.refs_0_.moved_first), channel_id=1, source_target_pairs={{1,0},{2,1},{3,2},{4,3},{5,4},{6,5},{7,6},{8,7},{9,8},{10,9},{11,1... | collective-permute-start | bytes 983048 | tf_op jit(solution)/shard_map/ppermute | solution.py:429
  102.3 11.2 %collective-permute-start.6 = (f32[5,64,256]{2,1,0:T(8,128)S(1)}, f32[5,64,256]{2,1,0:T(8,128)S(1)}, u32[]{:S(2)}, u32[]{:S(2)}) collective-permute-start(f32[5,64,256]{2,1,0:T(8,128)S(1)} %collective-permute-done.4.rest.refs_0_.moved_first), channel_id=1, source_target_pairs={{0,1},{1,2},{2,3},{3,4},{4,5},{5,6},{6,7},{7,8},{8,9},{9,10},{10,1... | collective-permute-start | bytes 983048 | tf_op jit(solution)/shard_map/ppermute | solution.py:429
  131.5 11.6 %collective-permute-start.8 = (f32[5,64,256]{2,1,0:T(8,128)S(1)}, f32[5,64,256]{2,1,0:T(8,128)S(1)}, u32[]{:S(2)}, u32[]{:S(2)}) collective-permute-start(f32[5,64,256]{2,1,0:T(8,128)S(1)} %get-tuple-element.51), channel_id=1, source_target_pairs={{0,32},{32,64},{64,96},{96,128},{128,160},{160,192},{192,224},{1,3... | collective-permute-start | bytes 983048 | tf_op jit(solution)/shard_map/ppermute | solution.py:429
  159.9 1.9 %collective-permute-start.9 = (f32[32,32,128]{2,1,0:T(8,128)S(1)}, f32[32,32,128]{2,1,0:T(8,128)S(1)}, u32[]{:S(2)}, u32[]{:S(2)}) collective-permute-start(f32[32,32,128]{2,1,0:T(8,128)S(1)} %all_to_all.53.ours), channel_id=1, source_target_pairs={{0,1},{1,0},{2,3},{3,2},{4,5},{5,4},{6,7},{7,6},{8,9},{9,8},{10,11... | collective-permute-start | bytes 1572872 | tf_op jit(solution)/shard_map/ppermute | solution.py:440

commit v6 on v5

--- a/solution.py
+++ b/solution.py
@@ -8,6 +8,7 @@
 from jax.sharding import PartitionSpec as P
 
 PHASES = 3
+CG_COARSE = 4
 F32 = jnp.float32
 HIGHEST = lax.Precision.HIGHEST
 VMEM = pltpu.MemorySpace.VMEM
@@ -67,40 +68,30 @@
     return out + jnp.where(inner == 0, 0.0, pltpu.roll(v, 1, 2)) + jnp.where(inner == 63, 0.0, pltpu.roll(v, 127, 2))
 
 
-def coarse_solve(start, source, scaled):
+def coarse_solve(start, source, diagonal):
     def apply(v):
-        return scaled * v - 0.1 * coarse_beside(v)
-
-    v0 = source - 0.375 * start + 0.0625 * coarse_beside(start)
-    v1 = apply(v0)
-    v2 = 2.0 * apply(v1) - v0
-    v3 = 2.0 * apply(v2) - v1
-    p = [total(a * b) for a, b in ((v0, v0), (v0, v1), (v1, v1), (v1, v2), (v2, v2), (v2, v3), (v3, v3))]
-    m = p[:2] + [2.0 * p[k] - p[k & 1] for k in range(2, 7)]
-    last = total(v3 * apply(v3))
-
-    def entry(i, j):
-        both = 0.5 * (m[i + j] + m[abs(i - j)])
-        if i == j == 3:
-            return both + last
-        return both + 0.25 * (m[i + j + 1] + m[abs(i + j - 1)] + m[abs(i - j + 1)] + m[abs(i - j - 1)])
-
-    right = m[:4]
-    rows = {(i, j): entry(i, j) for i in range(4) for j in range(i + 1)}
-    whole = [rows[k, k] for k in range(4)]
-    inverse = []
-    for k in range(4):
-        inverse.append(jnp.where(rows[k, k] > 1e-6 * whole[k], 1.0 / rows[k, k], 0.0))
-        for i in range(k + 1, 4):
-            factor = rows[i, k] * inverse[k]
-            right[i] = right[i] - factor * right[k]
-            for j in range(k + 1, i + 1):
-                rows[i, j] = rows[i, j] - factor * rows[j, k]
-    y = [None] * 4
-    for k in (3, 2, 1, 0):
-        y[k] = (right[k] - sum(rows[i, k] * y[i] for i in range(k + 1, 4))) * inverse[k]
-    y = [1.6 * value[None] for value in y]
-    return start + (y[0] * v0 + y[1] * v1) + (y[2] * v2 + y[3] * v3)
+        return diagonal * v - 0.0625 * coarse_beside(v)
+
+    x = start
+    residual = source - 0.375 * start + 0.0625 * coarse_beside(start)
+    image = apply(residual)
+    norm, product = total(residual * residual), total(residual * image)
+    step = norm / product
+    direction, moved = residual, image
+    for turn in range(CG_COARSE):
+        inverse = 1.0 / norm
+        scaled = inverse / step
+        x = x + step[None] * direction
+        if turn + 1 < CG_COARSE:
+            residual = residual - step[None] * moved
+            image = apply(residual)
+            new, product = total(residual * residual), total(residual * image)
+            ratio = new * inverse
+            step = new / (product - new * (new * scaled))
+            direction = residual + ratio[None] * direction
+            moved = image + ratio[None] * moved
+            norm = new
+    return x
 
 
 def cut_planes(state, place, offsets):
@@ -188,7 +179,7 @@
 
 
 def solve_slice(cur, state, static, n):
-    state[...] = coarse_solve(state[...], slice_source(cur, static, n), 0.8 * static[1] - 0.4)
+    state[...] = coarse_solve(state[...], slice_source(cur, static, n), 0.5 * static[1] + 0.375)
 
 
 AROUND = (-1, 0, 1, 2)

time: 171 us -> 177 us (1.035)
  Pallas kernels: 39.1 us -> 46.2 us
    pallas_call x10, Pallas kernels: 39.1 us -> 46.2 us  [call(): pl.pallas_call(body, out_shape=tuple((jax.ShapeDtypeStruct(s, F32) for s...]
  transfers between devices with their start and end apart: 10 -> 10, of which waited for: 3 -> 2; matrix products, arithmetic and copies ran while one was open for 0% -> 0% of each run, Pallas kernels for 9% -> 11%
where the time goes in v6:
time: 177 us
  blocking collectives  104 us (59%)
  Pallas kernels  46.2 us (26%)
  starting transfers between devices  17.1 us (10%)
  waiting for transfers between devices  7.74 us (4%)
    all_to_all x7, blocking collectives, exchange(): return lax.all_to_all(x, axis, split_axis=0, concat_axis=0, tiled=True)  104 us
    pallas_call x10, Pallas kernels, call(): pl.pallas_call(body, out_shape=tuple((jax.ShapeDtypeStruct(s, F32) for s...  46.2 us
    ppermute x7, starting transfers between devices, shifted(): return lax.ppermute(x, axis, pairs)  13.8 us
    ppermute x1, waiting for transfers between devices, body(): theirs = lax.ppermute(currents[0], ('tm', 'space'), pairs)  6.18 us
  transfers between devices with their start and end apart: 10, of which 2 were waited for; matrix products, arithmetic and copies ran while one was open for 0% of the time, Pallas kernels for 11%

profile of v6, /device:TPU:225, one launch (start us, length us, event | category | flops | bytes accessed | tf_op | source)
XLA Modules:
  0.0 176.5 jit_solution(5377960570185142701)
XLA Ops:
  0.6 2.6 %collective-permute-start = (f32[2,3]{1,0:T(2,128)}, f32[2,3]{1,0:T(2,128)S(1)}, u32[]{:S(2)}, u32[]{:S(2)}) collective-permute-start(f32[2,3]{1,0:T(2,128)} %bitcast.24), channel_id=1, source_target_pairs={{0,0},{8,8},{16,16},{24,24},{32,1},{40,9},{48,17},{56,25},{64,2},{... | collective-permute-start | bytes 80 | tf_op jit(solution)/shard_map/ppermute | solution.py:446
  3.2 6.2 %collective-permute-done.theirs = f32[2,3]{1,0:T(2,128)S(1)} collective-permute-done((f32[2,3]{1,0:T(2,128)}, f32[2,3]{1,0:T(2,128)S(1)}, u32[]{:S(2)}, u32[]{:S(2)}) %collective-permute-start) | collective-permute-done | bytes 56 | tf_op jit(solution)/shard_map/ppermute | solution.py:446
  9.9 5.0 %shard_map.68 = (f32[4,4,64,256]{3,2,1,0:T(8,128)}, f32[10,64,256]{2,1,0:T(8,128)}, f32[13,64,256]{2,1,0:T(8,128)}, f32[1,64,256]{2,1,0:T(8,128)}, f32[32,48,128]{2,1,0:T(8,128)}) custom-call(f32[4]{0:T(128)} %cond.1, f32[2,3]{1,0:T(2,128)} %bitcast.25, f32[2,3]{1,0:T(2,128)} %copy-done.1, s32[4,64,256]{2,1,0:T(8,128)} %labels_far.1, ...), custom_call_target="tpu_custom_call" | custom-call | tf_op jit(solution)/shard_map/pallas_call | solution.py:113
  14.9 22.4 %all_to_all.47.whole = f32[32,48,128]{2,1,0:T(8,128)S(1)} all-to-all(f32[32,48,128]{2,1,0:T(8,128)} %get-tuple-element.28), channel_id=1, replica_groups=mesh['tm'=8,'space'=32] {'space'}, dimensions={0} | all-to-all | bytes 1572864 | tf_op jit(solution)/shard_map/all_to_all | solution.py:424
  37.3 2.4 %collective-permute-start.2 = (f32[13,64,256]{2,1,0:T(8,128)}, f32[13,64,256]{2,1,0:T(8,128)S(1)}, u32[]{:S(2)}, u32[]{:S(2)}) collective-permute-start(f32[13,64,256]{2,1,0:T(8,128)} %get-tuple-element.38), channel_id=1, source_target_pairs={{1,0},{2,1},{3,2},{4,3},{5,4},{6,5},{7,6},{8,7},{9,8},{10,9},{11,1... | collective-permute-start | bytes 2555912 | tf_op jit(solution)/shard_map/ppermute | solution.py:420
  39.7 3.1 %collective-permute-start.1 = (f32[10,64,256]{2,1,0:T(8,128)}, f32[10,64,256]{2,1,0:T(8,128)S(1)}, u32[]{:S(2)}, u32[]{:S(2)}) collective-permute-start(f32[10,64,256]{2,1,0:T(8,128)} %get-tuple-element.37), channel_id=1, source_target_pairs={{0,1},{1,2},{2,3},{3,4},{4,5},{5,6},{6,7},{7,8},{8,9},{9,10},{10,1... | collective-permute-start | bytes 1966088 | tf_op jit(solution)/shard_map/ppermute | solution.py:420
  42.9 1.3 collective-permute-start.3
  44.3 9.6 %shard_map.69 = (f32[5,16,16,128]{3,2,1,0:T(8,128)S(1)}, f32[64,128]{1,0:T(8,128)S(1)}, f32[8,128]{1,0:T(8,128)S(1)}, f32[16,16,128]{2,1,0:T(8,128)S(1)}) custom-call(s32[2]{0:T(128)S(1)} %pad_add_fusion.where, f32[8,128]{1,0:T(8,128)S(1)} %bitcast.16, f32[32,48,128]{2,1,0:T(8,128)S(1)} %all_to_all.47.whole), custom_call_target="tpu_custom_call" | custom-call | flops 67108864 | bytes 1048576 | tf_op jit(solution)/shard_map/pallas_call | solution.py:113
  53.9 4.7 %shard_map.70 = (f32[9,5,64,256]{3,2,1,0:T(8,128)S(1)}, f32[32,128]{1,0:T(8,128)S(1)}) custom-call(s32[2]{0:T(128)S(1)} %pad_add_fusion.where, f32[64,128]{1,0:T(8,128)S(1)} %get-tuple-element.35.planes.old, f32[4,4,64,256]{3,2,1,0:T(8,128)S(1)} %copy-done, f32[10,64,256]{2,1,0:T(8,128)S(1)} %collective-permute-done.1.up, ...), custom_call_target="tpu_custom_call" | custom-call | tf_op jit(solution)/shard_map/pallas_call | solution.py:113
  58.6 14.5 %all_to_all.48 = f32[32,1,128]{2,1,0:T(1,128)S(1)} all-to-all(f32[32,1,128]{2,1,0:T(1,128)S(1)} %bitcast.22), channel_id=1, replica_groups=mesh['tm'=8,'space'=32] {'space'}, dimensions={0} | all-to-all | bytes 32768 | tf_op jit(solution)/shard_map/all_to_all | solution.py:424
  73.1 1.1 shard_map.71
  74.4 11.1 %all_to_all.49.ends = f32[8,8,128]{2,1,0:T(8,128)S(1)} all-to-all(f32[8,8,128]{2,1,0:T(8,128)S(1)} %get-tuple-element.43), channel_id=1, replica_groups=mesh['tm'=8,'space'=32] {'tm'}, dimensions={0} | all-to-all | bytes 65536 | tf_op jit(solution)/shard_map/all_to_all | solution.py:424
  85.6 16.8 %all_to_all.50.ours = f32[32,32,128]{2,1,0:T(8,128)S(1)} all-to-all(f32[32,32,128]{2,1,0:T(8,128)S(1)} %shard_map.72), channel_id=1, replica_groups=mesh['tm'=8,'space'=32] {'space'}, dimensions={0} | all-to-all | bytes 1048576 | tf_op jit(solution)/shard_map/all_to_all | solution.py:424
  102.7 2.0 %collective-permute-start.7 = (f32[5,64,256]{2,1,0:T(8,128)S(1)}, f32[5,64,256]{2,1,0:T(8,128)S(1)}, u32[]{:S(2)}, u32[]{:S(2)}) collective-permute-start(f32[5,64,256]{2,1,0:T(8,128)S(1)} %collective-permute-done.4.rest.refs_0_.moved_first), channel_id=1, source_target_pairs={{1,0},{2,1},{3,2},{4,3},{5,4},{6,5},{7,6},{8,7},{9,8},{10,9},{11,1... | collective-permute-start | bytes 983048 | tf_op jit(solution)/shard_map/ppermute | solution.py:420
  104.8 3.5 %collective-permute-start.6 = (f32[5,64,256]{2,1,0:T(8,128)S(1)}, f32[5,64,256]{2,1,0:T(8,128)S(1)}, u32[]{:S(2)}, u32[]{:S(2)}) collective-permute-start(f32[5,64,256]{2,1,0:T(8,128)S(1)} %collective-permute-done.4.rest.refs_0_.moved_first), channel_id=1, source_target_pairs={{0,1},{1,2},{2,3},{3,4},{4,5},{5,6},{6,7},{7,8},{8,9},{9,10},{10,1... | collective-permute-start | bytes 983048 | tf_op jit(solution)/shard_map/ppermute | solution.py:420
  108.3 10.1 %shard_map.73 = (f32[64,128]{1,0:T(8,128)S(1)}, f32[8,128]{1,0:T(8,128)S(1)}, f32[16,16,128]{2,1,0:T(8,128)S(1)}, f32[16,128]{1,0:T(8,128)S(1)}) custom-call(s32[2]{0:T(128)S(1)} %pad_add_fusion.where, f32[8,128]{1,0:T(8,128)S(1)} %bitcast.17, f32[5,16,16,128]{3,2,1,0:T(8,128)S(1)} %get-tuple-element.33.static, f32[16,16,128]{2,1,0:T(8,128)S(1)} %get-tuple-element.34.begin, ...), custom_call_target="tpu_custom_call" | custom-call | flops 67108864 | bytes 1048576 | tf_op jit(solution)/shard_map/pallas_call | solution.py:113
  118.4 4.7 %shard_map.74 = (f32[9,5,64,256]{3,2,1,0:T(8,128)S(1)}, f32[32,128]{1,0:T(8,128)S(1)}) custom-call(s32[2]{0:T(128)S(1)} %pad_add_fusion.where, f32[64,128]{1,0:T(8,128)S(1)} %get-tuple-element.47.planes, f32[4,4,64,256]{3,2,1,0:T(8,128)S(1)} %copy-done, f32[10,64,256]{2,1,0:T(8,128)S(1)} %collective-permute-done.1.up, ...), custom_call_target="tpu_custom_call" | custom-call | tf_op jit(solution)/shard_map/pallas_call | solution.py:113
  123.1 12.1 %all_to_all.51 = f32[32,1,128]{2,1,0:T(1,128)S(1)} all-to-all(f32[32,1,128]{2,1,0:T(1,128)S(1)} %bitcast.21), channel_id=1, replica_groups=mesh['tm'=8,'space'=32] {'space'}, dimensions={0} | all-to-all | bytes 32768 | tf_op jit(solution)/shard_map/all_to_all | solution.py:424
  135.2 1.1 shard_map.75
  136.4 1.3 collective-permute-start.8
  137.7 10.3 %all_to_all.52.ends = f32[8,8,128]{2,1,0:T(8,128)S(1)} all-to-all(f32[8,8,128]{2,1,0:T(8,128)S(1)} %get-tuple-element.52), channel_id=1, replica_groups=mesh['tm'=8,'space'=32] {'tm'}, dimensions={0} | all-to-all | bytes 65536 | tf_op jit(solution)/shard_map/all_to_all | solution.py:424
  148.0 16.8 %all_to_all.53.ours = f32[32,32,128]{2,1,0:T(8,128)S(1)} all-to-all(f32[32,32,128]{2,1,0:T(8,128)S(1)} %shard_map.76), channel_id=1, replica_groups=mesh['tm'=8,'space'=32] {'space'}, dimensions={0} | all-to-all | bytes 1048576 | tf_op jit(solution)/shard_map/all_to_all | solution.py:424
  165.2 1.5 collective-permute-done.9.theirs
  166.7 9.8 %shard_map.77 = f32[4,64,256]{2,1,0:T(8,128)} custom-call(s32[2]{0:T(128)S(1)} %pad_add_fusion.where, f32[8,128]{1,0:T(8,128)S(1)} %bitcast.18, f32[5,16,16,128]{3,2,1,0:T(8,128)S(1)} %get-tuple-element.33.static, f32[16,16,128]{2,1,0:T(8,128)S(1)} %get-tuple-element.45.begin, f32[16,128]{1,0:T(8,128)S(1)} %get-tuple-element.46.kept, ...), custom_call_target="tpu_custom_call" | custom-call | flops 67108864 | bytes 1048576 | tf_op jit(solution)/shard_map/pallas_call | solution.py:113
  (19 shorter events, 1.7 us)
Async XLA Ops:
  0.6 8.7 %collective-permute-start = (f32[2,3]{1,0:T(2,128)}, f32[2,3]{1,0:T(2,128)S(1)}, u32[]{:S(2)}, u32[]{:S(2)}) collective-permute-start(f32[2,3]{1,0:T(2,128)} %bitcast.24), channel_id=1, source_target_pairs={{0,0},{8,8},{16,16},{24,24},{32,1},{40,9},{48,17},{56,25},{64,2},{... | collective-permute-start | bytes 80 | tf_op jit(solution)/shard_map/ppermute | solution.py:446
  9.4 0.6 copy-start.1
  14.9 39.0 %copy-start = (f32[4,4,64,256]{3,2,1,0:T(8,128)S(1)}, f32[4,4,64,256]{3,2,1,0:T(8,128)}, u32[]{:S(2)}) copy-start(f32[4,4,64,256]{3,2,1,0:T(8,128)} %get-tuple-element.36.own) | copy-start | bytes 3145732
  37.3 16.6 %collective-permute-start.2 = (f32[13,64,256]{2,1,0:T(8,128)}, f32[13,64,256]{2,1,0:T(8,128)S(1)}, u32[]{:S(2)}, u32[]{:S(2)}) collective-permute-start(f32[13,64,256]{2,1,0:T(8,128)} %get-tuple-element.38), channel_id=1, source_target_pairs={{1,0},{2,1},{3,2},{4,3},{5,4},{6,5},{7,6},{8,7},{9,8},{10,9},{11,1... | collective-permute-start | bytes 2555912 | tf_op jit(solution)/shard_map/ppermute | solution.py:420
  39.7 14.2 %collective-permute-start.1 = (f32[10,64,256]{2,1,0:T(8,128)}, f32[10,64,256]{2,1,0:T(8,128)S(1)}, u32[]{:S(2)}, u32[]{:S(2)}) collective-permute-start(f32[10,64,256]{2,1,0:T(8,128)} %get-tuple-element.37), channel_id=1, source_target_pairs={{0,1},{1,2},{2,3},{3,4},{4,5},{5,6},{6,7},{7,8},{8,9},{9,10},{10,1... | collective-permute-start | bytes 1966088 | tf_op jit(solution)/shard_map/ppermute | solution.py:420
  42.9 11.0 %collective-permute-start.3 = (f32[1,64,256]{2,1,0:T(8,128)}, f32[1,64,256]{2,1,0:T(8,128)S(1)}, u32[]{:S(2)}, u32[]{:S(2)}) collective-permute-start(f32[1,64,256]{2,1,0:T(8,128)} %get-tuple-element.39), channel_id=1, source_target_pairs={{2,0},{3,1},{4,2},{5,3},{6,4},{7,5},{8,6},{9,7},{10,8},{11,9},{12,... | collective-permute-start | bytes 196616 | tf_op jit(solution)/shard_map/ppermute | solution.py:420
  74.3 11.2 %collective-permute-start.4 = (f32[5,64,256]{2,1,0:T(8,128)S(1)}, f32[5,64,256]{2,1,0:T(8,128)S(1)}, u32[]{:S(2)}, u32[]{:S(2)}) collective-permute-start(f32[5,64,256]{2,1,0:T(8,128)S(1)} %get-tuple-element.44), channel_id=1, source_target_pairs={{0,32},{32,64},{64,96},{96,128},{128,160},{160,192},{192,224},{224... | collective-permute-start | bytes 983048 | tf_op jit(solution)/shard_map/ppermute | solution.py:420
  102.3 6.0 %collective-permute-start.5 = (f32[32,32,128]{2,1,0:T(8,128)S(1)}, f32[32,32,128]{2,1,0:T(8,128)S(1)}, u32[]{:S(2)}, u32[]{:S(2)}) collective-permute-start(f32[32,32,128]{2,1,0:T(8,128)S(1)} %all_to_all.50.ours), channel_id=1, source_target_pairs={{0,1},{1,0},{2,3},{3,2},{4,5},{5,4},{6,7},{7,6},{8,9},{9,8},{10,11... | collective-permute-start | bytes 1572872 | tf_op jit(solution)/shard_map/ppermute | solution.py:431
  102.7 15.7 %collective-permute-start.7 = (f32[5,64,256]{2,1,0:T(8,128)S(1)}, f32[5,64,256]{2,1,0:T(8,128)S(1)}, u32[]{:S(2)}, u32[]{:S(2)}) collective-permute-start(f32[5,64,256]{2,1,0:T(8,128)S(1)} %collective-permute-done.4.rest.refs_0_.moved_first), channel_id=1, source_target_pairs={{1,0},{2,1},{3,2},{4,3},{5,4},{6,5},{7,6},{8,7},{9,8},{10,9},{11,1... | collective-permute-start | bytes 983048 | tf_op jit(solution)/shard_map/ppermute | solution.py:420
  104.8 13.7 %collective-permute-start.6 = (f32[5,64,256]{2,1,0:T(8,128)S(1)}, f32[5,64,256]{2,1,0:T(8,128)S(1)}, u32[]{:S(2)}, u32[]{:S(2)}) collective-permute-start(f32[5,64,256]{2,1,0:T(8,128)S(1)} %collective-permute-done.4.rest.refs_0_.moved_first), channel_id=1, source_target_pairs={{0,1},{1,2},{2,3},{3,4},{4,5},{5,6},{6,7},{7,8},{8,9},{9,10},{10,1... | collective-permute-start | bytes 983048 | tf_op jit(solution)/shard_map/ppermute | solution.py:420
  136.4 11.6 %collective-permute-start.8 = (f32[5,64,256]{2,1,0:T(8,128)S(1)}, f32[5,64,256]{2,1,0:T(8,128)S(1)}, u32[]{:S(2)}, u32[]{:S(2)}) collective-permute-start(f32[5,64,256]{2,1,0:T(8,128)S(1)} %get-tuple-element.51), channel_id=1, source_target_pairs={{0,32},{32,64},{64,96},{96,128},{128,160},{160,192},{192,224},{1,3... | collective-permute-start | bytes 983048 | tf_op jit(solution)/shard_map/ppermute | solution.py:420
  164.8 1.9 %collective-permute-start.9 = (f32[32,32,128]{2,1,0:T(8,128)S(1)}, f32[32,32,128]{2,1,0:T(8,128)S(1)}, u32[]{:S(2)}, u32[]{:S(2)}) collective-permute-start(f32[32,32,128]{2,1,0:T(8,128)S(1)} %all_to_all.53.ours), channel_id=1, source_target_pairs={{0,1},{1,0},{2,3},{3,2},{4,5},{5,4},{6,7},{7,6},{8,9},{9,8},{10,11... | collective-permute-start | bytes 1572872 | tf_op jit(solution)/shard_map/ppermute | solution.py:431

commit v7 on v6

--- a/solution.py
+++ b/solution.py
@@ -424,11 +424,12 @@
     return lax.all_to_all(x, axis, split_axis=0, concat_axis=0, tiled=True)
 
 
-def everywhere(ends, rest):
+def everywhere(ends, rest, halos=()):
     (packed,) = call(spread_kernel, ((32, 32, 128),), (exchange(ends, "tm"), rest), far=(1,))
     half = exchange(packed, "space")
+    half, *halos = lax.optimization_barrier((half, *halos))
     places = lax.axis_size("space")
-    return half, lax.ppermute(half, "space", [(i, i ^ 1) for i in range(places)])
+    return half, lax.ppermute(half, "space", [(i, i ^ 1) for i in range(places)]), *halos
 
 
 def body(labels, conductivity, coil_pattern, currents, initial_state):
@@ -457,7 +458,6 @@
     )
     whole = exchange(packed, "space")
     table = whole[:8, 40, :]
-    up, down, far, whole = lax.optimization_barrier((up, down, far, whole))
     up, down = shifted(up, "space", 1, False), shifted(down, "space", -1, False)
     far = shifted(far, "space", -2, False)
     static, planes, advanced, state = call(
@@ -484,15 +484,16 @@
 
     _, moved, ends = fine(True, planes, advanced, (far,))
     moved_first = shifted(moved, "tm", 1, True)
+    around = (shifted(moved_first, "space", 1, False), shifted(moved_first, "space", -1, False))
+    ours, theirs, *around = everywhere(ends, moved_first, around)
     planes, advanced, state, kept = call(
         next_sweep_kernel,
         ((64, 128), (8, 128), field, (16, 128)),
-        (where, table, static, state, planes, *everywhere(ends, moved_first)),
+        (where, table, static, state, planes, ours, theirs),
         small=(0, 1),
         scratch=((8, *field),),
         flops=1 << 26,
     )
-    around = (shifted(moved_first, "space", 1, False), shifted(moved_first, "space", -1, False))
     fine_state, moved, ends = fine(False, planes, advanced, (moved_first, *around))
     moved_other = shifted(moved, "tm", 1, False)
     (start,) = call(

time: 177 us -> 178 us (level)
  blocking collectives: 104 us -> 66.1 us
  waiting for transfers between devices: 7.74 us -> 25.1 us
  starting transfers between devices: 17.1 us -> 32.3 us
  local copies, waits for them, and re-layouts: 0.57 us -> 5.54 us
    all_to_all x7 -> x5, blocking collectives: 104 us -> 66.1 us  [exchange(): return lax.all_to_all(x, axis, split_axis=0, concat_axis=0, tiled=True)]
    all_to_all x0 -> x2, starting transfers between devices: none -> 15.3 us  [exchange(): return lax.all_to_all(x, axis, split_axis=0, concat_axis=0, tiled=True)]
    all_to_all x0 -> x2, waiting for transfers between devices: none -> 9.53 us  [exchange(): return lax.all_to_all(x, axis, split_axis=0, concat_axis=0, tiled=True)]
    ppermute x7, waiting for transfers between devices: 0.02 us -> 5.98 us  [shifted(): return lax.ppermute(x, axis, pairs)]
    unnamed x4 -> x16, local copies, waits for them, and re-layouts: 0.57 us -> 5.54 us
    ppermute x2, waiting for transfers between devices: 1.54 us -> 3.44 us  [everywhere(): lax.ppermute(half, 'space', [(i, i ^ 1) for i in range(places)])]
  transfers between devices with their start and end apart: 10 -> 12, of which waited for: 2 -> 5; matrix products, arithmetic and copies ran while one was open for 0% -> 0% of each run, Pallas kernels for 11% -> 5%
where the time goes in v7:
time: 178 us; the launch traced here: 177 us
  blocking collectives  66.1 us (37%)
  Pallas kernels  47.2 us (27%)
  starting transfers between devices  32.3 us (18%)
  waiting for transfers between devices  25.1 us (14%)
  local copies, waits for them, and re-layouts  5.54 us (3%)
    all_to_all x5, blocking collectives, exchange(): return lax.all_to_all(x, axis, split_axis=0, concat_axis=0, tiled=True)  66.1 us
    pallas_call x10, Pallas kernels, call(): pl.pallas_call(body, out_shape=tuple((jax.ShapeDtypeStruct(s, F32) for s...  47.2 us
    all_to_all x2, starting transfers between devices, exchange(): return lax.all_to_all(x, axis, split_axis=0, concat_axis=0, tiled=True)  15.3 us
    ppermute x7, starting transfers between devices, shifted(): return lax.ppermute(x, axis, pairs)  14.1 us
    all_to_all x2, waiting for transfers between devices, exchange(): return lax.all_to_all(x, axis, split_axis=0, concat_axis=0, tiled=True)  9.53 us
    ppermute x1, waiting for transfers between devices, body(): theirs = lax.ppermute(currents[0], ('tm', 'space'), pairs)  6.18 us
    ppermute x7, waiting for transfers between devices, shifted(): return lax.ppermute(x, axis, pairs)  5.98 us
    unnamed x16, local copies, waits for them, and re-layouts  5.54 us
  transfers between devices with their start and end apart: 12, of which 5 were waited for; matrix products, arithmetic and copies ran while one was open for 0% of the time, Pallas kernels for 5%

profile of v7, /device:TPU:225, one launch (start us, length us, event | category | flops | bytes accessed | tf_op | source)
XLA Modules:
  0.0 177.2 jit_solution(15038845980591608574)
XLA Ops:
  0.6 2.6 %collective-permute-start = (f32[2,3]{1,0:T(2,128)}, f32[2,3]{1,0:T(2,128)S(1)}, u32[]{:S(2)}, u32[]{:S(2)}) collective-permute-start(f32[2,3]{1,0:T(2,128)} %bitcast.24), channel_id=1, source_target_pairs={{0,0},{8,8},{16,16},{24,24},{32,1},{40,9},{48,17},{56,25},{64,2},{... | collective-permute-start | bytes 80 | tf_op jit(solution)/shard_map/ppermute | solution.py:447
  3.2 6.2 %collective-permute-done.theirs = f32[2,3]{1,0:T(2,128)S(1)} collective-permute-done((f32[2,3]{1,0:T(2,128)}, f32[2,3]{1,0:T(2,128)S(1)}, u32[]{:S(2)}, u32[]{:S(2)}) %collective-permute-start) | collective-permute-done | bytes 56 | tf_op jit(solution)/shard_map/ppermute | solution.py:447
  9.9 5.0 %shard_map.68 = (f32[4,4,64,256]{3,2,1,0:T(8,128)}, f32[10,64,256]{2,1,0:T(8,128)}, f32[13,64,256]{2,1,0:T(8,128)}, f32[1,64,256]{2,1,0:T(8,128)}, f32[32,48,128]{2,1,0:T(8,128)}) custom-call(f32[4]{0:T(128)} %cond.1, f32[2,3]{1,0:T(2,128)} %bitcast.25, f32[2,3]{1,0:T(2,128)} %copy-done.7, s32[4,64,256]{2,1,0:T(8,128)} %labels_far.1, ...), custom_call_target="tpu_custom_call" | custom-call | tf_op jit(solution)/shard_map/pallas_call | solution.py:113
  14.9 2.4 %collective-permute-start.2 = (f32[13,64,256]{2,1,0:T(8,128)}, f32[13,64,256]{2,1,0:T(8,128)S(1)}, u32[]{:S(2)}, u32[]{:S(2)}) collective-permute-start(f32[13,64,256]{2,1,0:T(8,128)} %get-tuple-element.33), channel_id=1, source_target_pairs={{1,0},{2,1},{3,2},{4,3},{5,4},{6,5},{7,6},{8,7},{9,8},{10,9},{11,1... | collective-permute-start | bytes 2555912 | tf_op jit(solution)/shard_map/ppermute | solution.py:420
  17.3 9.5 %all-to-all-start = ((f32[32,48,128]{2,1,0:T(8,128)}), f32[32,48,128]{2,1,0:T(8,128)S(1)}, u32[]{:S(2)}, u32[]{:S(2)}) async-start(f32[32,48,128]{2,1,0:T(8,128)} %get-tuple-element.27), calls=%async_computation | async-start | bytes 1572864 | tf_op jit(solution)/shard_map/all_to_all | solution.py:424
  26.8 3.5 %collective-permute-start.1 = (f32[10,64,256]{2,1,0:T(8,128)}, f32[10,64,256]{2,1,0:T(8,128)}, u32[]{:S(2)}, u32[]{:S(2)}) collective-permute-start(f32[10,64,256]{2,1,0:T(8,128)} %get-tuple-element.32), channel_id=1, source_target_pairs={{0,1},{1,2},{2,3},{3,4},{4,5},{5,6},{6,7},{7,8},{8,9},{9,10},{10,1... | collective-permute-start | bytes 1966088 | tf_op jit(solution)/shard_map/ppermute | solution.py:420
  30.4 1.3 collective-permute-start.3
  31.8 9.5 %all-to-all-done.whole = f32[32,48,128]{2,1,0:T(8,128)S(1)} async-done(((f32[32,48,128]{2,1,0:T(8,128)}), f32[32,48,128]{2,1,0:T(8,128)S(1)}, u32[]{:S(2)}, u32[]{:S(2)}) %all-to-all-start) | async-done | bytes 786464 | tf_op jit(solution)/shard_map/all_to_all | solution.py:424
  41.3 9.6 %shard_map.69 = (f32[5,16,16,128]{3,2,1,0:T(8,128)S(1)}, f32[64,128]{1,0:T(8,128)S(1)}, f32[8,128]{1,0:T(8,128)S(1)}, f32[16,16,128]{2,1,0:T(8,128)S(1)}) custom-call(s32[2]{0:T(128)S(1)} %pad_add_fusion.where, f32[8,128]{1,0:T(8,128)S(1)} %bitcast.16, f32[32,48,128]{2,1,0:T(8,128)S(1)} %all-to-all-done.whole), custom_call_target="tpu_custom_call" | custom-call | flops 67108864 | bytes 1048576 | tf_op jit(solution)/shard_map/pallas_call | solution.py:113
  51.6 4.9 %shard_map.70 = (f32[9,5,64,256]{3,2,1,0:T(8,128)S(1)}, f32[32,128]{1,0:T(8,128)S(1)}) custom-call(s32[2]{0:T(128)S(1)} %pad_add_fusion.where, f32[64,128]{1,0:T(8,128)S(1)} %get-tuple-element.30.planes.old, f32[4,4,64,256]{3,2,1,0:T(8,128)S(1)} %copy-done, f32[10,64,256]{2,1,0:T(8,128)} %collective-permute-done.1.up, ...), custom_call_target="tpu_custom_call" | custom-call | tf_op jit(solution)/shard_map/pallas_call | solution.py:113
  56.5 13.0 %all_to_all.47 = f32[32,1,128]{2,1,0:T(1,128)S(1)} all-to-all(f32[32,1,128]{2,1,0:T(1,128)S(1)} %bitcast.22), channel_id=1, replica_groups=mesh['tm'=8,'space'=32] {'space'}, dimensions={0} | all-to-all | bytes 32768 | tf_op jit(solution)/shard_map/all_to_all | solution.py:424
  70.6 11.2 %all_to_all.48.ends = f32[8,8,128]{2,1,0:T(8,128)S(1)} all-to-all(f32[8,8,128]{2,1,0:T(8,128)S(1)} %get-tuple-element.38), channel_id=1, replica_groups=mesh['tm'=8,'space'=32] {'tm'}, dimensions={0} | all-to-all | bytes 65536 | tf_op jit(solution)/shard_map/all_to_all | solution.py:424
  82.7 5.8 %all-to-all-start.3 = ((f32[32,32,128]{2,1,0:T(8,128)}), f32[32,32,128]{2,1,0:T(8,128)S(1)}, u32[]{:S(2)}, u32[]{:S(2)}) async-start(f32[32,32,128]{2,1,0:T(8,128)} %shard_map.72), calls=%async_computation.3 | async-start | bytes 1048576 | tf_op jit(solution)/shard_map/all_to_all | solution.py:424
  88.5 2.3 %collective-permute-start.6 = (f32[5,64,256]{2,1,0:T(8,128)S(1)}, f32[5,64,256]{2,1,0:T(8,128)S(1)}, u32[]{:S(2)}, u32[]{:S(2)}) collective-permute-start(f32[5,64,256]{2,1,0:T(8,128)S(1)} %collective-permute-done.4.rest.refs_0_.moved_first), channel_id=1, source_target_pairs={{1,0},{2,1},{3,2},{4,3},{5,4},{6,5},{7,6},{8,7},{9,8},{10,9},{11,1... | collective-permute-start | bytes 983048 | tf_op jit(solution)/shard_map/ppermute | solution.py:420
  90.8 3.3 %collective-permute-start.5 = (f32[5,64,256]{2,1,0:T(8,128)S(1)}, f32[5,64,256]{2,1,0:T(8,128)S(1)}, u32[]{:S(2)}, u32[]{:S(2)}) collective-permute-start(f32[5,64,256]{2,1,0:T(8,128)S(1)} %collective-permute-done.4.rest.refs_0_.moved_first), channel_id=1, source_target_pairs={{0,1},{1,2},{2,3},{3,4},{4,5},{5,6},{6,7},{7,8},{8,9},{9,10},{10,1... | collective-permute-start | bytes 983048 | tf_op jit(solution)/shard_map/ppermute | solution.py:420
  94.1 6.0 %collective-permute-done.6.refs_2_ = f32[5,64,256]{2,1,0:T(8,128)S(1)} collective-permute-done((f32[5,64,256]{2,1,0:T(8,128)S(1)}, f32[5,64,256]{2,1,0:T(8,128)S(1)}, u32[]{:S(2)}, u32[]{:S(2)}) %collective-permute-start.6) | collective-permute-done | bytes 327712 | tf_op jit(solution)/shard_map/ppermute | solution.py:420
  101.6 1.9 %collective-permute-done.7.theirs = f32[32,32,128]{2,1,0:T(8,128)S(1)} collective-permute-done((f32[32,32,128]{2,1,0:T(8,128)S(1)}, f32[32,32,128]{2,1,0:T(8,128)S(1)}, u32[]{:S(2)}, u32[]{:S(2)}) %collective-permute-start.7) | collective-permute-done | bytes 524320 | tf_op jit(solution)/shard_map/ppermute | solution.py:432
  104.4 10.1 %shard_map.73 = (f32[64,128]{1,0:T(8,128)S(1)}, f32[8,128]{1,0:T(8,128)S(1)}, f32[16,16,128]{2,1,0:T(8,128)S(1)}, f32[16,128]{1,0:T(8,128)S(1)}) custom-call(s32[2]{0:T(128)S(1)} %pad_add_fusion.where, f32[8,128]{1,0:T(8,128)S(1)} %bitcast.17, f32[5,16,16,128]{3,2,1,0:T(8,128)S(1)} %get-tuple-element.28.static, f32[16,16,128]{2,1,0:T(8,128)S(1)} %copy-done.6, ...), custom_call_target="tpu_custom_call" | custom-call | flops 67108864 | bytes 1048576 | tf_op jit(solution)/shard_map/pallas_call | solution.py:113
  116.4 4.9 %shard_map.74 = (f32[9,5,64,256]{3,2,1,0:T(8,128)S(1)}, f32[32,128]{1,0:T(8,128)S(1)}) custom-call(s32[2]{0:T(128)S(1)} %pad_add_fusion.where, f32[64,128]{1,0:T(8,128)S(1)} %get-tuple-element.43.planes, f32[4,4,64,256]{3,2,1,0:T(8,128)S(1)} %copy-done, f32[10,64,256]{2,1,0:T(8,128)} %collective-permute-done.1.up, ...), custom_call_target="tpu_custom_call" | custom-call | tf_op jit(solution)/shard_map/pallas_call | solution.py:113
  121.3 14.4 %all_to_all.49 = f32[32,1,128]{2,1,0:T(1,128)S(1)} all-to-all(f32[32,1,128]{2,1,0:T(1,128)S(1)} %bitcast.21), channel_id=1, replica_groups=mesh['tm'=8,'space'=32] {'space'}, dimensions={0} | all-to-all | bytes 32768 | tf_op jit(solution)/shard_map/all_to_all | solution.py:424
  138.0 10.7 %all_to_all.50.ends = f32[8,8,128]{2,1,0:T(8,128)S(1)} all-to-all(f32[8,8,128]{2,1,0:T(8,128)S(1)} %get-tuple-element.50), channel_id=1, replica_groups=mesh['tm'=8,'space'=32] {'tm'}, dimensions={0} | all-to-all | bytes 65536 | tf_op jit(solution)/shard_map/all_to_all | solution.py:424
  148.8 16.8 %all_to_all.51.ours = f32[32,32,128]{2,1,0:T(8,128)S(1)} all-to-all(f32[32,32,128]{2,1,0:T(8,128)S(1)} %shard_map.76), channel_id=1, replica_groups=mesh['tm'=8,'space'=32] {'space'}, dimensions={0} | all-to-all | bytes 1048576 | tf_op jit(solution)/shard_map/all_to_all | solution.py:424
  166.0 1.5 collective-permute-done.9.theirs
  167.5 9.7 %shard_map.77 = f32[4,64,256]{2,1,0:T(8,128)} custom-call(s32[2]{0:T(128)S(1)} %pad_add_fusion.where, f32[8,128]{1,0:T(8,128)S(1)} %bitcast.18, f32[5,16,16,128]{3,2,1,0:T(8,128)S(1)} %get-tuple-element.28.static, f32[16,16,128]{2,1,0:T(8,128)S(1)} %get-tuple-element.41.begin, f32[16,128]{1,0:T(8,128)S(1)} %get-tuple-element.42.kept, ...), custom_call_target="tpu_custom_call" | custom-call | flops 67108864 | bytes 1048576 | tf_op jit(solution)/shard_map/pallas_call | solution.py:113
  (33 shorter events, 10.4 us)
Async XLA Ops:
  0.6 8.7 %collective-permute-start = (f32[2,3]{1,0:T(2,128)}, f32[2,3]{1,0:T(2,128)S(1)}, u32[]{:S(2)}, u32[]{:S(2)}) collective-permute-start(f32[2,3]{1,0:T(2,128)} %bitcast.24), channel_id=1, source_target_pairs={{0,0},{8,8},{16,16},{24,24},{32,1},{40,9},{48,17},{56,25},{64,2},{... | collective-permute-start | bytes 80 | tf_op jit(solution)/shard_map/ppermute | solution.py:447
  9.4 0.6 copy-start.7
  14.9 36.6 %copy-start = (f32[4,4,64,256]{3,2,1,0:T(8,128)S(1)}, f32[4,4,64,256]{3,2,1,0:T(8,128)}, u32[]{:S(2)}) copy-start(f32[4,4,64,256]{3,2,1,0:T(8,128)} %get-tuple-element.31.own) | copy-start | bytes 3145732
  14.9 36.6 %collective-permute-start.2 = (f32[13,64,256]{2,1,0:T(8,128)}, f32[13,64,256]{2,1,0:T(8,128)S(1)}, u32[]{:S(2)}, u32[]{:S(2)}) collective-permute-start(f32[13,64,256]{2,1,0:T(8,128)} %get-tuple-element.33), channel_id=1, source_target_pairs={{1,0},{2,1},{3,2},{4,3},{5,4},{6,5},{7,6},{8,7},{9,8},{10,9},{11,1... | collective-permute-start | bytes 2555912 | tf_op jit(solution)/shard_map/ppermute | solution.py:420
  17.3 24.0 %all-to-all-start = ((f32[32,48,128]{2,1,0:T(8,128)}), f32[32,48,128]{2,1,0:T(8,128)S(1)}, u32[]{:S(2)}, u32[]{:S(2)}) async-start(f32[32,48,128]{2,1,0:T(8,128)} %get-tuple-element.27), calls=%async_computation | async-start | bytes 1572864 | tf_op jit(solution)/shard_map/all_to_all | solution.py:424
  26.8 24.7 %collective-permute-start.1 = (f32[10,64,256]{2,1,0:T(8,128)}, f32[10,64,256]{2,1,0:T(8,128)}, u32[]{:S(2)}, u32[]{:S(2)}) collective-permute-start(f32[10,64,256]{2,1,0:T(8,128)} %get-tuple-element.32), channel_id=1, source_target_pairs={{0,1},{1,2},{2,3},{3,4},{4,5},{5,6},{6,7},{7,8},{8,9},{9,10},{10,1... | collective-permute-start | bytes 1966088 | tf_op jit(solution)/shard_map/ppermute | solution.py:420
  30.4 21.2 %collective-permute-start.3 = (f32[1,64,256]{2,1,0:T(8,128)}, f32[1,64,256]{2,1,0:T(8,128)S(1)}, u32[]{:S(2)}, u32[]{:S(2)}) collective-permute-start(f32[1,64,256]{2,1,0:T(8,128)} %get-tuple-element.34), channel_id=1, source_target_pairs={{2,0},{3,1},{4,2},{5,3},{6,4},{7,5},{8,6},{9,7},{10,8},{11,9},{12,... | collective-permute-start | bytes 196616 | tf_op jit(solution)/shard_map/ppermute | solution.py:420
  50.9 0.7 copy-start.5
  70.6 11.2 %collective-permute-start.4 = (f32[5,64,256]{2,1,0:T(8,128)S(1)}, f32[5,64,256]{2,1,0:T(8,128)S(1)}, u32[]{:S(2)}, u32[]{:S(2)}) collective-permute-start(f32[5,64,256]{2,1,0:T(8,128)S(1)} %get-tuple-element.39), channel_id=1, source_target_pairs={{0,32},{32,64},{64,96},{96,128},{128,160},{160,192},{192,224},{224... | collective-permute-start | bytes 983048 | tf_op jit(solution)/shard_map/ppermute | solution.py:420
  82.7 18.9 %all-to-all-start.3 = ((f32[32,32,128]{2,1,0:T(8,128)}), f32[32,32,128]{2,1,0:T(8,128)S(1)}, u32[]{:S(2)}, u32[]{:S(2)}) async-start(f32[32,32,128]{2,1,0:T(8,128)} %shard_map.72), calls=%async_computation.3 | async-start | bytes 1048576 | tf_op jit(solution)/shard_map/all_to_all | solution.py:424
  88.5 11.5 %collective-permute-start.6 = (f32[5,64,256]{2,1,0:T(8,128)S(1)}, f32[5,64,256]{2,1,0:T(8,128)S(1)}, u32[]{:S(2)}, u32[]{:S(2)}) collective-permute-start(f32[5,64,256]{2,1,0:T(8,128)S(1)} %collective-permute-done.4.rest.refs_0_.moved_first), channel_id=1, source_target_pairs={{1,0},{2,1},{3,2},{4,3},{5,4},{6,5},{7,6},{8,7},{9,8},{10,9},{11,1... | collective-permute-start | bytes 983048 | tf_op jit(solution)/shard_map/ppermute | solution.py:420
  90.8 10.0 %collective-permute-start.5 = (f32[5,64,256]{2,1,0:T(8,128)S(1)}, f32[5,64,256]{2,1,0:T(8,128)S(1)}, u32[]{:S(2)}, u32[]{:S(2)}) collective-permute-start(f32[5,64,256]{2,1,0:T(8,128)S(1)} %collective-permute-done.4.rest.refs_0_.moved_first), channel_id=1, source_target_pairs={{0,1},{1,2},{2,3},{3,4},{4,5},{5,6},{6,7},{7,8},{8,9},{9,10},{10,1... | collective-permute-start | bytes 983048 | tf_op jit(solution)/shard_map/ppermute | solution.py:420
  100.1 0.7 copy-start.1
  100.8 0.7 copy-start.3
  101.6 1.9 %collective-permute-start.7 = (f32[32,32,128]{2,1,0:T(8,128)S(1)}, f32[32,32,128]{2,1,0:T(8,128)S(1)}, u32[]{:S(2)}, u32[]{:S(2)}) collective-permute-start(f32[32,32,128]{2,1,0:T(8,128)S(1)} %all-to-all-done.3.ours), channel_id=1, source_target_pairs={{0,1},{1,0},{2,3},{3,2},{4,5},{5,4},{6,7},{7,6},{8,9},{9,8},{10,11... | collective-permute-start | bytes 1572872 | tf_op jit(solution)/shard_map/ppermute | solution.py:432
  103.5 0.9 copy-start.6
  114.4 1.0 copy-start.2
  115.4 1.0 copy-start.4
  136.8 12.0 %collective-permute-start.8 = (f32[5,64,256]{2,1,0:T(8,128)S(1)}, f32[5,64,256]{2,1,0:T(8,128)S(1)}, u32[]{:S(2)}, u32[]{:S(2)}) collective-permute-start(f32[5,64,256]{2,1,0:T(8,128)S(1)} %get-tuple-element.49), channel_id=1, source_target_pairs={{0,32},{32,64},{64,96},{96,128},{128,160},{160,192},{192,224},{1,3... | collective-permute-start | bytes 983048 | tf_op jit(solution)/shard_map/ppermute | solution.py:420
  165.6 1.9 %collective-permute-start.9 = (f32[32,32,128]{2,1,0:T(8,128)S(1)}, f32[32,32,128]{2,1,0:T(8,128)S(1)}, u32[]{:S(2)}, u32[]{:S(2)}) collective-permute-start(f32[32,32,128]{2,1,0:T(8,128)S(1)} %all_to_all.51.ours), channel_id=1, source_target_pairs={{0,1},{1,0},{2,3},{3,2},{4,5},{5,4},{6,7},{7,6},{8,9},{9,8},{10,11... | collective-permute-start | bytes 1572872 | tf_op jit(solution)/shard_map/ppermute | solution.py:432

commit v8 on v6

--- a/solution.py
+++ b/solution.py
@@ -14,6 +14,7 @@
 VMEM = pltpu.MemorySpace.VMEM
 SMEM = pltpu.MemorySpace.SMEM
 INTERPRET = False
+SHIFT = 4.0
 LIMIT = 12 << 20
 
 
@@ -332,14 +333,14 @@
     for plane in range(-3, 8):
         r[plane + 3] = guarded(source(0, plane) + spread(u, -4, plane), plane, first)
     for plane in range(-2, 7):
-        w[plane + 2] = guarded(weight(plane) * r[plane + 3] - beside(r, -3, plane), plane, first)
+        w[plane + 2] = guarded((weight(plane) + (6.0 - SHIFT)) * r[plane + 3] - beside(r, -3, plane), plane, first)
     for plane in range(-1, 6):
         q[0, plane + 1] = guarded(source(1, plane) + spread(u, -4, plane), plane, first)
         q[1, plane + 1] = guarded(spread(r, -3, plane), plane, first)
         q[2, plane + 1] = guarded(spread(w, -2, plane), plane, first)
     for plane in range(5):
         for k in range(3):
-            image = weight(plane) * q[k, plane + 1] - beside(q.at[k], -1, plane)
+            image = (weight(plane) + (6.0 - SHIFT)) * q[k, plane + 1] - beside(q.at[k], -1, plane)
             a[k, plane] = guarded(image, plane, first)
     sums = [jnp.zeros((8, 128), F32)] * 28
     for plane in range(4):
@@ -377,11 +378,11 @@
 
 
 def weights(norm, cross, square, product):
-    first = cross + 6.0 * norm
+    first = cross + SHIFT * norm
     step = norm / first
-    keep = 1.0 - 6.0 * step
+    keep = 1.0 - SHIFT * step
     new = keep * keep * norm - 2.0 * keep * step * cross + step * step * square
-    second = keep * keep * first - 2.0 * keep * step * (square + 6.0 * cross) + step * step * product
+    second = keep * keep * first - 2.0 * keep * step * (square + SHIFT * cross) + step * step * product
     ratio = new / norm
     second = new / (second - ratio * new / step)
     return step + second * (keep + ratio), -second * step
@@ -457,7 +458,6 @@
     )
     whole = exchange(packed, "space")
     table = whole[:8, 40, :]
-    up, down, far, whole = lax.optimization_barrier((up, down, far, whole))
     up, down = shifted(up, "space", 1, False), shifted(down, "space", -1, False)
     far = shifted(far, "space", -2, False)
     static, planes, advanced, state = call(

time: 177 us -> 173 us (0.977)
  blocking collectives: 104 us -> 80.6 us
  starting transfers between devices: 17.1 us -> 26.9 us
  waiting for transfers between devices: 7.74 us -> 17.3 us
    all_to_all x7 -> x6, blocking collectives: 104 us -> 80.6 us  [exchange(): return lax.all_to_all(x, axis, split_axis=0, concat_axis=0, tiled=True)]
    all_to_all x0 -> x1, waiting for transfers between devices: none -> 9.53 us  [exchange(): return lax.all_to_all(x, axis, split_axis=0, concat_axis=0, tiled=True)]
    all_to_all x0 -> x1, starting transfers between devices: none -> 9.49 us  [exchange(): return lax.all_to_all(x, axis, split_axis=0, concat_axis=0, tiled=True)]
  transfers between devices with their start and end apart: 10 -> 11, of which waited for: 2 -> 3; matrix products, arithmetic and copies ran while one was open for 0% -> 0% of each run, Pallas kernels for 11% -> 11%
where the time goes in v8:
time: 173 us; the launch traced here: 172 us
  blocking collectives  80.6 us (47%)
  Pallas kernels  46 us (27%)
  starting transfers between devices  26.9 us (16%)
  waiting for transfers between devices  17.3 us (10%)
    all_to_all x6, blocking collectives, exchange(): return lax.all_to_all(x, axis, split_axis=0, concat_axis=0, tiled=True)  80.6 us
    pallas_call x10, Pallas kernels, call(): pl.pallas_call(body, out_shape=tuple((jax.ShapeDtypeStruct(s, F32) for s...  46 us
    ppermute x7, starting transfers between devices, shifted(): return lax.ppermute(x, axis, pairs)  14.1 us
    all_to_all x1, waiting for transfers between devices, exchange(): return lax.all_to_all(x, axis, split_axis=0, concat_axis=0, tiled=True)  9.53 us
    all_to_all x1, starting transfers between devices, exchange(): return lax.all_to_all(x, axis, split_axis=0, concat_axis=0, tiled=True)  9.49 us
    ppermute x1, waiting for transfers between devices, body(): theirs = lax.ppermute(currents[0], ('tm', 'space'), pairs)  6.18 us
  transfers between devices with their start and end apart: 11, of which 3 were waited for; matrix products, arithmetic and copies ran while one was open for 0% of the time, Pallas kernels for 11%

profile of v8, /device:TPU:225, one launch (start us, length us, event | category | flops | bytes accessed | tf_op | source)
XLA Modules:
  0.0 172.2 jit_solution(11484530245079625612)
XLA Ops:
  0.6 2.6 %collective-permute-start = (f32[2,3]{1,0:T(2,128)}, f32[2,3]{1,0:T(2,128)S(1)}, u32[]{:S(2)}, u32[]{:S(2)}) collective-permute-start(f32[2,3]{1,0:T(2,128)} %bitcast.24), channel_id=1, source_target_pairs={{0,0},{8,8},{16,16},{24,24},{32,1},{40,9},{48,17},{56,25},{64,2},{... | collective-permute-start | bytes 80 | tf_op jit(solution)/shard_map/ppermute | solution.py:447
  3.2 6.2 %collective-permute-done.theirs = f32[2,3]{1,0:T(2,128)S(1)} collective-permute-done((f32[2,3]{1,0:T(2,128)}, f32[2,3]{1,0:T(2,128)S(1)}, u32[]{:S(2)}, u32[]{:S(2)}) %collective-permute-start) | collective-permute-done | bytes 56 | tf_op jit(solution)/shard_map/ppermute | solution.py:447
  9.9 5.0 %shard_map.68 = (f32[4,4,64,256]{3,2,1,0:T(8,128)}, f32[10,64,256]{2,1,0:T(8,128)}, f32[13,64,256]{2,1,0:T(8,128)}, f32[1,64,256]{2,1,0:T(8,128)}, f32[32,48,128]{2,1,0:T(8,128)}) custom-call(f32[4]{0:T(128)} %cond.1, f32[2,3]{1,0:T(2,128)} %bitcast.25, f32[2,3]{1,0:T(2,128)} %copy-done.1, s32[4,64,256]{2,1,0:T(8,128)} %labels_far.1, ...), custom_call_target="tpu_custom_call" | custom-call | tf_op jit(solution)/shard_map/pallas_call | solution.py:114
  14.9 2.4 %collective-permute-start.2 = (f32[13,64,256]{2,1,0:T(8,128)}, f32[13,64,256]{2,1,0:T(8,128)S(1)}, u32[]{:S(2)}, u32[]{:S(2)}) collective-permute-start(f32[13,64,256]{2,1,0:T(8,128)} %get-tuple-element.30), channel_id=1, source_target_pairs={{1,0},{2,1},{3,2},{4,3},{5,4},{6,5},{7,6},{8,7},{9,8},{10,9},{11,1... | collective-permute-start | bytes 2555912 | tf_op jit(solution)/shard_map/ppermute | solution.py:421
  17.3 9.5 %all-to-all-start = ((f32[32,48,128]{2,1,0:T(8,128)}), f32[32,48,128]{2,1,0:T(8,128)S(1)}, u32[]{:S(2)}, u32[]{:S(2)}) async-start(f32[32,48,128]{2,1,0:T(8,128)} %get-tuple-element.24), calls=%async_computation | async-start | bytes 1572864 | tf_op jit(solution)/shard_map/all_to_all | solution.py:425
  26.8 3.5 %collective-permute-start.1 = (f32[10,64,256]{2,1,0:T(8,128)}, f32[10,64,256]{2,1,0:T(8,128)S(1)}, u32[]{:S(2)}, u32[]{:S(2)}) collective-permute-start(f32[10,64,256]{2,1,0:T(8,128)} %get-tuple-element.29), channel_id=1, source_target_pairs={{0,1},{1,2},{2,3},{3,4},{4,5},{5,6},{6,7},{7,8},{8,9},{9,10},{10,1... | collective-permute-start | bytes 1966088 | tf_op jit(solution)/shard_map/ppermute | solution.py:421
  30.4 1.3 collective-permute-start.3
  31.7 9.5 %all-to-all-done.whole = f32[32,48,128]{2,1,0:T(8,128)S(1)} async-done(((f32[32,48,128]{2,1,0:T(8,128)}), f32[32,48,128]{2,1,0:T(8,128)S(1)}, u32[]{:S(2)}, u32[]{:S(2)}) %all-to-all-start) | async-done | bytes 786464 | tf_op jit(solution)/shard_map/all_to_all | solution.py:425
  41.3 9.6 %shard_map.69 = (f32[5,16,16,128]{3,2,1,0:T(8,128)S(1)}, f32[64,128]{1,0:T(8,128)S(1)}, f32[8,128]{1,0:T(8,128)S(1)}, f32[16,16,128]{2,1,0:T(8,128)S(1)}) custom-call(s32[2]{0:T(128)S(1)} %pad_add_fusion.where, f32[8,128]{1,0:T(8,128)S(1)} %bitcast.16, f32[32,48,128]{2,1,0:T(8,128)S(1)} %all-to-all-done.whole), custom_call_target="tpu_custom_call" | custom-call | flops 67108864 | bytes 1048576 | tf_op jit(solution)/shard_map/pallas_call | solution.py:114
  50.9 4.8 %shard_map.70 = (f32[9,5,64,256]{3,2,1,0:T(8,128)S(1)}, f32[32,128]{1,0:T(8,128)S(1)}) custom-call(s32[2]{0:T(128)S(1)} %pad_add_fusion.where, f32[64,128]{1,0:T(8,128)S(1)} %get-tuple-element.27.planes.old, f32[4,4,64,256]{3,2,1,0:T(8,128)S(1)} %copy-done, f32[10,64,256]{2,1,0:T(8,128)S(1)} %collective-permute-done.1.up, ...), custom_call_target="tpu_custom_call" | custom-call | tf_op jit(solution)/shard_map/pallas_call | solution.py:114
  55.7 13.0 %all_to_all.47 = f32[32,1,128]{2,1,0:T(1,128)S(1)} all-to-all(f32[32,1,128]{2,1,0:T(1,128)S(1)} %bitcast.22), channel_id=1, replica_groups=mesh['tm'=8,'space'=32] {'space'}, dimensions={0} | all-to-all | bytes 32768 | tf_op jit(solution)/shard_map/all_to_all | solution.py:425
  68.7 1.1 shard_map.71
  69.8 11.2 %all_to_all.48.ends = f32[8,8,128]{2,1,0:T(8,128)S(1)} all-to-all(f32[8,8,128]{2,1,0:T(8,128)S(1)} %get-tuple-element.35), channel_id=1, replica_groups=mesh['tm'=8,'space'=32] {'tm'}, dimensions={0} | all-to-all | bytes 65536 | tf_op jit(solution)/shard_map/all_to_all | solution.py:425
  81.1 16.8 %all_to_all.49.ours = f32[32,32,128]{2,1,0:T(8,128)S(1)} all-to-all(f32[32,32,128]{2,1,0:T(8,128)S(1)} %shard_map.72), channel_id=1, replica_groups=mesh['tm'=8,'space'=32] {'space'}, dimensions={0} | all-to-all | bytes 1048576 | tf_op jit(solution)/shard_map/all_to_all | solution.py:425
  98.3 2.0 %collective-permute-start.7 = (f32[5,64,256]{2,1,0:T(8,128)S(1)}, f32[5,64,256]{2,1,0:T(8,128)S(1)}, u32[]{:S(2)}, u32[]{:S(2)}) collective-permute-start(f32[5,64,256]{2,1,0:T(8,128)S(1)} %collective-permute-done.4.rest.refs_0_.moved_first), channel_id=1, source_target_pairs={{1,0},{2,1},{3,2},{4,3},{5,4},{6,5},{7,6},{8,7},{9,8},{10,9},{11,1... | collective-permute-start | bytes 983048 | tf_op jit(solution)/shard_map/ppermute | solution.py:421
  100.3 3.5 %collective-permute-start.6 = (f32[5,64,256]{2,1,0:T(8,128)S(1)}, f32[5,64,256]{2,1,0:T(8,128)S(1)}, u32[]{:S(2)}, u32[]{:S(2)}) collective-permute-start(f32[5,64,256]{2,1,0:T(8,128)S(1)} %collective-permute-done.4.rest.refs_0_.moved_first), channel_id=1, source_target_pairs={{0,1},{1,2},{2,3},{3,4},{4,5},{5,6},{6,7},{7,8},{8,9},{9,10},{10,1... | collective-permute-start | bytes 983048 | tf_op jit(solution)/shard_map/ppermute | solution.py:421
  103.9 10.1 %shard_map.73 = (f32[64,128]{1,0:T(8,128)S(1)}, f32[8,128]{1,0:T(8,128)S(1)}, f32[16,16,128]{2,1,0:T(8,128)S(1)}, f32[16,128]{1,0:T(8,128)S(1)}) custom-call(s32[2]{0:T(128)S(1)} %pad_add_fusion.where, f32[8,128]{1,0:T(8,128)S(1)} %bitcast.17, f32[5,16,16,128]{3,2,1,0:T(8,128)S(1)} %get-tuple-element.25.static, f32[16,16,128]{2,1,0:T(8,128)S(1)} %get-tuple-element.26.begin, ...), custom_call_target="tpu_custom_call" | custom-call | flops 67108864 | bytes 1048576 | tf_op jit(solution)/shard_map/pallas_call | solution.py:114
  114.0 4.5 %shard_map.74 = (f32[9,5,64,256]{3,2,1,0:T(8,128)S(1)}, f32[32,128]{1,0:T(8,128)S(1)}) custom-call(s32[2]{0:T(128)S(1)} %pad_add_fusion.where, f32[64,128]{1,0:T(8,128)S(1)} %get-tuple-element.39.planes, f32[4,4,64,256]{3,2,1,0:T(8,128)S(1)} %copy-done, f32[10,64,256]{2,1,0:T(8,128)S(1)} %collective-permute-done.1.up, ...), custom_call_target="tpu_custom_call" | custom-call | tf_op jit(solution)/shard_map/pallas_call | solution.py:114
  118.5 12.1 %all_to_all.50 = f32[32,1,128]{2,1,0:T(1,128)S(1)} all-to-all(f32[32,1,128]{2,1,0:T(1,128)S(1)} %bitcast.21), channel_id=1, replica_groups=mesh['tm'=8,'space'=32] {'space'}, dimensions={0} | all-to-all | bytes 32768 | tf_op jit(solution)/shard_map/all_to_all | solution.py:425
  131.7 1.3 collective-permute-start.8
  133.0 10.7 %all_to_all.51.ends = f32[8,8,128]{2,1,0:T(8,128)S(1)} all-to-all(f32[8,8,128]{2,1,0:T(8,128)S(1)} %get-tuple-element.44), channel_id=1, replica_groups=mesh['tm'=8,'space'=32] {'tm'}, dimensions={0} | all-to-all | bytes 65536 | tf_op jit(solution)/shard_map/all_to_all | solution.py:425
  143.7 16.8 %all_to_all.52.ours = f32[32,32,128]{2,1,0:T(8,128)S(1)} all-to-all(f32[32,32,128]{2,1,0:T(8,128)S(1)} %shard_map.76), channel_id=1, replica_groups=mesh['tm'=8,'space'=32] {'space'}, dimensions={0} | all-to-all | bytes 1048576 | tf_op jit(solution)/shard_map/all_to_all | solution.py:425
  160.9 1.5 collective-permute-done.9.theirs
  162.4 9.8 %shard_map.77 = f32[4,64,256]{2,1,0:T(8,128)} custom-call(s32[2]{0:T(128)S(1)} %pad_add_fusion.where, f32[8,128]{1,0:T(8,128)S(1)} %bitcast.18, f32[5,16,16,128]{3,2,1,0:T(8,128)S(1)} %get-tuple-element.25.static, f32[16,16,128]{2,1,0:T(8,128)S(1)} %get-tuple-element.37.begin, f32[16,128]{1,0:T(8,128)S(1)} %get-tuple-element.38.kept, ...), custom_call_target="tpu_custom_call" | custom-call | flops 67108864 | bytes 1048576 | tf_op jit(solution)/shard_map/pallas_call | solution.py:114
  (20 shorter events, 2.7 us)
Async XLA Ops:
  0.6 8.7 %collective-permute-start = (f32[2,3]{1,0:T(2,128)}, f32[2,3]{1,0:T(2,128)S(1)}, u32[]{:S(2)}, u32[]{:S(2)}) collective-permute-start(f32[2,3]{1,0:T(2,128)} %bitcast.24), channel_id=1, source_target_pairs={{0,0},{8,8},{16,16},{24,24},{32,1},{40,9},{48,17},{56,25},{64,2},{... | collective-permute-start | bytes 80 | tf_op jit(solution)/shard_map/ppermute | solution.py:447
  9.4 0.6 copy-start.1
  14.9 36.0 %copy-start = (f32[4,4,64,256]{3,2,1,0:T(8,128)S(1)}, f32[4,4,64,256]{3,2,1,0:T(8,128)}, u32[]{:S(2)}) copy-start(f32[4,4,64,256]{3,2,1,0:T(8,128)} %get-tuple-element.28.own) | copy-start | bytes 3145732
  14.9 36.0 %collective-permute-start.2 = (f32[13,64,256]{2,1,0:T(8,128)}, f32[13,64,256]{2,1,0:T(8,128)S(1)}, u32[]{:S(2)}, u32[]{:S(2)}) collective-permute-start(f32[13,64,256]{2,1,0:T(8,128)} %get-tuple-element.30), channel_id=1, source_target_pairs={{1,0},{2,1},{3,2},{4,3},{5,4},{6,5},{7,6},{8,7},{9,8},{10,9},{11,1... | collective-permute-start | bytes 2555912 | tf_op jit(solution)/shard_map/ppermute | solution.py:421
  17.3 24.0 %all-to-all-start = ((f32[32,48,128]{2,1,0:T(8,128)}), f32[32,48,128]{2,1,0:T(8,128)S(1)}, u32[]{:S(2)}, u32[]{:S(2)}) async-start(f32[32,48,128]{2,1,0:T(8,128)} %get-tuple-element.24), calls=%async_computation | async-start | bytes 1572864 | tf_op jit(solution)/shard_map/all_to_all | solution.py:425
  26.8 24.1 %collective-permute-start.1 = (f32[10,64,256]{2,1,0:T(8,128)}, f32[10,64,256]{2,1,0:T(8,128)S(1)}, u32[]{:S(2)}, u32[]{:S(2)}) collective-permute-start(f32[10,64,256]{2,1,0:T(8,128)} %get-tuple-element.29), channel_id=1, source_target_pairs={{0,1},{1,2},{2,3},{3,4},{4,5},{5,6},{6,7},{7,8},{8,9},{9,10},{10,1... | collective-permute-start | bytes 1966088 | tf_op jit(solution)/shard_map/ppermute | solution.py:421
  30.4 20.5 %collective-permute-start.3 = (f32[1,64,256]{2,1,0:T(8,128)}, f32[1,64,256]{2,1,0:T(8,128)S(1)}, u32[]{:S(2)}, u32[]{:S(2)}) collective-permute-start(f32[1,64,256]{2,1,0:T(8,128)} %get-tuple-element.31), channel_id=1, source_target_pairs={{2,0},{3,1},{4,2},{5,3},{6,4},{7,5},{8,6},{9,7},{10,8},{11,9},{12,... | collective-permute-start | bytes 196616 | tf_op jit(solution)/shard_map/ppermute | solution.py:421
  69.8 11.2 %collective-permute-start.4 = (f32[5,64,256]{2,1,0:T(8,128)S(1)}, f32[5,64,256]{2,1,0:T(8,128)S(1)}, u32[]{:S(2)}, u32[]{:S(2)}) collective-permute-start(f32[5,64,256]{2,1,0:T(8,128)S(1)} %get-tuple-element.36), channel_id=1, source_target_pairs={{0,32},{32,64},{64,96},{96,128},{128,160},{160,192},{192,224},{224... | collective-permute-start | bytes 983048 | tf_op jit(solution)/shard_map/ppermute | solution.py:421
  97.9 6.0 %collective-permute-start.5 = (f32[32,32,128]{2,1,0:T(8,128)S(1)}, f32[32,32,128]{2,1,0:T(8,128)S(1)}, u32[]{:S(2)}, u32[]{:S(2)}) collective-permute-start(f32[32,32,128]{2,1,0:T(8,128)S(1)} %all_to_all.49.ours), channel_id=1, source_target_pairs={{0,1},{1,0},{2,3},{3,2},{4,5},{5,4},{6,7},{7,6},{8,9},{9,8},{10,11... | collective-permute-start | bytes 1572872 | tf_op jit(solution)/shard_map/ppermute | solution.py:432
  98.3 15.6 %collective-permute-start.7 = (f32[5,64,256]{2,1,0:T(8,128)S(1)}, f32[5,64,256]{2,1,0:T(8,128)S(1)}, u32[]{:S(2)}, u32[]{:S(2)}) collective-permute-start(f32[5,64,256]{2,1,0:T(8,128)S(1)} %collective-permute-done.4.rest.refs_0_.moved_first), channel_id=1, source_target_pairs={{1,0},{2,1},{3,2},{4,3},{5,4},{6,5},{7,6},{8,7},{9,8},{10,9},{11,1... | collective-permute-start | bytes 983048 | tf_op jit(solution)/shard_map/ppermute | solution.py:421
  100.3 13.6 %collective-permute-start.6 = (f32[5,64,256]{2,1,0:T(8,128)S(1)}, f32[5,64,256]{2,1,0:T(8,128)S(1)}, u32[]{:S(2)}, u32[]{:S(2)}) collective-permute-start(f32[5,64,256]{2,1,0:T(8,128)S(1)} %collective-permute-done.4.rest.refs_0_.moved_first), channel_id=1, source_target_pairs={{0,1},{1,2},{2,3},{3,4},{4,5},{5,6},{6,7},{7,8},{8,9},{9,10},{10,1... | collective-permute-start | bytes 983048 | tf_op jit(solution)/shard_map/ppermute | solution.py:421
  131.7 12.0 %collective-permute-start.8 = (f32[5,64,256]{2,1,0:T(8,128)S(1)}, f32[5,64,256]{2,1,0:T(8,128)S(1)}, u32[]{:S(2)}, u32[]{:S(2)}) collective-permute-start(f32[5,64,256]{2,1,0:T(8,128)S(1)} %get-tuple-element.43), channel_id=1, source_target_pairs={{0,32},{32,64},{64,96},{96,128},{128,160},{160,192},{192,224},{1,3... | collective-permute-start | bytes 983048 | tf_op jit(solution)/shard_map/ppermute | solution.py:421
  160.5 1.9 %collective-permute-start.9 = (f32[32,32,128]{2,1,0:T(8,128)S(1)}, f32[32,32,128]{2,1,0:T(8,128)S(1)}, u32[]{:S(2)}, u32[]{:S(2)}) collective-permute-start(f32[32,32,128]{2,1,0:T(8,128)S(1)} %all_to_all.52.ours), channel_id=1, source_target_pairs={{0,1},{1,0},{2,3},{3,2},{4,5},{5,4},{6,7},{7,6},{8,9},{9,8},{10,11... | collective-permute-start | bytes 1572872 | tf_op jit(solution)/shard_map/ppermute | solution.py:432

commit v9 on v8

--- a/solution.py
+++ b/solution.py
@@ -58,13 +58,16 @@
 
 def coarse_beside(v):
     one = (1, 16, 128)
-    lane, row = iota(one, 2), iota(one, 1)
+    lane, row = iota(one, 2), iota((1, 8, 128), 1)
     left = lane < 64
     first, last = pltpu.roll(v[:1], 64, 2), pltpu.roll(v[15:], 64, 2)
     after = jnp.concatenate([v[1:], jnp.where(left, first, 0.0)], axis=0)
     before = jnp.concatenate([jnp.where(left, 0.0, last), v[:15]], axis=0)
     out = after + before
-    out = out + jnp.where(row == 0, 0.0, pltpu.roll(v, 1, 1)) + jnp.where(row == 15, 0.0, pltpu.roll(v, 15, 1))
+    up, down = pltpu.roll(v, 1, 1), pltpu.roll(v, 15, 1)
+    up = jnp.concatenate([jnp.where(row == 0, 0.0, up[:, :8]), up[:, 8:]], axis=1)
+    down = jnp.concatenate([down[:, :8], jnp.where(row == 7, 0.0, down[:, 8:])], axis=1)
+    out = out + (up + down)
     inner = lane & 63
     return out + jnp.where(inner == 0, 0.0, pltpu.roll(v, 1, 2)) + jnp.where(inner == 63, 0.0, pltpu.roll(v, 127, 2))
 
@@ -280,9 +283,14 @@
 
 
 def fine_beside(v):
-    rows, lanes = iota(v.shape, 0), iota(v.shape, 1)
-    out = jnp.where(rows == 0, 0.0, pltpu.roll(v, 1, 0)) + jnp.where(rows == 63, 0.0, pltpu.roll(v, 63, 0))
-    return out + jnp.where(lanes == 0, 0.0, pltpu.roll(v, 1, 1)) + jnp.where(lanes == 255, 0.0, pltpu.roll(v, 255, 1))
+    head, tail = iota((8, 256), 0), iota((64, 128), 1)
+    before, after = pltpu.roll(v, 1, 0), pltpu.roll(v, 63, 0)
+    before = jnp.concatenate([jnp.where(head == 0, 0.0, before[:8]), before[8:]], axis=0)
+    after = jnp.concatenate([after[:56], jnp.where(head == 7, 0.0, after[56:])], axis=0)
+    left, right = pltpu.roll(v, 1, 1), pltpu.roll(v, 255, 1)
+    left = jnp.concatenate([jnp.where(tail == 0, 0.0, left[:, :128]), left[:, 128:]], axis=1)
+    right = jnp.concatenate([right[:, :128], jnp.where(tail == 127, 0.0, right[:, 128:])], axis=1)
+    return (before + after) + (left + right)
 
 
 def inside(plane):
@@ -331,12 +339,16 @@
         return beside(field, low, plane) - 6.0 * field[plane - low]
 
     for plane in range(-3, 8):
-        r[plane + 3] = guarded(source(0, plane) + spread(u, -4, plane), plane, first)
+        lap = spread(u, -4, plane)
+        r[plane + 3] = guarded(source(0, plane) + lap, plane, first)
+        if -1 <= plane < 6:
+            q[0, plane + 1] = guarded(source(1, plane) + lap, plane, first)
     for plane in range(-2, 7):
-        w[plane + 2] = guarded((weight(plane) + (6.0 - SHIFT)) * r[plane + 3] - beside(r, -3, plane), plane, first)
+        v, around = r[plane + 3], beside(r, -3, plane)
+        w[plane + 2] = guarded((weight(plane) + (6.0 - SHIFT)) * v - around, plane, first)
+        if -1 <= plane < 6:
+            q[1, plane + 1] = guarded(around - 6.0 * v, plane, first)
     for plane in range(-1, 6):
-        q[0, plane + 1] = guarded(source(1, plane) + spread(u, -4, plane), plane, first)
-        q[1, plane + 1] = guarded(spread(r, -3, plane), plane, first)
         q[2, plane + 1] = guarded(spread(w, -2, plane), plane, first)
     for plane in range(5):
         for k in range(3):
@@ -348,7 +360,7 @@
         rv, wv = r[plane + 3], w[plane + 2]
         heavy = weight(plane) + 6.0
         terms += [rv * rv, rv * wv, wv * wv]
-        terms += [wv * (heavy * wv - fine_beside(wv) - 2.0 * w[plane + 3])]
+        terms += [wv * (weight(plane) * wv - q[2, plane + 1] + w[plane + 1] - w[plane + 3])]
         qs = [q[k, plane + 1] for k in range(3)]
         images = [a[k, plane] for k in range(3)]
         twice = []

time: 173 us -> 172 us (level)
  no operation moved by 1% of the time
where the time goes in v9:
time: 172 us; the launch traced here: 171 us
  blocking collectives  80.7 us (47%)
  Pallas kernels  44.6 us (26%)
  starting transfers between devices  26.9 us (16%)
  waiting for transfers between devices  17.3 us (10%)
    all_to_all x6, blocking collectives, exchange(): return lax.all_to_all(x, axis, split_axis=0, concat_axis=0, tiled=True)  80.7 us
    pallas_call x10, Pallas kernels, call(): pl.pallas_call(body, out_shape=tuple((jax.ShapeDtypeStruct(s, F32) for s...  44.6 us
    ppermute x7, starting transfers between devices, shifted(): return lax.ppermute(x, axis, pairs)  14.1 us
    all_to_all x1, waiting for transfers between devices, exchange(): return lax.all_to_all(x, axis, split_axis=0, concat_axis=0, tiled=True)  9.53 us
    all_to_all x1, starting transfers between devices, exchange(): return lax.all_to_all(x, axis, split_axis=0, concat_axis=0, tiled=True)  9.49 us
    ppermute x1, waiting for transfers between devices, body(): theirs = lax.ppermute(currents[0], ('tm', 'space'), pairs)  6.18 us
  transfers between devices with their start and end apart: 11, of which 3 were waited for; matrix products, arithmetic and copies ran while one was open for 0% of the time, Pallas kernels for 11%

profile of v9, /device:TPU:225, one launch (start us, length us, event | category | flops | bytes accessed | tf_op | source)
XLA Modules:
  0.0 170.9 jit_solution(17437025930110155354)
XLA Ops:
  0.6 2.6 %collective-permute-start = (f32[2,3]{1,0:T(2,128)}, f32[2,3]{1,0:T(2,128)S(1)}, u32[]{:S(2)}, u32[]{:S(2)}) collective-permute-start(f32[2,3]{1,0:T(2,128)} %bitcast.24), channel_id=1, source_target_pairs={{0,0},{8,8},{16,16},{24,24},{32,1},{40,9},{48,17},{56,25},{64,2},{... | collective-permute-start | bytes 80 | tf_op jit(solution)/shard_map/ppermute | solution.py:459
  3.2 6.2 %collective-permute-done.theirs = f32[2,3]{1,0:T(2,128)S(1)} collective-permute-done((f32[2,3]{1,0:T(2,128)}, f32[2,3]{1,0:T(2,128)S(1)}, u32[]{:S(2)}, u32[]{:S(2)}) %collective-permute-start) | collective-permute-done | bytes 56 | tf_op jit(solution)/shard_map/ppermute | solution.py:459
  9.9 5.0 %shard_map.68 = (f32[4,4,64,256]{3,2,1,0:T(8,128)}, f32[10,64,256]{2,1,0:T(8,128)}, f32[13,64,256]{2,1,0:T(8,128)}, f32[1,64,256]{2,1,0:T(8,128)}, f32[32,48,128]{2,1,0:T(8,128)}) custom-call(f32[4]{0:T(128)} %cond.1, f32[2,3]{1,0:T(2,128)} %bitcast.25, f32[2,3]{1,0:T(2,128)} %copy-done.1, s32[4,64,256]{2,1,0:T(8,128)} %labels_far.1, ...), custom_call_target="tpu_custom_call" | custom-call | tf_op jit(solution)/shard_map/pallas_call | solution.py:117
  14.9 2.4 %collective-permute-start.2 = (f32[13,64,256]{2,1,0:T(8,128)}, f32[13,64,256]{2,1,0:T(8,128)S(1)}, u32[]{:S(2)}, u32[]{:S(2)}) collective-permute-start(f32[13,64,256]{2,1,0:T(8,128)} %get-tuple-element.30), channel_id=1, source_target_pairs={{1,0},{2,1},{3,2},{4,3},{5,4},{6,5},{7,6},{8,7},{9,8},{10,9},{11,1... | collective-permute-start | bytes 2555912 | tf_op jit(solution)/shard_map/ppermute | solution.py:433
  17.3 9.5 %all-to-all-start = ((f32[32,48,128]{2,1,0:T(8,128)}), f32[32,48,128]{2,1,0:T(8,128)S(1)}, u32[]{:S(2)}, u32[]{:S(2)}) async-start(f32[32,48,128]{2,1,0:T(8,128)} %get-tuple-element.24), calls=%async_computation | async-start | bytes 1572864 | tf_op jit(solution)/shard_map/all_to_all | solution.py:437
  26.8 3.5 %collective-permute-start.1 = (f32[10,64,256]{2,1,0:T(8,128)}, f32[10,64,256]{2,1,0:T(8,128)S(1)}, u32[]{:S(2)}, u32[]{:S(2)}) collective-permute-start(f32[10,64,256]{2,1,0:T(8,128)} %get-tuple-element.29), channel_id=1, source_target_pairs={{0,1},{1,2},{2,3},{3,4},{4,5},{5,6},{6,7},{7,8},{8,9},{9,10},{10,1... | collective-permute-start | bytes 1966088 | tf_op jit(solution)/shard_map/ppermute | solution.py:433
  30.4 1.3 collective-permute-start.3
  31.7 9.5 %all-to-all-done.whole = f32[32,48,128]{2,1,0:T(8,128)S(1)} async-done(((f32[32,48,128]{2,1,0:T(8,128)}), f32[32,48,128]{2,1,0:T(8,128)S(1)}, u32[]{:S(2)}, u32[]{:S(2)}) %all-to-all-start) | async-done | bytes 786464 | tf_op jit(solution)/shard_map/all_to_all | solution.py:437
  41.3 9.6 %shard_map.69 = (f32[5,16,16,128]{3,2,1,0:T(8,128)S(1)}, f32[64,128]{1,0:T(8,128)S(1)}, f32[8,128]{1,0:T(8,128)S(1)}, f32[16,16,128]{2,1,0:T(8,128)S(1)}) custom-call(s32[2]{0:T(128)S(1)} %pad_add_fusion.where, f32[8,128]{1,0:T(8,128)S(1)} %bitcast.16, f32[32,48,128]{2,1,0:T(8,128)S(1)} %all-to-all-done.whole), custom_call_target="tpu_custom_call" | custom-call | flops 67108864 | bytes 1048576 | tf_op jit(solution)/shard_map/pallas_call | solution.py:117
  50.9 4.1 %shard_map.70 = (f32[9,5,64,256]{3,2,1,0:T(8,128)S(1)}, f32[32,128]{1,0:T(8,128)S(1)}) custom-call(s32[2]{0:T(128)S(1)} %pad_add_fusion.where, f32[64,128]{1,0:T(8,128)S(1)} %get-tuple-element.27.planes.old, f32[4,4,64,256]{3,2,1,0:T(8,128)S(1)} %copy-done, f32[10,64,256]{2,1,0:T(8,128)S(1)} %collective-permute-done.1.up, ...), custom_call_target="tpu_custom_call" | custom-call | tf_op jit(solution)/shard_map/pallas_call | solution.py:117
  55.0 13.0 %all_to_all.47 = f32[32,1,128]{2,1,0:T(1,128)S(1)} all-to-all(f32[32,1,128]{2,1,0:T(1,128)S(1)} %bitcast.22), channel_id=1, replica_groups=mesh['tm'=8,'space'=32] {'space'}, dimensions={0} | all-to-all | bytes 32768 | tf_op jit(solution)/shard_map/all_to_all | solution.py:437
  68.0 1.1 shard_map.71
  69.1 11.2 %all_to_all.48.ends = f32[8,8,128]{2,1,0:T(8,128)S(1)} all-to-all(f32[8,8,128]{2,1,0:T(8,128)S(1)} %get-tuple-element.35), channel_id=1, replica_groups=mesh['tm'=8,'space'=32] {'tm'}, dimensions={0} | all-to-all | bytes 65536 | tf_op jit(solution)/shard_map/all_to_all | solution.py:437
  80.4 16.8 %all_to_all.49.ours = f32[32,32,128]{2,1,0:T(8,128)S(1)} all-to-all(f32[32,32,128]{2,1,0:T(8,128)S(1)} %shard_map.72), channel_id=1, replica_groups=mesh['tm'=8,'space'=32] {'space'}, dimensions={0} | all-to-all | bytes 1048576 | tf_op jit(solution)/shard_map/all_to_all | solution.py:437
  97.6 2.0 %collective-permute-start.7 = (f32[5,64,256]{2,1,0:T(8,128)S(1)}, f32[5,64,256]{2,1,0:T(8,128)S(1)}, u32[]{:S(2)}, u32[]{:S(2)}) collective-permute-start(f32[5,64,256]{2,1,0:T(8,128)S(1)} %collective-permute-done.4.rest.refs_0_.moved_first), channel_id=1, source_target_pairs={{1,0},{2,1},{3,2},{4,3},{5,4},{6,5},{7,6},{8,7},{9,8},{10,9},{11,1... | collective-permute-start | bytes 983048 | tf_op jit(solution)/shard_map/ppermute | solution.py:433
  99.6 3.5 %collective-permute-start.6 = (f32[5,64,256]{2,1,0:T(8,128)S(1)}, f32[5,64,256]{2,1,0:T(8,128)S(1)}, u32[]{:S(2)}, u32[]{:S(2)}) collective-permute-start(f32[5,64,256]{2,1,0:T(8,128)S(1)} %collective-permute-done.4.rest.refs_0_.moved_first), channel_id=1, source_target_pairs={{0,1},{1,2},{2,3},{3,4},{4,5},{5,6},{6,7},{7,8},{8,9},{9,10},{10,1... | collective-permute-start | bytes 983048 | tf_op jit(solution)/shard_map/ppermute | solution.py:433
  103.2 10.0 %shard_map.73 = (f32[64,128]{1,0:T(8,128)S(1)}, f32[8,128]{1,0:T(8,128)S(1)}, f32[16,16,128]{2,1,0:T(8,128)S(1)}, f32[16,128]{1,0:T(8,128)S(1)}) custom-call(s32[2]{0:T(128)S(1)} %pad_add_fusion.where, f32[8,128]{1,0:T(8,128)S(1)} %bitcast.17, f32[5,16,16,128]{3,2,1,0:T(8,128)S(1)} %get-tuple-element.25.static, f32[16,16,128]{2,1,0:T(8,128)S(1)} %get-tuple-element.26.begin, ...), custom_call_target="tpu_custom_call" | custom-call | flops 67108864 | bytes 1048576 | tf_op jit(solution)/shard_map/pallas_call | solution.py:117
  113.2 3.9 %shard_map.74 = (f32[9,5,64,256]{3,2,1,0:T(8,128)S(1)}, f32[32,128]{1,0:T(8,128)S(1)}) custom-call(s32[2]{0:T(128)S(1)} %pad_add_fusion.where, f32[64,128]{1,0:T(8,128)S(1)} %get-tuple-element.39.planes, f32[4,4,64,256]{3,2,1,0:T(8,128)S(1)} %copy-done, f32[10,64,256]{2,1,0:T(8,128)S(1)} %collective-permute-done.1.up, ...), custom_call_target="tpu_custom_call" | custom-call | tf_op jit(solution)/shard_map/pallas_call | solution.py:117
  117.1 12.1 %all_to_all.50 = f32[32,1,128]{2,1,0:T(1,128)S(1)} all-to-all(f32[32,1,128]{2,1,0:T(1,128)S(1)} %bitcast.21), channel_id=1, replica_groups=mesh['tm'=8,'space'=32] {'space'}, dimensions={0} | all-to-all | bytes 32768 | tf_op jit(solution)/shard_map/all_to_all | solution.py:437
  130.4 1.3 collective-permute-start.8
  131.6 10.7 %all_to_all.51.ends = f32[8,8,128]{2,1,0:T(8,128)S(1)} all-to-all(f32[8,8,128]{2,1,0:T(8,128)S(1)} %get-tuple-element.44), channel_id=1, replica_groups=mesh['tm'=8,'space'=32] {'tm'}, dimensions={0} | all-to-all | bytes 65536 | tf_op jit(solution)/shard_map/all_to_all | solution.py:437
  142.4 16.8 %all_to_all.52.ours = f32[32,32,128]{2,1,0:T(8,128)S(1)} all-to-all(f32[32,32,128]{2,1,0:T(8,128)S(1)} %shard_map.76), channel_id=1, replica_groups=mesh['tm'=8,'space'=32] {'space'}, dimensions={0} | all-to-all | bytes 1048576 | tf_op jit(solution)/shard_map/all_to_all | solution.py:437
  159.6 1.5 collective-permute-done.9.theirs
  161.1 9.8 %shard_map.77 = f32[4,64,256]{2,1,0:T(8,128)} custom-call(s32[2]{0:T(128)S(1)} %pad_add_fusion.where, f32[8,128]{1,0:T(8,128)S(1)} %bitcast.18, f32[5,16,16,128]{3,2,1,0:T(8,128)S(1)} %get-tuple-element.25.static, f32[16,16,128]{2,1,0:T(8,128)S(1)} %get-tuple-element.37.begin, f32[16,128]{1,0:T(8,128)S(1)} %get-tuple-element.38.kept, ...), custom_call_target="tpu_custom_call" | custom-call | flops 67108864 | bytes 1048576 | tf_op jit(solution)/shard_map/pallas_call | solution.py:117
  (20 shorter events, 2.7 us)
Async XLA Ops:
  0.6 8.7 %collective-permute-start = (f32[2,3]{1,0:T(2,128)}, f32[2,3]{1,0:T(2,128)S(1)}, u32[]{:S(2)}, u32[]{:S(2)}) collective-permute-start(f32[2,3]{1,0:T(2,128)} %bitcast.24), channel_id=1, source_target_pairs={{0,0},{8,8},{16,16},{24,24},{32,1},{40,9},{48,17},{56,25},{64,2},{... | collective-permute-start | bytes 80 | tf_op jit(solution)/shard_map/ppermute | solution.py:459
  9.4 0.6 copy-start.1
  14.9 35.9 %copy-start = (f32[4,4,64,256]{3,2,1,0:T(8,128)S(1)}, f32[4,4,64,256]{3,2,1,0:T(8,128)}, u32[]{:S(2)}) copy-start(f32[4,4,64,256]{3,2,1,0:T(8,128)} %get-tuple-element.28.own) | copy-start | bytes 3145732
  14.9 35.9 %collective-permute-start.2 = (f32[13,64,256]{2,1,0:T(8,128)}, f32[13,64,256]{2,1,0:T(8,128)S(1)}, u32[]{:S(2)}, u32[]{:S(2)}) collective-permute-start(f32[13,64,256]{2,1,0:T(8,128)} %get-tuple-element.30), channel_id=1, source_target_pairs={{1,0},{2,1},{3,2},{4,3},{5,4},{6,5},{7,6},{8,7},{9,8},{10,9},{11,1... | collective-permute-start | bytes 2555912 | tf_op jit(solution)/shard_map/ppermute | solution.py:433
  17.3 24.0 %all-to-all-start = ((f32[32,48,128]{2,1,0:T(8,128)}), f32[32,48,128]{2,1,0:T(8,128)S(1)}, u32[]{:S(2)}, u32[]{:S(2)}) async-start(f32[32,48,128]{2,1,0:T(8,128)} %get-tuple-element.24), calls=%async_computation | async-start | bytes 1572864 | tf_op jit(solution)/shard_map/all_to_all | solution.py:437
  26.8 24.0 %collective-permute-start.1 = (f32[10,64,256]{2,1,0:T(8,128)}, f32[10,64,256]{2,1,0:T(8,128)S(1)}, u32[]{:S(2)}, u32[]{:S(2)}) collective-permute-start(f32[10,64,256]{2,1,0:T(8,128)} %get-tuple-element.29), channel_id=1, source_target_pairs={{0,1},{1,2},{2,3},{3,4},{4,5},{5,6},{6,7},{7,8},{8,9},{9,10},{10,1... | collective-permute-start | bytes 1966088 | tf_op jit(solution)/shard_map/ppermute | solution.py:433
  30.4 20.5 %collective-permute-start.3 = (f32[1,64,256]{2,1,0:T(8,128)}, f32[1,64,256]{2,1,0:T(8,128)S(1)}, u32[]{:S(2)}, u32[]{:S(2)}) collective-permute-start(f32[1,64,256]{2,1,0:T(8,128)} %get-tuple-element.31), channel_id=1, source_target_pairs={{2,0},{3,1},{4,2},{5,3},{6,4},{7,5},{8,6},{9,7},{10,8},{11,9},{12,... | collective-permute-start | bytes 196616 | tf_op jit(solution)/shard_map/ppermute | solution.py:433
  69.1 11.2 %collective-permute-start.4 = (f32[5,64,256]{2,1,0:T(8,128)S(1)}, f32[5,64,256]{2,1,0:T(8,128)S(1)}, u32[]{:S(2)}, u32[]{:S(2)}) collective-permute-start(f32[5,64,256]{2,1,0:T(8,128)S(1)} %get-tuple-element.36), channel_id=1, source_target_pairs={{0,32},{32,64},{64,96},{96,128},{128,160},{160,192},{192,224},{224... | collective-permute-start | bytes 983048 | tf_op jit(solution)/shard_map/ppermute | solution.py:433
  97.2 6.0 %collective-permute-start.5 = (f32[32,32,128]{2,1,0:T(8,128)S(1)}, f32[32,32,128]{2,1,0:T(8,128)S(1)}, u32[]{:S(2)}, u32[]{:S(2)}) collective-permute-start(f32[32,32,128]{2,1,0:T(8,128)S(1)} %all_to_all.49.ours), channel_id=1, source_target_pairs={{0,1},{1,0},{2,3},{3,2},{4,5},{5,4},{6,7},{7,6},{8,9},{9,8},{10,11... | collective-permute-start | bytes 1572872 | tf_op jit(solution)/shard_map/ppermute | solution.py:444
  97.6 15.6 %collective-permute-start.7 = (f32[5,64,256]{2,1,0:T(8,128)S(1)}, f32[5,64,256]{2,1,0:T(8,128)S(1)}, u32[]{:S(2)}, u32[]{:S(2)}) collective-permute-start(f32[5,64,256]{2,1,0:T(8,128)S(1)} %collective-permute-done.4.rest.refs_0_.moved_first), channel_id=1, source_target_pairs={{1,0},{2,1},{3,2},{4,3},{5,4},{6,5},{7,6},{8,7},{9,8},{10,9},{11,1... | collective-permute-start | bytes 983048 | tf_op jit(solution)/shard_map/ppermute | solution.py:433
  99.6 13.6 %collective-permute-start.6 = (f32[5,64,256]{2,1,0:T(8,128)S(1)}, f32[5,64,256]{2,1,0:T(8,128)S(1)}, u32[]{:S(2)}, u32[]{:S(2)}) collective-permute-start(f32[5,64,256]{2,1,0:T(8,128)S(1)} %collective-permute-done.4.rest.refs_0_.moved_first), channel_id=1, source_target_pairs={{0,1},{1,2},{2,3},{3,4},{4,5},{5,6},{6,7},{7,8},{8,9},{9,10},{10,1... | collective-permute-start | bytes 983048 | tf_op jit(solution)/shard_map/ppermute | solution.py:433
  130.4 12.0 %collective-permute-start.8 = (f32[5,64,256]{2,1,0:T(8,128)S(1)}, f32[5,64,256]{2,1,0:T(8,128)S(1)}, u32[]{:S(2)}, u32[]{:S(2)}) collective-permute-start(f32[5,64,256]{2,1,0:T(8,128)S(1)} %get-tuple-element.43), channel_id=1, source_target_pairs={{0,32},{32,64},{64,96},{96,128},{128,160},{160,192},{192,224},{1,3... | collective-permute-start | bytes 983048 | tf_op jit(solution)/shard_map/ppermute | solution.py:433
  159.2 1.9 %collective-permute-start.9 = (f32[32,32,128]{2,1,0:T(8,128)S(1)}, f32[32,32,128]{2,1,0:T(8,128)S(1)}, u32[]{:S(2)}, u32[]{:S(2)}) collective-permute-start(f32[32,32,128]{2,1,0:T(8,128)S(1)} %all_to_all.52.ours), channel_id=1, source_target_pairs={{0,1},{1,0},{2,3},{3,2},{4,5},{5,4},{6,7},{7,6},{8,9},{9,8},{10,11... | collective-permute-start | bytes 1572872 | tf_op jit(solution)/shard_map/ppermute | solution.py:444

commit v10 on v9

--- a/solution.py
+++ b/solution.py
@@ -138,14 +138,15 @@
     ]
     for copy in copies:
         copy.start()
-    for copy in copies:
-        copy.wait()
+    copies[0].wait()
     region = labels[...]
     cell = jnp.where(region == 0, cond[0], 0.0)
     for k in range(1, 4):
         cell = cell + jnp.where(region == k, cond[k], 0.0)
     own[0] = cell
+    copies[2].wait()
     own[3] = initial[...]
+    copies[1].wait()
     pattern = [coils[p] for p in range(PHASES)]
     for step in range(2):
         source = cur[step, 0] * pattern[0]

time: 172 us -> 171 us (level)
  no operation moved by 1% of the time
where the time goes in v10:
time: 171 us
  blocking collectives  80.7 us (47%)
  Pallas kernels  44.4 us (26%)
  starting transfers between devices  26.9 us (16%)
  waiting for transfers between devices  17.3 us (10%)
    all_to_all x6, blocking collectives, exchange(): return lax.all_to_all(x, axis, split_axis=0, concat_axis=0, tiled=True)  80.7 us
    pallas_call x10, Pallas kernels, call(): pl.pallas_call(body, out_shape=tuple((jax.ShapeDtypeStruct(s, F32) for s...  44.4 us
    ppermute x7, starting transfers between devices, shifted(): return lax.ppermute(x, axis, pairs)  14.1 us
    all_to_all x1, waiting for transfers between devices, exchange(): return lax.all_to_all(x, axis, split_axis=0, concat_axis=0, tiled=True)  9.53 us
    all_to_all x1, starting transfers between devices, exchange(): return lax.all_to_all(x, axis, split_axis=0, concat_axis=0, tiled=True)  9.49 us
    ppermute x1, waiting for transfers between devices, body(): theirs = lax.ppermute(currents[0], ('tm', 'space'), pairs)  6.18 us
  transfers between devices with their start and end apart: 11, of which 3 were waited for; matrix products, arithmetic and copies ran while one was open for 0% of the time, Pallas kernels for 11%

profile of v10, /device:TPU:225, one launch (start us, length us, event | category | flops | bytes accessed | tf_op | source)
XLA Modules:
  0.0 170.6 jit_solution(16348868595108002580)
XLA Ops:
  0.6 2.6 %collective-permute-start = (f32[2,3]{1,0:T(2,128)}, f32[2,3]{1,0:T(2,128)S(1)}, u32[]{:S(2)}, u32[]{:S(2)}) collective-permute-start(f32[2,3]{1,0:T(2,128)} %bitcast.24), channel_id=1, source_target_pairs={{0,0},{8,8},{16,16},{24,24},{32,1},{40,9},{48,17},{56,25},{64,2},{... | collective-permute-start | bytes 80 | tf_op jit(solution)/shard_map/ppermute | solution.py:460
  3.2 6.2 %collective-permute-done.theirs = f32[2,3]{1,0:T(2,128)S(1)} collective-permute-done((f32[2,3]{1,0:T(2,128)}, f32[2,3]{1,0:T(2,128)S(1)}, u32[]{:S(2)}, u32[]{:S(2)}) %collective-permute-start) | collective-permute-done | bytes 56 | tf_op jit(solution)/shard_map/ppermute | solution.py:460
  9.9 4.7 %shard_map.68 = (f32[4,4,64,256]{3,2,1,0:T(8,128)}, f32[10,64,256]{2,1,0:T(8,128)}, f32[13,64,256]{2,1,0:T(8,128)}, f32[1,64,256]{2,1,0:T(8,128)}, f32[32,48,128]{2,1,0:T(8,128)}) custom-call(f32[4]{0:T(128)} %cond.1, f32[2,3]{1,0:T(2,128)} %bitcast.25, f32[2,3]{1,0:T(2,128)} %copy-done.1, s32[4,64,256]{2,1,0:T(8,128)} %labels_far.1, ...), custom_call_target="tpu_custom_call" | custom-call | tf_op jit(solution)/shard_map/pallas_call | solution.py:117
  14.7 2.4 %collective-permute-start.2 = (f32[13,64,256]{2,1,0:T(8,128)}, f32[13,64,256]{2,1,0:T(8,128)S(1)}, u32[]{:S(2)}, u32[]{:S(2)}) collective-permute-start(f32[13,64,256]{2,1,0:T(8,128)} %get-tuple-element.30), channel_id=1, source_target_pairs={{1,0},{2,1},{3,2},{4,3},{5,4},{6,5},{7,6},{8,7},{9,8},{10,9},{11,1... | collective-permute-start | bytes 2555912 | tf_op jit(solution)/shard_map/ppermute | solution.py:434
  17.1 9.5 %all-to-all-start = ((f32[32,48,128]{2,1,0:T(8,128)}), f32[32,48,128]{2,1,0:T(8,128)S(1)}, u32[]{:S(2)}, u32[]{:S(2)}) async-start(f32[32,48,128]{2,1,0:T(8,128)} %get-tuple-element.24), calls=%async_computation | async-start | bytes 1572864 | tf_op jit(solution)/shard_map/all_to_all | solution.py:438
  26.6 3.5 %collective-permute-start.1 = (f32[10,64,256]{2,1,0:T(8,128)}, f32[10,64,256]{2,1,0:T(8,128)S(1)}, u32[]{:S(2)}, u32[]{:S(2)}) collective-permute-start(f32[10,64,256]{2,1,0:T(8,128)} %get-tuple-element.29), channel_id=1, source_target_pairs={{0,1},{1,2},{2,3},{3,4},{4,5},{5,6},{6,7},{7,8},{8,9},{9,10},{10,1... | collective-permute-start | bytes 1966088 | tf_op jit(solution)/shard_map/ppermute | solution.py:434
  30.1 1.3 collective-permute-start.3
  31.5 9.5 %all-to-all-done.whole = f32[32,48,128]{2,1,0:T(8,128)S(1)} async-done(((f32[32,48,128]{2,1,0:T(8,128)}), f32[32,48,128]{2,1,0:T(8,128)S(1)}, u32[]{:S(2)}, u32[]{:S(2)}) %all-to-all-start) | async-done | bytes 786464 | tf_op jit(solution)/shard_map/all_to_all | solution.py:438
  41.0 9.6 %shard_map.69 = (f32[5,16,16,128]{3,2,1,0:T(8,128)S(1)}, f32[64,128]{1,0:T(8,128)S(1)}, f32[8,128]{1,0:T(8,128)S(1)}, f32[16,16,128]{2,1,0:T(8,128)S(1)}) custom-call(s32[2]{0:T(128)S(1)} %pad_add_fusion.where, f32[8,128]{1,0:T(8,128)S(1)} %bitcast.16, f32[32,48,128]{2,1,0:T(8,128)S(1)} %all-to-all-done.whole), custom_call_target="tpu_custom_call" | custom-call | flops 67108864 | bytes 1048576 | tf_op jit(solution)/shard_map/pallas_call | solution.py:117
  50.6 4.1 %shard_map.70 = (f32[9,5,64,256]{3,2,1,0:T(8,128)S(1)}, f32[32,128]{1,0:T(8,128)S(1)}) custom-call(s32[2]{0:T(128)S(1)} %pad_add_fusion.where, f32[64,128]{1,0:T(8,128)S(1)} %get-tuple-element.27.planes.old, f32[4,4,64,256]{3,2,1,0:T(8,128)S(1)} %copy-done, f32[10,64,256]{2,1,0:T(8,128)S(1)} %collective-permute-done.1.up, ...), custom_call_target="tpu_custom_call" | custom-call | tf_op jit(solution)/shard_map/pallas_call | solution.py:117
  54.7 13.0 %all_to_all.47 = f32[32,1,128]{2,1,0:T(1,128)S(1)} all-to-all(f32[32,1,128]{2,1,0:T(1,128)S(1)} %bitcast.22), channel_id=1, replica_groups=mesh['tm'=8,'space'=32] {'space'}, dimensions={0} | all-to-all | bytes 32768 | tf_op jit(solution)/shard_map/all_to_all | solution.py:438
  67.7 1.1 shard_map.71
  68.9 11.2 %all_to_all.48.ends = f32[8,8,128]{2,1,0:T(8,128)S(1)} all-to-all(f32[8,8,128]{2,1,0:T(8,128)S(1)} %get-tuple-element.35), channel_id=1, replica_groups=mesh['tm'=8,'space'=32] {'tm'}, dimensions={0} | all-to-all | bytes 65536 | tf_op jit(solution)/shard_map/all_to_all | solution.py:438
  80.2 16.8 %all_to_all.49.ours = f32[32,32,128]{2,1,0:T(8,128)S(1)} all-to-all(f32[32,32,128]{2,1,0:T(8,128)S(1)} %shard_map.72), channel_id=1, replica_groups=mesh['tm'=8,'space'=32] {'space'}, dimensions={0} | all-to-all | bytes 1048576 | tf_op jit(solution)/shard_map/all_to_all | solution.py:438
  97.3 2.0 %collective-permute-start.7 = (f32[5,64,256]{2,1,0:T(8,128)S(1)}, f32[5,64,256]{2,1,0:T(8,128)S(1)}, u32[]{:S(2)}, u32[]{:S(2)}) collective-permute-start(f32[5,64,256]{2,1,0:T(8,128)S(1)} %collective-permute-done.4.rest.refs_0_.moved_first), channel_id=1, source_target_pairs={{1,0},{2,1},{3,2},{4,3},{5,4},{6,5},{7,6},{8,7},{9,8},{10,9},{11,1... | collective-permute-start | bytes 983048 | tf_op jit(solution)/shard_map/ppermute | solution.py:434
  99.4 3.5 %collective-permute-start.6 = (f32[5,64,256]{2,1,0:T(8,128)S(1)}, f32[5,64,256]{2,1,0:T(8,128)S(1)}, u32[]{:S(2)}, u32[]{:S(2)}) collective-permute-start(f32[5,64,256]{2,1,0:T(8,128)S(1)} %collective-permute-done.4.rest.refs_0_.moved_first), channel_id=1, source_target_pairs={{0,1},{1,2},{2,3},{3,4},{4,5},{5,6},{6,7},{7,8},{8,9},{9,10},{10,1... | collective-permute-start | bytes 983048 | tf_op jit(solution)/shard_map/ppermute | solution.py:434
  102.9 10.0 %shard_map.73 = (f32[64,128]{1,0:T(8,128)S(1)}, f32[8,128]{1,0:T(8,128)S(1)}, f32[16,16,128]{2,1,0:T(8,128)S(1)}, f32[16,128]{1,0:T(8,128)S(1)}) custom-call(s32[2]{0:T(128)S(1)} %pad_add_fusion.where, f32[8,128]{1,0:T(8,128)S(1)} %bitcast.17, f32[5,16,16,128]{3,2,1,0:T(8,128)S(1)} %get-tuple-element.25.static, f32[16,16,128]{2,1,0:T(8,128)S(1)} %get-tuple-element.26.begin, ...), custom_call_target="tpu_custom_call" | custom-call | flops 67108864 | bytes 1048576 | tf_op jit(solution)/shard_map/pallas_call | solution.py:117
  112.9 3.9 %shard_map.74 = (f32[9,5,64,256]{3,2,1,0:T(8,128)S(1)}, f32[32,128]{1,0:T(8,128)S(1)}) custom-call(s32[2]{0:T(128)S(1)} %pad_add_fusion.where, f32[64,128]{1,0:T(8,128)S(1)} %get-tuple-element.39.planes, f32[4,4,64,256]{3,2,1,0:T(8,128)S(1)} %copy-done, f32[10,64,256]{2,1,0:T(8,128)S(1)} %collective-permute-done.1.up, ...), custom_call_target="tpu_custom_call" | custom-call | tf_op jit(solution)/shard_map/pallas_call | solution.py:117
  116.9 12.1 %all_to_all.50 = f32[32,1,128]{2,1,0:T(1,128)S(1)} all-to-all(f32[32,1,128]{2,1,0:T(1,128)S(1)} %bitcast.21), channel_id=1, replica_groups=mesh['tm'=8,'space'=32] {'space'}, dimensions={0} | all-to-all | bytes 32768 | tf_op jit(solution)/shard_map/all_to_all | solution.py:438
  130.1 1.3 collective-permute-start.8
  131.4 10.7 %all_to_all.51.ends = f32[8,8,128]{2,1,0:T(8,128)S(1)} all-to-all(f32[8,8,128]{2,1,0:T(8,128)S(1)} %get-tuple-element.44), channel_id=1, replica_groups=mesh['tm'=8,'space'=32] {'tm'}, dimensions={0} | all-to-all | bytes 65536 | tf_op jit(solution)/shard_map/all_to_all | solution.py:438
  142.1 16.8 %all_to_all.52.ours = f32[32,32,128]{2,1,0:T(8,128)S(1)} all-to-all(f32[32,32,128]{2,1,0:T(8,128)S(1)} %shard_map.76), channel_id=1, replica_groups=mesh['tm'=8,'space'=32] {'space'}, dimensions={0} | all-to-all | bytes 1048576 | tf_op jit(solution)/shard_map/all_to_all | solution.py:438
  159.3 1.5 collective-permute-done.9.theirs
  160.8 9.8 %shard_map.77 = f32[4,64,256]{2,1,0:T(8,128)} custom-call(s32[2]{0:T(128)S(1)} %pad_add_fusion.where, f32[8,128]{1,0:T(8,128)S(1)} %bitcast.18, f32[5,16,16,128]{3,2,1,0:T(8,128)S(1)} %get-tuple-element.25.static, f32[16,16,128]{2,1,0:T(8,128)S(1)} %get-tuple-element.37.begin, f32[16,128]{1,0:T(8,128)S(1)} %get-tuple-element.38.kept, ...), custom_call_target="tpu_custom_call" | custom-call | flops 67108864 | bytes 1048576 | tf_op jit(solution)/shard_map/pallas_call | solution.py:117
  (20 shorter events, 2.7 us)
Async XLA Ops:
  0.6 8.7 %collective-permute-start = (f32[2,3]{1,0:T(2,128)}, f32[2,3]{1,0:T(2,128)S(1)}, u32[]{:S(2)}, u32[]{:S(2)}) collective-permute-start(f32[2,3]{1,0:T(2,128)} %bitcast.24), channel_id=1, source_target_pairs={{0,0},{8,8},{16,16},{24,24},{32,1},{40,9},{48,17},{56,25},{64,2},{... | collective-permute-start | bytes 80 | tf_op jit(solution)/shard_map/ppermute | solution.py:460
  9.4 0.6 copy-start.1
  14.7 35.9 %copy-start = (f32[4,4,64,256]{3,2,1,0:T(8,128)S(1)}, f32[4,4,64,256]{3,2,1,0:T(8,128)}, u32[]{:S(2)}) copy-start(f32[4,4,64,256]{3,2,1,0:T(8,128)} %get-tuple-element.28.own) | copy-start | bytes 3145732
  14.7 35.9 %collective-permute-start.2 = (f32[13,64,256]{2,1,0:T(8,128)}, f32[13,64,256]{2,1,0:T(8,128)S(1)}, u32[]{:S(2)}, u32[]{:S(2)}) collective-permute-start(f32[13,64,256]{2,1,0:T(8,128)} %get-tuple-element.30), channel_id=1, source_target_pairs={{1,0},{2,1},{3,2},{4,3},{5,4},{6,5},{7,6},{8,7},{9,8},{10,9},{11,1... | collective-permute-start | bytes 2555912 | tf_op jit(solution)/shard_map/ppermute | solution.py:434
  17.1 23.9 %all-to-all-start = ((f32[32,48,128]{2,1,0:T(8,128)}), f32[32,48,128]{2,1,0:T(8,128)S(1)}, u32[]{:S(2)}, u32[]{:S(2)}) async-start(f32[32,48,128]{2,1,0:T(8,128)} %get-tuple-element.24), calls=%async_computation | async-start | bytes 1572864 | tf_op jit(solution)/shard_map/all_to_all | solution.py:438
  26.6 24.0 %collective-permute-start.1 = (f32[10,64,256]{2,1,0:T(8,128)}, f32[10,64,256]{2,1,0:T(8,128)S(1)}, u32[]{:S(2)}, u32[]{:S(2)}) collective-permute-start(f32[10,64,256]{2,1,0:T(8,128)} %get-tuple-element.29), channel_id=1, source_target_pairs={{0,1},{1,2},{2,3},{3,4},{4,5},{5,6},{6,7},{7,8},{8,9},{9,10},{10,1... | collective-permute-start | bytes 1966088 | tf_op jit(solution)/shard_map/ppermute | solution.py:434
  30.1 20.5 %collective-permute-start.3 = (f32[1,64,256]{2,1,0:T(8,128)}, f32[1,64,256]{2,1,0:T(8,128)S(1)}, u32[]{:S(2)}, u32[]{:S(2)}) collective-permute-start(f32[1,64,256]{2,1,0:T(8,128)} %get-tuple-element.31), channel_id=1, source_target_pairs={{2,0},{3,1},{4,2},{5,3},{6,4},{7,5},{8,6},{9,7},{10,8},{11,9},{12,... | collective-permute-start | bytes 196616 | tf_op jit(solution)/shard_map/ppermute | solution.py:434
  68.9 11.2 %collective-permute-start.4 = (f32[5,64,256]{2,1,0:T(8,128)S(1)}, f32[5,64,256]{2,1,0:T(8,128)S(1)}, u32[]{:S(2)}, u32[]{:S(2)}) collective-permute-start(f32[5,64,256]{2,1,0:T(8,128)S(1)} %get-tuple-element.36), channel_id=1, source_target_pairs={{0,32},{32,64},{64,96},{96,128},{128,160},{160,192},{192,224},{224... | collective-permute-start | bytes 983048 | tf_op jit(solution)/shard_map/ppermute | solution.py:434
  97.0 6.0 %collective-permute-start.5 = (f32[32,32,128]{2,1,0:T(8,128)S(1)}, f32[32,32,128]{2,1,0:T(8,128)S(1)}, u32[]{:S(2)}, u32[]{:S(2)}) collective-permute-start(f32[32,32,128]{2,1,0:T(8,128)S(1)} %all_to_all.49.ours), channel_id=1, source_target_pairs={{0,1},{1,0},{2,3},{3,2},{4,5},{5,4},{6,7},{7,6},{8,9},{9,8},{10,11... | collective-permute-start | bytes 1572872 | tf_op jit(solution)/shard_map/ppermute | solution.py:445
  97.3 15.6 %collective-permute-start.7 = (f32[5,64,256]{2,1,0:T(8,128)S(1)}, f32[5,64,256]{2,1,0:T(8,128)S(1)}, u32[]{:S(2)}, u32[]{:S(2)}) collective-permute-start(f32[5,64,256]{2,1,0:T(8,128)S(1)} %collective-permute-done.4.rest.refs_0_.moved_first), channel_id=1, source_target_pairs={{1,0},{2,1},{3,2},{4,3},{5,4},{6,5},{7,6},{8,7},{9,8},{10,9},{11,1... | collective-permute-start | bytes 983048 | tf_op jit(solution)/shard_map/ppermute | solution.py:434
  99.4 13.6 %collective-permute-start.6 = (f32[5,64,256]{2,1,0:T(8,128)S(1)}, f32[5,64,256]{2,1,0:T(8,128)S(1)}, u32[]{:S(2)}, u32[]{:S(2)}) collective-permute-start(f32[5,64,256]{2,1,0:T(8,128)S(1)} %collective-permute-done.4.rest.refs_0_.moved_first), channel_id=1, source_target_pairs={{0,1},{1,2},{2,3},{3,4},{4,5},{5,6},{6,7},{7,8},{8,9},{9,10},{10,1... | collective-permute-start | bytes 983048 | tf_op jit(solution)/shard_map/ppermute | solution.py:434
  130.1 12.0 %collective-permute-start.8 = (f32[5,64,256]{2,1,0:T(8,128)S(1)}, f32[5,64,256]{2,1,0:T(8,128)S(1)}, u32[]{:S(2)}, u32[]{:S(2)}) collective-permute-start(f32[5,64,256]{2,1,0:T(8,128)S(1)} %get-tuple-element.43), channel_id=1, source_target_pairs={{0,32},{32,64},{64,96},{96,128},{128,160},{160,192},{192,224},{1,3... | collective-permute-start | bytes 983048 | tf_op jit(solution)/shard_map/ppermute | solution.py:434
  158.9 1.9 %collective-permute-start.9 = (f32[32,32,128]{2,1,0:T(8,128)S(1)}, f32[32,32,128]{2,1,0:T(8,128)S(1)}, u32[]{:S(2)}, u32[]{:S(2)}) collective-permute-start(f32[32,32,128]{2,1,0:T(8,128)S(1)} %all_to_all.52.ours), channel_id=1, source_target_pairs={{0,1},{1,0},{2,3},{3,2},{4,5},{5,4},{6,7},{7,6},{8,9},{9,8},{10,11... | collective-permute-start | bytes 1572872 | tf_op jit(solution)/shard_map/ppermute | solution.py:445
